TPU v7x, 8 devices: a whole 2x2x1 slice. The times are simulated.
8 devices in a mesh: data: 2 (over z, y), dap: 4 (over x, core).
Axes of the slice: x: 2, y: 2, z: 1, core: 2. Of those that a mesh axis runs over, the one named last changes fastest.
Arguments:
- pair_act: bfloat16 [768, 384, 128], P(('data', 'dap')), parts along dimension 0
- pair_mask: int32 [768, 384], P(('data', 'dap')), parts along dimension 0
- d_pair_out: bfloat16 [768, 384, 128], P(('data', 'dap')), parts along dimension 0
- ln_pair: bfloat16 [2, 2, 128], replicated
- w_proj: bfloat16 [2, 128, 512], replicated
- w_gate: bfloat16 [2, 128, 128], replicated
- ln_chan: bfloat16 [2, 2, 128], replicated
- w_out: bfloat16 [2, 128, 128], replicated
Outputs:
- output 1: bfloat16 [768, 384, 128], P(('data', 'dap')), parts along dimension 0
- output 2: bfloat16 [768, 384, 128], P(('data', 'dap')), parts along dimension 0
- output 3: bfloat16 [4, 2, 128], P('data'), parts along dimension 0
- output 4: bfloat16 [4, 128, 512], P('data'), parts along dimension 0
- output 5: bfloat16 [4, 128, 128], P('data'), parts along dimension 0
- output 6: bfloat16 [4, 2, 128], P('data'), parts along dimension 0
- output 7: bfloat16 [4, 128, 128], P('data'), parts along dimension 0
There are 2 independent parts. A program takes and returns all parts, laid end to end along the dimension named above; an argument that names none is the same for every part.
All inputs are finite; a program needn't handle non-finite values.
Results may differ from a plain program's by a relative error of at most 0.0142309.
Values are sent between devices in bfloat16 or wider.
A program may use at most 1 GiB of HBM per device.

v0:
```python
import jax
import jax.numpy as jnp
from jax import lax
from jax.sharding import PartitionSpec as P

LN_EPS = 1e-5
GROUP_AXIS = 'dap'


def layer_norm(values, gain_vec, shift_vec, norm_axis):
    mean_val = jnp.mean(values, axis=norm_axis, keepdims=True)
    centered = values - mean_val
    variance = jnp.mean(centered * centered, axis=norm_axis, keepdims=True)
    return centered * lax.rsqrt(variance + LN_EPS) * gain_vec + shift_vec


def norm_pair(values, ln_params):
    return layer_norm(values, ln_params[0], ln_params[1], -1)


def norm_chan(values, ln_params):
    return layer_norm(values, ln_params[0][:, None, None], ln_params[1][:, None, None], 0)


def to_channels(row_blocks):
    chan_dim = row_blocks.ndim - 3
    return lax.all_to_all(row_blocks, GROUP_AXIS, chan_dim, chan_dim + 1, tiled=True)


def to_rows(chan_blocks):
    chan_dim = chan_blocks.ndim - 3
    return lax.all_to_all(chan_blocks, GROUP_AXIS, chan_dim + 1, chan_dim, tiled=True)


def update_forward(z_rows, mask_f, ln_p, w_proj, w_gate, ln_q, w_out, incoming):
    z_float = z_rows.astype(jnp.float32)
    x_float, pair_back = jax.vjp(norm_pair, z_float, ln_p.astype(jnp.float32))
    x_norm = x_float.astype(jnp.bfloat16)
    proj_all = jnp.einsum('ijd,de->eij', x_norm, w_proj, preferred_element_type=jnp.float32)
    gate_val = jax.nn.sigmoid(jnp.einsum('ijd,de->ije', x_norm, w_gate, preferred_element_type=jnp.float32))
    lin_a, pre_ga, lin_b, pre_gb = jnp.split(proj_all, 4, axis=0)
    sig_a = jax.nn.sigmoid(pre_ga)
    sig_b = jax.nn.sigmoid(pre_gb)
    left_proj = (mask_f * sig_a * lin_a).astype(jnp.bfloat16)
    right_proj = (mask_f * sig_b * lin_b).astype(jnp.bfloat16)
    chan_pair = to_channels(jnp.stack([left_proj, right_proj]))
    if incoming:
        tri_prod = jnp.einsum('cki,ckj->cij', chan_pair[0], chan_pair[1], preferred_element_type=jnp.float32)
    else:
        tri_prod = jnp.einsum('cik,cjk->cij', chan_pair[0], chan_pair[1], preferred_element_type=jnp.float32)
    t_rows = to_rows(tri_prod.astype(jnp.bfloat16))
    y_float, chan_back = jax.vjp(norm_chan, t_rows.astype(jnp.float32), ln_q.astype(jnp.float32))
    y_norm = y_float.astype(jnp.bfloat16)
    update_f = jnp.einsum('cij,cd->ijd', y_norm, w_out, preferred_element_type=jnp.float32)
    z_new = (z_float + gate_val * update_f).astype(jnp.bfloat16)
    saved_fwd = dict(pair_back=pair_back, chan_back=chan_back, x_norm=x_norm, lin_a=lin_a, sig_a=sig_a, lin_b=lin_b, sig_b=sig_b, chan_pair=chan_pair, y_norm=y_norm, update_f=update_f, gate_val=gate_val)
    return z_new, saved_fwd


def update_backward(d_new, saved_fwd, mask_f, w_proj, w_gate, w_out, incoming):
    d_newf = d_new.astype(jnp.float32)
    gate_val = saved_fwd['gate_val']
    d_gate = (d_newf * saved_fwd['update_f'] * gate_val * (1.0 - gate_val)).astype(jnp.bfloat16)
    d_update = (d_newf * gate_val).astype(jnp.bfloat16)
    g_w_out = jnp.einsum('cij,ijd->cd', saved_fwd['y_norm'], d_update, preferred_element_type=jnp.float32)
    d_y = jnp.einsum('ijd,cd->cij', d_update, w_out, preferred_element_type=jnp.float32).astype(jnp.bfloat16)
    d_t, g_ln_q = saved_fwd['chan_back'](d_y.astype(jnp.float32))
    d_chan = to_channels(d_t.astype(jnp.bfloat16))
    left_chan = saved_fwd['chan_pair'][0]
    right_chan = saved_fwd['chan_pair'][1]
    if incoming:
        d_left = jnp.einsum('ckj,cij->cki', right_chan, d_chan, preferred_element_type=jnp.float32)
        d_right = jnp.einsum('cki,cij->ckj', left_chan, d_chan, preferred_element_type=jnp.float32)
    else:
        d_left = jnp.einsum('cij,cjk->cik', d_chan, right_chan, preferred_element_type=jnp.float32)
        d_right = jnp.einsum('cij,cik->cjk', d_chan, left_chan, preferred_element_type=jnp.float32)
    d_rows = to_rows(jnp.stack([d_left.astype(jnp.bfloat16), d_right.astype(jnp.bfloat16)]))
    d_left_f = d_rows[0].astype(jnp.float32) * mask_f
    d_right_f = d_rows[1].astype(jnp.float32) * mask_f
    sig_a = saved_fwd['sig_a']
    sig_b = saved_fwd['sig_b']
    d_proj = jnp.concatenate([d_left_f * sig_a, d_left_f * saved_fwd['lin_a'] * sig_a * (1.0 - sig_a), d_right_f * sig_b, d_right_f * saved_fwd['lin_b'] * sig_b * (1.0 - sig_b)], axis=0).astype(jnp.bfloat16)
    x_norm = saved_fwd['x_norm']
    g_w_proj = jnp.einsum('ijd,eij->de', x_norm, d_proj, preferred_element_type=jnp.float32)
    g_w_gate = jnp.einsum('ijd,ije->de', x_norm, d_gate, preferred_element_type=jnp.float32)
    d_x = (jnp.einsum('eij,de->ijd', d_proj, w_proj, preferred_element_type=jnp.float32) + jnp.einsum('ije,de->ijd', d_gate, w_gate, preferred_element_type=jnp.float32)).astype(jnp.bfloat16)
    d_zf, g_ln_p = saved_fwd['pair_back'](d_x.astype(jnp.float32))
    d_prev = (d_newf + d_zf).astype(jnp.bfloat16)
    return d_prev, (g_ln_p, g_w_proj, g_w_gate, g_ln_q, g_w_out)


def solution(mesh):
    row_spec = P(('data', 'dap'), None, None)
    mask_spec = P(('data', 'dap'), None)
    full_spec = P()
    grad_spec = P('data', None, None)

    def device_step(pair_act, pair_mask, d_pair_out, ln_pair, w_proj, w_gate, ln_chan, w_out):
        mask_f = pair_mask.astype(jnp.float32)
        z_mid, saved_out = update_forward(pair_act, mask_f, ln_pair[0], w_proj[0], w_gate[0], ln_chan[0], w_out[0], False)
        pair_out, saved_in = update_forward(z_mid, mask_f, ln_pair[1], w_proj[1], w_gate[1], ln_chan[1], w_out[1], True)
        d_mid, grads_in = update_backward(d_pair_out, saved_in, mask_f, w_proj[1], w_gate[1], w_out[1], True)
        d_pair, grads_out = update_backward(d_mid, saved_out, mask_f, w_proj[0], w_gate[0], w_out[0], False)
        local_grads = tuple(jnp.stack([grad_a, grad_b]) for grad_a, grad_b in zip(grads_out, grads_in))
        group_grads = lax.psum(local_grads, GROUP_AXIS)
        return (pair_out, d_pair) + tuple(grad_sum.astype(jnp.bfloat16) for grad_sum in group_grads)

    return jax.shard_map(device_step, mesh=mesh, in_specs=(row_spec, mask_spec, row_spec, full_spec, full_spec, full_spec, full_spec, full_spec), out_specs=(row_spec, row_spec, grad_spec, grad_spec, grad_spec, grad_spec, grad_spec), check_vma=False)
```

profile of v0, /device:TPU:0, one launch (start us, length us, event | category | flops | bytes accessed | tf_op | source)
XLA Modules:
  0.0 2669.0 jit_solution(9418699081702484759)
XLA Ops:
  30.4 30.1 %convolution_bitcast_fusion.1 = f32[512,96,384]{0,2,1:T(8,128)} fusion(bf16[2,128,512]{2,1,0:T(8,128)(2,1)S(1)} %copy-done.37, bf16[96,384,128]{1,2,0:T(8,128)(2,1)} %copy.247, f32[128]{0:T(128)S(1)} %get-tuple-element.118, f32[128]{0:T(128)S(1)} %get-tuple-element.119, f32[96,384]{1,0:T(8,128)S(1)} %fusion.94, f32[96,384]{1,0:T(8,128)S(1)} %broadcast_multiply_fusion.3), kind=kOutput, calls=%fused_computation.33 | convolution fusion | flops 4860149760 | bytes 85361664 | tf_op jit(solution)/shard_map/ijd,de->eij/dot_general | solution.py:39
  60.5 25.0 fusion.62
  93.5 24.5 copy.251
  118.0 218.2 %all_to_all.114 = bf16[2,128,96,384]{3,2,0,1:T(8,128)(2,1)} all-to-all(bf16[2,128,96,384]{3,2,0,1:T(8,128)(2,1)} %copy.251), channel_id=1, replica_groups=mesh['data'=2,'dap'=4] {'dap'}, dimensions={1} | all-to-all | bytes 37748736 | tf_op jit(solution)/shard_map/all_to_all | solution.py:27
  415.9 93.8 %all-to-all-done.1 = bf16[32,384,384]{2,0,1:T(8,128)(2,1)} async-done(((bf16[32,384,384]{2,0,1:T(8,128)(2,1)}), bf16[32,384,384]{2,0,1:T(8,128)(2,1)}, u32[]{:S(2)}, u32[]{:S(2)}) %all-to-all-start.1) | async-done | bytes 9437216 | tf_op jit(solution)/shard_map/all_to_all | solution.py:32
  570.1 30.4 %convert_reduce_fusion.2 = (f32[96,384]{1,0:T(8,128)S(1)}, bf16[96,384,128]{1,2,0:T(8,128)(2,1)}, f32[96,384,128]{1,2,0:T(8,128)}) fusion(f32[96,384,128]{1,2,0:T(8,128)} %fusion.70, bf16[96,384,128]{1,2,0:T(8,128)(2,1)} %copy.247, bf16[2,128,128]{2,1,0:T(8,128)(2,1)S(1)} %copy-done.42, f32[128]{0:T(128)S(1)} %get-tuple-element.118, ...), kind=kOutput, calls=%fused_computation.20 | convolution fusion | flops 1278701568 | bytes 66536448 | tf_op jit(solution)/shard_map/ijd,de->ije/dot_general | solution.py:40
  621.3 30.1 %convolution_bitcast_fusion = f32[512,96,384]{0,2,1:T(8,128)} fusion(bf16[96,384,128]{1,2,0:T(8,128)(2,1)} %fusion.21, bf16[2,128,512]{2,1,0:T(8,128)(2,1)S(1)} %copy-done.38), kind=kOutput, calls=%fused_computation.32 | convolution fusion | flops 4831838208 | bytes 85065728 | tf_op jit(solution)/shard_map/ijd,de->eij/dot_general | solution.py:39
  651.4 24.8 fusion.64
  684.2 24.4 copy.265
  708.6 217.2 %all_to_all.115 = bf16[2,128,96,384]{3,2,0,1:T(8,128)(2,1)} all-to-all(bf16[2,128,96,384]{3,2,0,1:T(8,128)(2,1)} %copy.265), channel_id=1, replica_groups=mesh['data'=2,'dap'=4] {'dap'}, dimensions={1} | all-to-all | bytes 37748736 | tf_op jit(solution)/shard_map/all_to_all | solution.py:27
  1017.5 78.9 %all-to-all-done.3 = bf16[32,384,384]{2,0,1:T(8,128)(2,1)} async-done(((bf16[32,384,384]{2,0,1:T(8,128)(2,1)}), bf16[32,384,384]{2,0,1:T(8,128)(2,1)}, u32[]{:S(2)}, u32[]{:S(2)}) %all-to-all-start.3) | async-done | bytes 9437216 | tf_op jit(solution)/shard_map/all_to_all | solution.py:32
  1162.6 24.3 fusion.25
  1187.0 25.7 fusion.26
  1212.8 25.1 add_convert_fusion.5
  1250.7 112.1 %all_to_all.116 = bf16[128,96,384]{2,1,0:T(8,128)(2,1)} all-to-all(bf16[128,96,384]{2,1,0:T(8,128)(2,1)} %copy.281), channel_id=1, replica_groups=mesh['data'=2,'dap'=4] {'dap'}, dimensions={0} | all-to-all | bytes 18874368 | tf_op jit(solution)/shard_map/all_to_all | solution.py:27
  1410.1 45.8 %copy.283 = bf16[2,32,384,384]{3,1,0,2:T(8,128)(2,1)} copy(bf16[2,32,384,384]{3,2,1,0:T(8,128)(2,1)S(1)} %pad_maximum_fusion.4) | data formatting | bytes 37748736 | tf_op jit(solution)/shard_map/stack | solution.py:77
  1529.6 25.7 fusion.37
  1555.3 113.7 %all-to-all-done.5 = bf16[2,32,384,384]{3,1,0,2:T(8,128)(2,1)} async-done(((bf16[2,32,384,384]{3,1,0,2:T(8,128)(2,1)}), bf16[2,32,384,384]{3,1,0,2:T(8,128)(2,1)}, u32[]{:S(2)}, u32[]{:S(2)}) %all-to-all-start.5) | async-done | bytes 18874400 | tf_op jit(solution)/shard_map/all_to_all | solution.py:32
  1761.1 51.1 %multiply_convert_fusion.7 = (bf16[128,96,384]{0,2,1:T(8,128)(2,1)}, bf16[128,96,384]{0,2,1:T(8,128)(2,1)}, bf16[128,96,384]{0,2,1:T(8,128)(2,1)}, bf16[128,96,384]{0,2,1:T(8,128)(2,1)}) fusion(f32[128,96,384]{0,2,1:T(8,128)} %copy.286, f32[96,384]{1,0:T(8,128)S(1)} %copy-done.20, f32[512,96,384]{0,2,1:T(8,128)} %convolution_bitcast_fusion, ...), kind=kLoop, calls=%fused_computation.110 | loop fusion | flops 103809024 | bytes 151142400 | tf_op jit(solution)/shard_map/convert.18
  1812.2 23.4 fusion.85
  1835.6 19.6 convert_reduce_fusion.1
  1873.8 24.8 fusion.43
  1898.6 23.8 fusion.24
  1922.6 25.7 fusion.27
  1948.3 25.1 add_convert_fusion.3
  1986.4 112.2 %all_to_all.117 = bf16[128,96,384]{2,1,0:T(8,128)(2,1)} all-to-all(bf16[128,96,384]{2,1,0:T(8,128)(2,1)} %copy.297), channel_id=1, replica_groups=mesh['data'=2,'dap'=4] {'dap'}, dimensions={0} | all-to-all | bytes 18874368 | tf_op jit(solution)/shard_map/all_to_all | solution.py:27
  2141.6 46.0 %copy.300 = bf16[2,32,384,384]{3,1,0,2:T(8,128)(2,1)} copy(bf16[2,32,384,384]{3,2,1,0:T(8,128)(2,1)S(1)} %pad_maximum_fusion.5) | data formatting | bytes 37748736 | tf_op jit(solution)/shard_map/stack | solution.py:77
  2226.4 19.9 fusion.88
  2246.5 21.2 fusion.89
  2305.7 94.9 %all-to-all-done.7 = bf16[2,32,384,384]{3,1,0,2:T(8,128)(2,1)} async-done(((bf16[2,32,384,384]{3,1,0,2:T(8,128)(2,1)}), bf16[2,32,384,384]{3,1,0,2:T(8,128)(2,1)}, u32[]{:S(2)}, u32[]{:S(2)}) %all-to-all-start.7) | async-done | bytes 18874400 | tf_op jit(solution)/shard_map/all_to_all | solution.py:32
  2492.9 51.2 %multiply_convert_fusion.3 = (bf16[128,96,384]{0,2,1:T(8,128)(2,1)}, bf16[128,96,384]{0,2,1:T(8,128)(2,1)}, bf16[128,96,384]{0,2,1:T(8,128)(2,1)}, bf16[128,96,384]{0,2,1:T(8,128)(2,1)}) fusion(f32[128,96,384]{0,2,1:T(8,128)} %copy.303, f32[96,384]{1,0:T(8,128)S(1)} %copy-done.21, f32[512,96,384]{0,2,1:T(8,128)} %convolution_bitcast_fusion.1, ...), kind=kLoop, calls=%fused_computation.104 | loop fusion | flops 103809024 | bytes 151142400 | tf_op jit(solution)/shard_map/convert.14
  2544.2 20.3 fusion.87
  (300 shorter events, 937.6 us)
Async XLA Ops:
  2.2 58.2 %copy-start.18 = (f32[96,384]{1,0:T(8,128)}, f32[96,384]{1,0:T(8,128)S(1)}, u32[]{:S(2)}) copy-start(f32[96,384]{1,0:T(8,128)S(1)} %convert_element_type.227) | copy-start | bytes 442372
  2.2 28.1 %copy-start.37 = (bf16[2,128,512]{2,1,0:T(8,128)(2,1)S(1)}, bf16[2,128,512]{2,1,0:T(8,128)(2,1)}, u32[]{:S(2)}) copy-start(bf16[2,128,512]{2,1,0:T(8,128)(2,1)} %param.12) | copy-start | bytes 786436
  21.3 548.8 %copy-start.10 = (f32[96,384]{1,0:T(8,128)}, f32[96,384]{1,0:T(8,128)S(1)}, u32[]{:S(2)}) copy-start(f32[96,384]{1,0:T(8,128)S(1)} %broadcast_multiply_fusion.3) | copy-start | bytes 442372
  29.8 540.3 %copy-start.22 = (f32[96,384]{1,0:T(8,128)}, f32[96,384]{1,0:T(8,128)S(1)}, u32[]{:S(2)}) copy-start(f32[96,384]{1,0:T(8,128)S(1)} %fusion.94) | copy-start | bytes 442372
  30.4 539.7 %copy-start.49 = (f32[128]{0:T(128)}, f32[128]{0:T(128)S(1)}, u32[]{:S(2)}) copy-start(f32[128]{0:T(128)S(1)} %get-tuple-element.119) | copy-start | bytes 1540
  30.4 539.7 %copy-start.57 = (f32[128]{0:T(128)}, f32[128]{0:T(128)S(1)}, u32[]{:S(2)}) copy-start(f32[128]{0:T(128)S(1)} %get-tuple-element.118) | copy-start | bytes 1540
  386.8 27.6 %copy-start.69 = (bf16[2,2,128]{2,1,0:T(2,128)(2,1)S(1)}, bf16[2,2,128]{2,1,0:T(2,128)(2,1)}, u32[]{:S(2)}) copy-start(bf16[2,2,128]{2,1,0:T(2,128)(2,1)} %param.14) | copy-start | bytes 3076
  399.8 109.9 %all-to-all-start.1 = ((bf16[32,384,384]{2,0,1:T(8,128)(2,1)}), bf16[32,384,384]{2,0,1:T(8,128)(2,1)}, u32[]{:S(2)}, u32[]{:S(2)}) async-start(bf16[32,384,384]{2,0,1:T(8,128)(2,1)} %copy.255), calls=%async_computation.1 | async-start | bytes 18874368 | tf_op jit(solution)/shard_map/all_to_all | solution.py:32
  525.4 28.3 %copy-start.6 = (f32[96,384]{1,0:T(8,128)}, f32[96,384]{1,0:T(8,128)S(1)}, u32[]{:S(2)}) copy-start(f32[96,384]{1,0:T(8,128)S(1)} %broadcast_multiply_fusion.2) | copy-start | bytes 442372
  570.1 38.9 %copy-start.52 = (f32[128]{0:T(128)S(1)}, f32[128]{0:T(128)}, u32[]{:S(2)}) copy-start(f32[128]{0:T(128)} %get-tuple-element.105) | copy-start | bytes 1540
  570.1 38.9 %copy-start.63 = (f32[128]{0:T(128)S(1)}, f32[128]{0:T(128)}, u32[]{:S(2)}) copy-start(f32[128]{0:T(128)} %get-tuple-element.106) | copy-start | bytes 1540
  621.3 30.1 %copy-start.19 = (f32[96,384]{1,0:T(8,128)S(1)}, f32[96,384]{1,0:T(8,128)}, u32[]{:S(2)}) copy-start(f32[96,384]{1,0:T(8,128)} %copy-done.18) | copy-start | bytes 442372
  986.4 110.0 %all-to-all-start.3 = ((bf16[32,384,384]{2,0,1:T(8,128)(2,1)}), bf16[32,384,384]{2,0,1:T(8,128)(2,1)}, u32[]{:S(2)}, u32[]{:S(2)}) async-start(bf16[32,384,384]{2,0,1:T(8,128)(2,1)} %copy.270), calls=%async_computation.3 | async-start | bytes 18874368 | tf_op jit(solution)/shard_map/all_to_all | solution.py:32
  1125.0 383.1 %copy-start.8 = (f32[96,384]{1,0:T(8,128)}, f32[96,384]{1,0:T(8,128)S(1)}, u32[]{:S(2)}) copy-start(f32[96,384]{1,0:T(8,128)S(1)} %broadcast_multiply_fusion) | copy-start | bytes 442372
  1186.9 25.8 slice-start.14
  1187.0 321.1 %copy-start.17 = (f32[96,384]{1,0:T(8,128)}, f32[96,384]{1,0:T(8,128)S(1)}, u32[]{:S(2)}) copy-start(f32[96,384]{1,0:T(8,128)S(1)} %get-tuple-element.94) | copy-start | bytes 442372
  1187.0 25.8 slice-start.15
  1187.0 25.8 slice-start.16
  1456.0 212.9 %all-to-all-start.5 = ((bf16[2,32,384,384]{3,1,0,2:T(8,128)(2,1)}), bf16[2,32,384,384]{3,1,0,2:T(8,128)(2,1)}, u32[]{:S(2)}, u32[]{:S(2)}) async-start(bf16[2,32,384,384]{3,1,0,2:T(8,128)(2,1)} %copy.283), calls=%async_computation.5 | async-start | bytes 37748736 | tf_op jit(solution)/shard_map/all_to_all | solution.py:32
  1761.1 51.1 %copy-start.39 = (bf16[2,128,512]{2,1,0:T(8,128)(2,1)S(1)}, bf16[2,128,512]{2,1,0:T(8,128)(2,1)}, u32[]{:S(2)}) copy-start(bf16[2,128,512]{2,1,0:T(8,128)(2,1)} %param.12) | copy-start | bytes 786436
  1873.7 24.9 copy-start.7
  1922.5 25.8 slice-start.17
  1922.5 25.7 slice-start.18
  1922.6 25.7 slice-start.19
  2187.6 213.0 %all-to-all-start.7 = ((bf16[2,32,384,384]{3,1,0,2:T(8,128)(2,1)}), bf16[2,32,384,384]{3,1,0,2:T(8,128)(2,1)}, u32[]{:S(2)}, u32[]{:S(2)}) async-start(bf16[2,32,384,384]{3,1,0,2:T(8,128)(2,1)} %copy.300), calls=%async_computation.7 | async-start | bytes 37748736 | tf_op jit(solution)/shard_map/all_to_all | solution.py:32
  2217.2 29.2 %slice-start = ((s8[18874368]{0:T(1024)(128)(4,1)}), s8[4194304]{0:T(1024)(128)(4,1)S(1)}, s32[]{:S(2)}) async-start(s8[18874368]{0:T(1024)(128)(4,1)} %bitcast.238), calls=%async_computation.8 | async-start | bytes 8388608
  2217.2 29.2 %slice-start.1 = ((s8[18874368]{0:T(1024)(128)(4,1)}), s8[2097152]{0:T(1024)(128)(4,1)S(1)}, s32[]{:S(2)}) async-start(s8[18874368]{0:T(1024)(128)(4,1)} %bitcast.238), calls=%async_computation.9 | async-start | bytes 4194304
  2217.2 29.2 %slice-start.11 = ((s8[9437184]{0:T(1024)(128)(4,1)}), s8[4194304]{0:T(1024)(128)(4,1)S(1)}, s32[]{:S(2)}) async-start(s8[9437184]{0:T(1024)(128)(4,1)} %bitcast.252), calls=%async_computation.19 | async-start | bytes 8388608
  2492.9 51.3 %copy-start.12 = (f32[96,384]{1,0:T(8,128)S(1)}, f32[96,384]{1,0:T(8,128)}, u32[]{:S(2)}) copy-start(f32[96,384]{1,0:T(8,128)} %copy-done.10) | copy-start | bytes 442372
  2492.9 51.3 %copy-start.23 = (f32[96,384]{1,0:T(8,128)S(1)}, f32[96,384]{1,0:T(8,128)}, u32[]{:S(2)}) copy-start(f32[96,384]{1,0:T(8,128)} %copy-done.22) | copy-start | bytes 442372
  2492.9 51.3 %copy-start.51 = (f32[128]{0:T(128)S(1)}, f32[128]{0:T(128)}, u32[]{:S(2)}) copy-start(f32[128]{0:T(128)} %copy-done.49) | copy-start | bytes 1540
  2492.9 51.3 %copy-start.59 = (f32[128]{0:T(128)S(1)}, f32[128]{0:T(128)}, u32[]{:S(2)}) copy-start(f32[128]{0:T(128)} %copy-done.57) | copy-start | bytes 1540
  (62 other events, 1151.9 us)
where the time goes:
time: 2680 us; the launch traced here: 2670 us
  blocking collectives  679 us (25%)
  local copies, waits for them, and re-layouts  597 us (22%)
  other arithmetic  521 us (19%)
  matrix products  452 us (17%)
  waiting for transfers between devices  381 us (14%)
  starting transfers between devices  36.2 us (1%)
    all_to_all x4, blocking collectives, to_channels(): lax.all_to_all(row_blocks, GROUP_AXIS, chan_dim, chan_dim + 1, tiled=True)  660 us
    all_to_all x4, waiting for transfers between devices, to_rows(): lax.all_to_all(chan_blocks, GROUP_AXIS, chan_dim + 1, chan_dim, tiled=True)  381 us
    reduce_sum x6, other arithmetic, layer_norm(): return centered * lax.rsqrt(variance + LN_EPS) * gain_vec + shift_vec  105 us
    another operation x2, other arithmetic  102 us
    another operation x2, local copies, waits for them, and re-layouts, update_backward(): jnp.stack([d_left.astype(jnp.bfloat16), d_right.astype(jnp.bfloat16)])  91.8 us
    another operation x4, other arithmetic, update_forward(): chan_pair = to_channels(jnp.stack([left_proj, right_proj]))  65.8 us
    convert_element_type x4, local copies, waits for them, and re-layouts, update_forward(): t_rows.astype(jnp.float32)  62.6 us
    convert_element_type x4, local copies, waits for them, and re-layouts, update_backward(): d_right_f = d_rows[1].astype(jnp.float32) * mask_f  62.5 us
  transfers between devices with their start and end apart: 4, of which 4 were waited for; matrix products, arithmetic and copies ran while one was open for 9% of the time, Pallas kernels for 0%

commit v1 on v0

v1 whole, which is shorter than its diff:
```python
import functools
import jax
import jax.numpy as jnp
from jax import lax
from jax.experimental import pallas as pl
from jax.experimental.pallas import tpu as pltpu
from jax.sharding import PartitionSpec as P

LN_EPS = 1e-5
AX = 'dap'
N = 384
C = 128
TI = 16
RB = 96
CB = 8
F32 = jnp.float32
BF16 = jnp.bfloat16
ICI_SWAP = [(0, 2), (2, 0), (1, 3), (3, 1)]
D2D_SWAP = [(0, 1), (1, 0), (2, 3), (3, 2)]
OWN, CROSS, PART, DIAG = 0, 2, 1, 3


def sig(v):
    return 0.5 * jnp.tanh(0.5 * v) + 0.5


def dot(a, b, ca, cb):
    return lax.dot_general(a, b, (((ca,), (cb,)), ((), ())), preferred_element_type=F32)


def hat_lanes(zr):
    mean = jnp.sum(zr, axis=-1, keepdims=True) * (1.0 / C)
    cen = zr - mean
    var = jnp.sum(cen * cen, axis=-1, keepdims=True) * (1.0 / C)
    rstd = lax.rsqrt(var + LN_EPS)
    return cen * rstd, rstd


def hat_rows(tr):
    mean = jnp.sum(tr, axis=0, keepdims=True) * (1.0 / C)
    cen = tr - mean
    var = jnp.sum(cen * cen, axis=0, keepdims=True) * (1.0 / C)
    rstd = lax.rsqrt(var + LN_EPS)
    return cen * rstd, rstd


def norm_x(zr, lnp_ref):
    xh, rstd = hat_lanes(zr)
    x = (xh * lnp_ref[0:1, :] + lnp_ref[1:2, :]).astype(BF16)
    return x, xh, rstd


def put_row(scr, i, val):
    for l in range(N // 128):
        scr[l, pl.ds(i, C, stride=TI), :] = val[:, l * 128:(l + 1) * 128]


def get_row(scr, i):
    return jnp.concatenate([scr[l, pl.ds(i, C, stride=TI), :] for l in range(N // 128)], axis=1)


def flush(scr, out_ref):
    for l in range(N // 128):
        out_ref[:, :, l * 128:(l + 1) * 128] = scr[l].reshape(C, TI, 128).astype(BF16)


def fill(scr, in_ref):
    for l in range(N // 128):
        scr[l] = in_ref[:, :, l * 128:(l + 1) * 128].astype(F32).reshape(C * TI, 128)


SCR = lambda: pltpu.VMEM((N // 128, C * TI, 128), F32)


def const_spec(shape):
    nd = len(shape)
    return pl.BlockSpec(shape, lambda *_: (0,) * nd)


def rows_spec(off=0):
    return pl.BlockSpec((TI, N, C), lambda i, *_: (i + off, 0, 0))


def chan_spec():
    return pl.BlockSpec((C, TI, N), lambda i, *_: (0, i, 0))


def cost(flops, nbytes, trans=0):
    return pl.CostEstimate(flops=int(flops), bytes_accessed=int(nbytes), transcendentals=int(trans))


def prep_body(base, z_ref, m_ref, lnp_ref, wt_ref, *rest):
    a_out, b_out, sa, sb = rest[-4:]

    def row(i, carry):
        zr = z_ref[i].astype(F32)
        x, _, _ = norm_x(zr, lnp_ref)
        mrow = m_ref[pl.ds(i, 1), :]
        p = dot(wt_ref[...], x, 1, 1)
        put_row(sa, i, mrow * sig(p[C:2 * C]) * p[0:C])
        put_row(sb, i, mrow * sig(p[3 * C:4 * C]) * p[2 * C:3 * C])
        return carry

    lax.fori_loop(0, TI, row, 0)
    flush(sa, a_out)
    flush(sb, b_out)


def prep(base, z, mask, lnp, wt, full=None):
    rows = z.shape[0]
    out = jax.ShapeDtypeStruct((C, N, N), BF16)
    spec = pl.BlockSpec((C, TI, N), lambda i, b: (0, b[0] + i, 0))
    extra = () if full is None else tuple(full)
    grid_spec = pltpu.PrefetchScalarGridSpec(
        num_scalar_prefetch=1, grid=(rows // TI,),
        in_specs=[rows_spec(), pl.BlockSpec((TI, N), lambda i, b: (i, 0)), const_spec((2, C)), const_spec((4 * C, C))]
        + [pl.BlockSpec(memory_space=pl.ANY)] * len(extra),
        out_specs=[spec, spec], scratch_shapes=[SCR(), SCR()])
    n = rows * N
    return pl.pallas_call(
        prep_body, grid_spec=grid_spec, out_shape=[out, out],
        input_output_aliases={5: 0, 6: 1} if extra else {},
        cost_estimate=cost(n * C * 4 * C * 2, n * C * 6, n * C * 2), name="prep",
    )(base, z, mask, lnp, wt, *extra)


def tri_out_body(idx, ao, ac, b, to, tc):
    for c in range(CB):
        lhs = jnp.concatenate([ao[c], ac[c]], axis=0)
        r = dot(lhs, b[c], 1, 1).astype(BF16)
        to[c] = r[:RB]
        tc[c] = r[RB:]


def row_block(k):
    return pl.BlockSpec((CB, RB, N), lambda c, idx: (c, idx[k], 0))


def part_block():
    return pl.BlockSpec((CB, RB, N), lambda c, idx: (c, 0, 0))


def full_block():
    return pl.BlockSpec((CB, N, N), lambda c, idx: (c, 0, 0))


PART_SHAPE = jax.ShapeDtypeStruct((C, RB, N), BF16)


def tri_call(body, idx, ins, specs, n_out, scratch, flops, name):
    grid_spec = pltpu.PrefetchScalarGridSpec(
        num_scalar_prefetch=1, grid=(C // CB,), in_specs=specs,
        out_specs=[part_block()] * n_out, scratch_shapes=scratch)
    return pl.pallas_call(body, grid_spec=grid_spec, out_shape=[PART_SHAPE] * n_out,
                          cost_estimate=cost(flops, 100e6), name=name)(idx, *ins)


def tri_out(idx, a, b):
    return tri_call(tri_out_body, idx, (a, a, b), [row_block(0), row_block(1), full_block()], 2, [], 2 * RB * N * N * C * 2, "tri_out")


def tri_in_body(idx, a, b, to, tc, s):
    ro = pl.multiple_of(idx[0] * RB, RB)
    rc = pl.multiple_of(idx[1] * RB, RB)
    for c in range(CB):
        s[c] = a[c].T
        lhs = jnp.concatenate([s[c, pl.ds(ro, RB), :], s[c, pl.ds(rc, RB), :]], axis=0)
        r = dot(lhs, b[c], 1, 0).astype(BF16)
        to[c] = r[:RB]
        tc[c] = r[RB:]


def tri_in(idx, a, b):
    return tri_call(tri_in_body, idx, (a, b), [full_block(), full_block()], 2, [pltpu.VMEM((CB, N, N), BF16)], 2 * RB * N * N * C * 2, "tri_in")


def gather_dt(idx, parts, c, s):
    for k, part in enumerate(parts):
        s[c, pl.ds(pl.multiple_of(idx[k] * RB, RB), RB), :] = part[c]


def tri_in_bwd_body(idx, d0, d1, d2, d3, ao, ac, bo, bc, dao, dac, dbo, dbc, s):
    for c in range(CB):
        gather_dt(idx, (d0, d1, d2, d3), c, s)
        da = dot(jnp.concatenate([bo[c], bc[c]], axis=0), s[c], 1, 1).astype(BF16)
        db = dot(jnp.concatenate([ao[c], ac[c]], axis=0), s[c], 1, 0).astype(BF16)
        dao[c] = da[:RB]
        dac[c] = da[RB:]
        dbo[c] = db[:RB]
        dbc[c] = db[RB:]


def tri_in_bwd(idx, dts, a, b):
    return tri_call(tri_in_bwd_body, idx, (*dts, a, a, b, b),
                    [part_block()] * 4 + [row_block(0), row_block(1)] * 2, 4, [pltpu.VMEM((CB, N, N), BF16)], 4 * RB * N * N * C * 2, "tri_in_bwd")


def tri_out_bwd_body(idx, d0, d1, d2, d3, a, b, da, db, s, st):
    ro = pl.multiple_of(idx[0] * RB, RB)
    for c in range(CB):
        gather_dt(idx, (d0, d1, d2, d3), c, s)
        da[c] = dot(d0[c], b[c], 1, 0).astype(BF16)
        st[c] = s[c].T
        db[c] = dot(st[c, pl.ds(ro, RB), :], a[c], 1, 0).astype(BF16)


def tri_out_bwd(idx, dts, a, b):
    return tri_call(tri_out_bwd_body, idx, (*dts, a, b), [part_block()] * 4 + [full_block()] * 2, 2,
                    [pltpu.VMEM((CB, N, N), BF16), pltpu.VMEM((CB, N, N), BF16)], 2 * RB * N * N * C * 2, "tri_out_bwd")


def finish_body(t_ref, z_ref, lnp_ref, wg_ref, lnq_ref, wo_ref, z_out, st):
    fill(st, t_ref)

    def row(i, carry):
        th, _ = hat_rows(get_row(st, i))
        y = (th * lnq_ref[:, 0:1] + lnq_ref[:, 1:2]).astype(BF16)
        upd = dot(y, wo_ref[...], 0, 0)
        zr = z_ref[i].astype(F32)
        x, _, _ = norm_x(zr, lnp_ref)
        gate = sig(dot(x, wg_ref[...], 1, 0))
        z_out[i] = (zr + gate * upd).astype(BF16)
        return carry

    lax.fori_loop(0, TI, row, 0)


def finish(t, z, lnp, wg, lnq, wo):
    n = RB * N
    return pl.pallas_call(
        finish_body, grid=(RB // TI,),
        in_specs=[chan_spec(), rows_spec(), const_spec((2, C)), const_spec((C, C)), const_spec((C, 2)), const_spec((C, C))],
        out_specs=rows_spec(), out_shape=jax.ShapeDtypeStruct((RB, N, C), BF16), scratch_shapes=[SCR()],
        cost_estimate=cost(n * C * C * 4, n * C * 6, n * C), name="finish",
    )(t, z, lnp, wg, lnq, wo)


def head_body(emit_z, emit_w, t_ref, z_ref, g_ref, lnp_ref, wg_ref, lnq_ref, wo_ref, *rest):
    rest = list(rest)
    st, sd = rest[-2:]
    dt_out, dg_out = rest[0], rest[1]
    k = 2
    if emit_z:
        z_out = rest[k]
        k += 1
    if emit_w:
        gwo, ggain, gshift = rest[k:k + 3]

        @pl.when(pl.program_id(0) == 0)
        def _():
            gwo[...] = jnp.zeros_like(gwo)
            ggain[...] = jnp.zeros_like(ggain)
            gshift[...] = jnp.zeros_like(gshift)

    fill(st, t_ref)

    def row(i, carry):
        th, rstd = hat_rows(get_row(st, i))
        gain = lnq_ref[:, 0:1]
        y = (th * gain + lnq_ref[:, 1:2]).astype(BF16)
        upd = dot(y, wo_ref[...], 0, 0)
        zr = z_ref[i].astype(F32)
        x, _, _ = norm_x(zr, lnp_ref)
        gate = sig(dot(x, wg_ref[...], 1, 0))
        if emit_z:
            z_out[i] = (zr + gate * upd).astype(BF16)
        d = g_ref[i].astype(F32)
        dgate = d * gate
        dg_out[i] = (dgate * upd * (1.0 - gate)).astype(BF16)
        du = dgate.astype(BF16)
        dy = dot(wo_ref[...], du, 1, 1).astype(BF16).astype(F32)
        dh = dy * gain
        m1 = jnp.sum(dh, axis=0, keepdims=True) * (1.0 / C)
        m2 = jnp.sum(dh * th, axis=0, keepdims=True) * (1.0 / C)
        put_row(sd, i, rstd * (dh - m1 - th * m2))
        if emit_w:
            gwo[...] += dot(y, du, 1, 0)
            ggain[...] += dy * th
            gshift[...] += dy
        return carry

    lax.fori_loop(0, TI, row, 0)
    flush(sd, dt_out)


def head(t, z, g, lnp, wg, lnq, wo, emit_z, emit_w):
    n = RB * N
    act = jax.ShapeDtypeStruct((RB, N, C), BF16)
    out_shape = [PART_SHAPE, act]
    out_specs = [chan_spec(), rows_spec()]
    if emit_z:
        out_shape.append(act)
        out_specs.append(rows_spec())
    if emit_w:
        for s in ((C, C), (C, N), (C, N)):
            out_shape.append(jax.ShapeDtypeStruct(s, F32))
            out_specs.append(const_spec(s))
    return pl.pallas_call(
        functools.partial(head_body, emit_z, emit_w), grid=(RB // TI,),
        in_specs=[chan_spec(), rows_spec(), rows_spec(), const_spec((2, C)), const_spec((C, C)), const_spec((C, 2)), const_spec((C, C))],
        out_specs=out_specs, out_shape=out_shape, scratch_shapes=[SCR(), SCR()],
        cost_estimate=cost(n * C * C * 6, n * C * 10, n * C), name="head",
    )(t, z, g, lnp, wg, lnq, wo)


def back_body(emit_w, da_ref, db_ref, z_ref, g_ref, dg_ref, m_ref, lnp_ref, wt_ref, w_ref, wg_ref, d_out, *rest):
    sa, sb = rest[-2:]
    if emit_w:
        gwp, gwg, gln = rest[:3]

        @pl.when(pl.program_id(0) == 0)
        def _():
            gwp[...] = jnp.zeros_like(gwp)
            gwg[...] = jnp.zeros_like(gwg)
            gln[...] = jnp.zeros_like(gln)

    fill(sa, da_ref)
    fill(sb, db_ref)

    def row(i, carry):
        zr = z_ref[i].astype(F32)
        x, xh, rstd = norm_x(zr, lnp_ref)
        p = dot(wt_ref[...], x, 1, 1)
        mrow = m_ref[pl.ds(i, 1), :]
        da = get_row(sa, i) * mrow
        s = sig(p[C:2 * C])
        t0 = da * s
        d0 = t0.astype(BF16)
        d1 = (t0 * p[0:C] * (1.0 - s)).astype(BF16)
        db = get_row(sb, i) * mrow
        s = sig(p[3 * C:4 * C])
        t0 = db * s
        d2 = t0.astype(BF16)
        d3 = (t0 * p[2 * C:3 * C] * (1.0 - s)).astype(BF16)
        dp = jnp.concatenate([d0, d1, d2, d3], axis=0)
        dg = dg_ref[i]
        dxt = dot(w_ref[...], dp, 1, 0) + dot(wg_ref[...], dg, 1, 1)
        dx = dxt.astype(BF16).T.astype(F32)
        dh = dx * lnp_ref[0:1, :]
        m1 = jnp.sum(dh, axis=-1, keepdims=True) * (1.0 / C)
        m2 = jnp.sum(dh * xh, axis=-1, keepdims=True) * (1.0 / C)
        d_out[i] = (g_ref[i].astype(F32) + rstd * (dh - m1 - xh * m2)).astype(BF16)
        if emit_w:
            gwp[...] += dot(dp, x, 1, 0)
            gwg[...] += dot(x, dg, 0, 0)
            gln[0:1, :] += jnp.sum(dx * xh, axis=0, keepdims=True)
            gln[1:2, :] += jnp.sum(dx, axis=0, keepdims=True)
        return carry

    lax.fori_loop(0, TI, row, 0)


def back(da, db, z, g, dg, mask, lnp, wt, w, wg, emit_w):
    n = RB * N
    out_shape = [jax.ShapeDtypeStruct((RB, N, C), BF16)]
    out_specs = [rows_spec()]
    if emit_w:
        for s in ((4 * C, C), (C, C), (2, C)):
            out_shape.append(jax.ShapeDtypeStruct(s, F32))
            out_specs.append(const_spec(s))
    return pl.pallas_call(
        functools.partial(back_body, emit_w), grid=(RB // TI,),
        in_specs=[chan_spec(), chan_spec(), rows_spec(), rows_spec(), rows_spec(), pl.BlockSpec((TI, N), lambda i: (i, 0)),
                  const_spec((2, C)), const_spec((4 * C, C)), const_spec((C, 4 * C)), const_spec((C, C))],
        out_specs=out_specs, out_shape=out_shape, scratch_shapes=[SCR(), SCR()],
        cost_estimate=cost(n * C * C * 20, n * C * 12, n * C * 2), name="back",
    )(da, db, z, g, dg, mask, lnp, wt, w, wg)


def solution(mesh):
    row_spec = P(('data', 'dap'), None, None)
    mask_spec = P(('data', 'dap'), None)
    full_spec = P()
    grad_spec = P('data', None, None)

    def ici(v):
        return lax.ppermute(v, AX, ICI_SWAP)

    def d2d(v):
        return lax.ppermute(v, AX, D2D_SWAP)

    def device_step(pair_act, pair_mask, d_pair_out, ln_pair, w_proj, w_gate, ln_chan, w_out):
        me = lax.axis_index(AX)
        blocks = jnp.stack([me ^ OWN, me ^ CROSS, me ^ PART, me ^ DIAG]).astype(jnp.int32)
        base = [blocks[k:k + 1] * (RB // TI) for k in range(4)]
        lnp = ln_pair.astype(F32)
        lnq = jnp.swapaxes(ln_chan, 1, 2).astype(F32)
        wt = jnp.swapaxes(w_proj, 1, 2)
        m_own = pair_mask.astype(F32)
        m_cross = ici(m_own)
        m_part = d2d(m_own)
        m_diag = d2d(m_cross)
        z_own = pair_act
        z_cross = ici(z_own)
        z_part = d2d(z_own)
        z_diag = d2d(z_cross)
        g_own = d_pair_out
        g_src, z_cross = lax.optimization_barrier((g_own, z_cross))
        g_cross = ici(g_src)

        a1, b1 = prep(base[0], z_own, m_own, lnp[0], wt[0])
        a1, b1 = prep(base[2], z_part, m_part, lnp[0], wt[0], (a1, b1))
        a1, b1 = prep(base[1], z_cross, m_cross, lnp[0], wt[0], (a1, b1))
        a1, b1 = prep(base[3], z_diag, m_diag, lnp[0], wt[0], (a1, b1))
        t1o, t1c = tri_out(blocks, a1, b1)
        y_own = finish(t1o, z_own, lnp[0], w_gate[0], lnq[0], w_out[0])
        y_part = d2d(y_own)
        y_cross = finish(t1c, z_cross, lnp[0], w_gate[0], lnq[0], w_out[0])
        y_diag = d2d(y_cross)

        a2, b2 = prep(base[0], y_own, m_own, lnp[1], wt[1])
        a2, b2 = prep(base[1], y_cross, m_cross, lnp[1], wt[1], (a2, b2))
        a2, b2 = prep(base[2], y_part, m_part, lnp[1], wt[1], (a2, b2))
        a2, b2 = prep(base[3], y_diag, m_diag, lnp[1], wt[1], (a2, b2))
        t2o, t2c = tri_in(blocks, a2, b2)
        dt2o, dg2o, pair_out, gwo2, gq2g, gq2s = head(t2o, y_own, g_own, lnp[1], w_gate[1], lnq[1], w_out[1], True, True)
        dt2p = d2d(dt2o)
        dt2c, dg2c = head(t2c, y_cross, g_cross, lnp[1], w_gate[1], lnq[1], w_out[1], False, False)
        dt2d = d2d(dt2c)
        dao, dac, dbo, dbc = tri_in_bwd(blocks, (dt2o, dt2c, dt2p, dt2d), a2, b2)
        dy_own, gwp2, gwg2, gln2 = back(dao, dbo, y_own, g_own, dg2o, m_own, lnp[1], wt[1], w_proj[1], w_gate[1], True)
        dy_cross, = back(dac, dbc, y_cross, g_cross, dg2c, m_cross, lnp[1], wt[1], w_proj[1], w_gate[1], False)

        dt1o, dg1o, gwo1, gq1g, gq1s = head(t1o, z_own, dy_own, lnp[0], w_gate[0], lnq[0], w_out[0], False, True)
        dt1p = d2d(dt1o)
        dt1c, _ = head(t1c, z_cross, dy_cross, lnp[0], w_gate[0], lnq[0], w_out[0], False, False)
        dt1d = d2d(dt1c)
        da1, db1 = tri_out_bwd(blocks, (dt1o, dt1c, dt1p, dt1d), a1, b1)
        d_pair, gwp1, gwg1, gln1 = back(da1, db1, z_own, dy_own, dg1o, m_own, lnp[0], wt[0], w_proj[0], w_gate[0], True)

        def chan(gg, gs):
            return jnp.stack([jnp.sum(gg, axis=1), jnp.sum(gs, axis=1)])

        local = (jnp.stack([gln1, gln2]),
                 jnp.stack([gwp1.T, gwp2.T]),
                 jnp.stack([gwg1, gwg2]),
                 jnp.stack([chan(gq1g, gq1s), chan(gq2g, gq2s)]),
                 jnp.stack([gwo1, gwo2]))
        sums = lax.psum(local, AX)
        return (pair_out, d_pair) + tuple(v.astype(BF16) for v in sums)

    return jax.shard_map(device_step, mesh=mesh, in_specs=(row_spec, mask_spec, row_spec, full_spec, full_spec, full_spec, full_spec, full_spec), out_specs=(row_spec, row_spec, grad_spec, grad_spec, grad_spec, grad_spec, grad_spec), check_vma=False)
```

time: 2680 us -> 1700 us (0.63)
  Pallas kernels: 0 us -> 1430 us
  blocking collectives: 679 us -> 21.3 us
  local copies, waits for them, and re-layouts: 597 us -> 7.5 us
  other arithmetic: 521 us -> 7.89 us
  matrix products: 452 us -> 0 us
  waiting for transfers between devices: 381 us -> 228 us
  starting transfers between devices: 36.2 us -> 7.5 us
    pallas_call x0 -> x21, Pallas kernels: none -> 1430 us  [the longest x8 511 us: prep(): pl.pallas_call(prep_body, grid_spec=grid_spec, out_shape=[out, out], inpu...]
    all_to_all x4 -> x0, blocking collectives: 660 us -> none  [to_channels(): lax.all_to_all(row_blocks, GROUP_AXIS, chan_dim, chan_dim + 1, tiled=True)]
    dot_general x24 -> x0, matrix products: 452 us -> none  [the longest x2 60.2 us: update_forward(): jnp.einsum('ijd,de->eij', x_norm, w_proj, preferred_element_type=jnp.floa...]
    all_to_all x4 -> x0, waiting for transfers between devices: 381 us -> none  [to_rows(): lax.all_to_all(chan_blocks, GROUP_AXIS, chan_dim + 1, chan_dim, tiled=True)]
    convert_element_type x18 -> x1, local copies, waits for them, and re-layouts: 256 us -> 0.8 us  [device_step(): lnq = jnp.swapaxes(ln_chan, 1, 2).astype(F32)]
    ppermute x0 -> x13, waiting for transfers between devices: none -> 228 us  [the longest x3 203 us: ici(): return lax.ppermute(v, AX, ICI_SWAP)]
    another operation x17 -> x8, other arithmetic: 189 us -> 4.01 us  [the longest x1 0.99 us: device_step(): jnp.stack([gwp1.T, gwp2.T])]
    convert_element_type x14 -> x2, other arithmetic: 182 us -> 1.6 us  [the longest x1 0.92 us: device_step(): m_own = pair_mask.astype(F32)]
  transfers between devices with their start and end apart: 4 -> 13, of which waited for: 4 -> 3; matrix products, arithmetic and copies ran while one was open for 9% -> 1% of each run, Pallas kernels for 0% -> 48%
where the time goes in v1:
time: 1700 us
  Pallas kernels  1430 us (84%)
  waiting for transfers between devices  228 us (13%)
  blocking collectives  21.3 us (1%)
    pallas_call x8, Pallas kernels, prep(): pl.pallas_call(prep_body, grid_spec=grid_spec, out_shape=[out, out], inpu...  511 us
    pallas_call x3, Pallas kernels, back(): pl.pallas_call(functools.partial(back_body, emit_w), grid=(RB // TI,), in...  333 us
    pallas_call x4, Pallas kernels, head(): pl.pallas_call(functools.partial(head_body, emit_z, emit_w), grid=(RB //...  306 us
    ppermute x3, waiting for transfers between devices, ici(): return lax.ppermute(v, AX, ICI_SWAP)  203 us
    pallas_call x4, Pallas kernels, tri_call(): pl.pallas_call(body, grid_spec=grid_spec, out_shape=[PART_SHAPE] * n_out,...  165 us
    pallas_call x2, Pallas kernels, finish(): pl.pallas_call(finish_body, grid=(RB // TI,), in_specs=[chan_spec(), rows...  116 us
  transfers between devices with their start and end apart: 13, of which 3 were waited for; matrix products, arithmetic and copies ran while one was open for 1% of the time, Pallas kernels for 48%

profile of v1, /device:TPU:0, one launch (start us, length us, event | category | flops | bytes accessed | tf_op | source)
XLA Modules:
  0.0 1703.8 jit_solution(12636342189587120338)
XLA Ops:
  0.6 3.4 collective-permute-start
  4.0 202.9 %collective-permute-done.z_ref = bf16[96,384,128]{2,1,0:T(8,128)(2,1)} collective-permute-done((bf16[96,384,128]{2,1,0:T(8,128)(2,1)}, bf16[96,384,128]{2,1,0:T(8,128)(2,1)}, u32[]{:S(2)}, u32[]{:S(2)}) %collective-permute-start) | collective-permute-done | bytes 9437216 | tf_op jit(solution)/shard_map/ppermute | solution.py:377
  206.9 0.9 convert_element_type.27.m_ref
  208.4 1.7 collective-permute-start.2
  211.6 1.1 copy.27
  214.7 63.9 %prep.8 = (bf16[128,384,384]{2,1,0:T(8,128)(2,1)}, bf16[128,384,384]{2,1,0:T(8,128)(2,1)}) custom-call(s32[1]{0:T(128)S(6)} %mul.15.base, bf16[96,384,128]{2,1,0:T(8,128)(2,1)} %z_ref.7, f32[96,384]{1,0:T(8,128)} %copy-done, f32[2,128]{1,0:T(2,128)} %get-tuple-element.130.lnp_ref, bf16[512,128]{1,0:T(8,128)(2,1)} %get-tuple-element.122.wt_ref), custom_call_target="tpu_custom_call" | custom-call | flops 4831838208 | bytes 28311552 | tf_op jit(solution)/shard_map/prep/pallas_call | solution.py:120
  280.7 63.8 %prep.9 = (bf16[128,384,384]{2,1,0:T(8,128)(2,1)}, bf16[128,384,384]{2,1,0:T(8,128)(2,1)}) custom-call(s32[1]{0:T(128)S(6)} %mul.14.base, bf16[96,384,128]{2,1,0:T(8,128)(2,1)} %collective-permute-done.4.z_ref, f32[96,384]{1,0:T(8,128)} %copy-done.3, f32[2,128]{1,0:T(2,128)} %get-tuple-element.130.lnp_ref, ...), custom_call_target="tpu_custom_call", output_to_operand_aliasing={{0}: (5, {}), {1}: (6, {})} | custom-call | flops 4831838208 | bytes 28311552 | tf_op jit(solution)/shard_map/prep/pallas_call | solution.py:120
  344.5 63.8 %prep.10 = (bf16[128,384,384]{2,1,0:T(8,128)(2,1)}, bf16[128,384,384]{2,1,0:T(8,128)(2,1)}) custom-call(s32[1]{0:T(128)S(6)} %mul.13.base, bf16[96,384,128]{2,1,0:T(8,128)(2,1)} %collective-permute-done.z_ref, f32[96,384]{1,0:T(8,128)} %copy-done.1, f32[2,128]{1,0:T(2,128)} %get-tuple-element.130.lnp_ref, ...), custom_call_target="tpu_custom_call", output_to_operand_aliasing={{0}: (5, {}), {1}: (6, {})} | custom-call | flops 4831838208 | bytes 28311552 | tf_op jit(solution)/shard_map/prep/pallas_call | solution.py:120
  409.0 63.8 %prep.11 = (bf16[128,384,384]{2,1,0:T(8,128)(2,1)}, bf16[128,384,384]{2,1,0:T(8,128)(2,1)}) custom-call(s32[1]{0:T(128)S(6)} %mul.12.base, bf16[96,384,128]{2,1,0:T(8,128)(2,1)} %collective-permute-done.1.z_ref, f32[96,384]{1,0:T(8,128)} %copy-done.4, f32[2,128]{1,0:T(2,128)} %get-tuple-element.130.lnp_ref, ...), custom_call_target="tpu_custom_call", output_to_operand_aliasing={{0}: (5, {}), {1}: (6, {})} | custom-call | flops 4831838208 | bytes 28311552 | tf_op jit(solution)/shard_map/prep/pallas_call | solution.py:120
  472.9 33.3 %tri_out.1 = (bf16[128,96,384]{2,1,0:T(8,128)(2,1)}, bf16[128,96,384]{2,1,0:T(8,128)(2,1)}) custom-call(s32[4]{0:T(128)} %pad_add_fusion.idx, bf16[128,384,384]{2,1,0:T(8,128)(2,1)} %get-tuple-element.64.ao.ac.a, bf16[128,384,384]{2,1,0:T(8,128)(2,1)} %get-tuple-element.64.ao.ac.a, bf16[128,384,384]{2,1,0:T(8,128)(2,1)} %get-tuple-element.65.b), custom_call_target="tpu_custom_call" | custom-call | flops 7247757312 | bytes 100000000 | tf_op jit(solution)/shard_map/tri_out/pallas_call | solution.py:154
  506.2 57.8 %finish.3.z_ref = bf16[96,384,128]{2,1,0:T(8,128)(2,1)} custom-call(bf16[128,96,384]{2,1,0:T(8,128)(2,1)} %get-tuple-element.67.t_ref, bf16[96,384,128]{2,1,0:T(8,128)(2,1)} %z_ref.7, f32[2,128]{1,0:T(2,128)} %get-tuple-element.130.lnp_ref, bf16[128,128]{1,0:T(8,128)(2,1)} %get-tuple-element.131.wg_ref, f32[128,2]{1,0:T(8,128)} %get-tuple-element.124.lnq_ref, ...), custom_call_target="tpu_custom_call" | custom-call | flops 2415919104 | bytes 28311552 | tf_op jit(solution)/shard_map/finish/pallas_call | solution.py:230
  564.6 57.9 %finish.2.z_ref = bf16[96,384,128]{2,1,0:T(8,128)(2,1)} custom-call(bf16[128,96,384]{2,1,0:T(8,128)(2,1)} %get-tuple-element.66.t_ref, bf16[96,384,128]{2,1,0:T(8,128)(2,1)} %collective-permute-done.z_ref, f32[2,128]{1,0:T(2,128)} %get-tuple-element.130.lnp_ref, bf16[128,128]{1,0:T(8,128)(2,1)} %get-tuple-element.131.wg_ref, ...), custom_call_target="tpu_custom_call" | custom-call | flops 2415919104 | bytes 28311552 | tf_op jit(solution)/shard_map/finish/pallas_call | solution.py:230
  622.7 63.8 %prep.12 = (bf16[128,384,384]{2,1,0:T(8,128)(2,1)}, bf16[128,384,384]{2,1,0:T(8,128)(2,1)}) custom-call(s32[1]{0:T(128)S(6)} %mul.15.base, bf16[96,384,128]{2,1,0:T(8,128)(2,1)} %finish.3.z_ref, f32[96,384]{1,0:T(8,128)} %copy-done, f32[2,128]{1,0:T(2,128)} %get-tuple-element.129.lnp_ref, bf16[512,128]{1,0:T(8,128)(2,1)} %get-tuple-element.121.wt_ref), custom_call_target="tpu_custom_call" | custom-call | flops 4831838208 | bytes 28311552 | tf_op jit(solution)/shard_map/prep/pallas_call | solution.py:120
  686.5 63.8 %prep.13 = (bf16[128,384,384]{2,1,0:T(8,128)(2,1)}, bf16[128,384,384]{2,1,0:T(8,128)(2,1)}) custom-call(s32[1]{0:T(128)S(6)} %mul.13.base, bf16[96,384,128]{2,1,0:T(8,128)(2,1)} %finish.2.z_ref, f32[96,384]{1,0:T(8,128)} %copy-done.1, f32[2,128]{1,0:T(2,128)} %get-tuple-element.129.lnp_ref, ...), custom_call_target="tpu_custom_call", output_to_operand_aliasing={{0}: (5, {}), {1}: (6, {})} | custom-call | flops 4831838208 | bytes 28311552 | tf_op jit(solution)/shard_map/prep/pallas_call | solution.py:120
  750.3 63.9 %prep.14 = (bf16[128,384,384]{2,1,0:T(8,128)(2,1)}, bf16[128,384,384]{2,1,0:T(8,128)(2,1)}) custom-call(s32[1]{0:T(128)S(6)} %mul.14.base, bf16[96,384,128]{2,1,0:T(8,128)(2,1)} %collective-permute-done.7.z_ref, f32[96,384]{1,0:T(8,128)} %copy-done.3, f32[2,128]{1,0:T(2,128)} %get-tuple-element.129.lnp_ref, ...), custom_call_target="tpu_custom_call", output_to_operand_aliasing={{0}: (5, {}), {1}: (6, {})} | custom-call | flops 4831838208 | bytes 28311552 | tf_op jit(solution)/shard_map/prep/pallas_call | solution.py:120
  814.2 63.8 %prep.15 = (bf16[128,384,384]{2,1,0:T(8,128)(2,1)}, bf16[128,384,384]{2,1,0:T(8,128)(2,1)}) custom-call(s32[1]{0:T(128)S(6)} %mul.12.base, bf16[96,384,128]{2,1,0:T(8,128)(2,1)} %collective-permute-done.6.z_ref, f32[96,384]{1,0:T(8,128)} %copy-done.4, f32[2,128]{1,0:T(2,128)} %get-tuple-element.129.lnp_ref, ...), custom_call_target="tpu_custom_call", output_to_operand_aliasing={{0}: (5, {}), {1}: (6, {})} | custom-call | flops 4831838208 | bytes 28311552 | tf_op jit(solution)/shard_map/prep/pallas_call | solution.py:120
  878.0 37.9 %tri_in.1 = (bf16[128,96,384]{2,1,0:T(8,128)(2,1)}, bf16[128,96,384]{2,1,0:T(8,128)(2,1)}) custom-call(s32[4]{0:T(128)} %pad_add_fusion.idx, bf16[128,384,384]{2,1,0:T(8,128)(2,1)} %get-tuple-element.74.a.ao.ac, bf16[128,384,384]{2,1,0:T(8,128)(2,1)} %get-tuple-element.75.b.bo.bc), custom_call_target="tpu_custom_call" | custom-call | flops 7247757312 | bytes 100000000 | tf_op jit(solution)/shard_map/tri_in/pallas_call | solution.py:154
  916.0 73.4 %head.5 = (bf16[128,96,384]{2,1,0:T(8,128)(2,1)}, bf16[96,384,128]{2,1,0:T(8,128)(2,1)}) custom-call(bf16[128,96,384]{2,1,0:T(8,128)(2,1)} %get-tuple-element.79.t_ref, bf16[96,384,128]{2,1,0:T(8,128)(2,1)} %finish.2.z_ref, bf16[96,384,128]{2,1,0:T(8,128)(2,1)} %collective-permute-done.8.g_ref, f32[2,128]{1,0:T(2,128)} %get-tuple-element.129.lnp_ref, ...), custom_call_target="tpu_custom_call" | custom-call | flops 3623878656 | bytes 47185920 | tf_op jit(solution)/shard_map/head/pallas_call | solution.py:298
  989.7 80.0 %head.4 = (bf16[128,96,384]{2,1,0:T(8,128)(2,1)}, bf16[96,384,128]{2,1,0:T(8,128)(2,1)}, bf16[96,384,128]{2,1,0:T(8,128)(2,1)}, f32[128,128]{1,0:T(8,128)}, f32[128,384]{1,0:T(8,128)}, /*index=5*/f32[128,384]{1,0:T(8,128)}) custom-call(bf16[128,96,384]{2,1,0:T(8,128)(2,1)} %get-tuple-element.76.t_ref, bf16[96,384,128]{2,1,0:T(8,128)(2,1)} %finish.3.z_ref, ...), custom_call_target="tpu_custom_call" | custom-call | flops 3623878656 | bytes 47185920 | tf_op jit(solution)/shard_map/head/pallas_call | solution.py:298
  1070.6 13.7 collective-permute-done.9.d2
  1084.4 48.0 %tri_in_bwd.1 = (bf16[128,96,384]{2,1,0:T(8,128)(2,1)}, bf16[128,96,384]{2,1,0:T(8,128)(2,1)}, bf16[128,96,384]{2,1,0:T(8,128)(2,1)}, bf16[128,96,384]{2,1,0:T(8,128)(2,1)}) custom-call(s32[4]{0:T(128)} %pad_add_fusion.idx, bf16[128,96,384]{2,1,0:T(8,128)(2,1)} %get-tuple-element.78.d0, bf16[128,96,384]{2,1,0:T(8,128)(2,1)} %get-tuple-element.81.d1, ...), custom_call_target="tpu_custom_call" | custom-call | flops 14495514624 | bytes 100000000 | tf_op jit(solution)/shard_map/tri_in_bwd/pallas_call | solution.py:154
  1132.3 110.0 %back.4.g_ref = bf16[96,384,128]{2,1,0:T(8,128)(2,1)} custom-call(bf16[128,96,384]{2,1,0:T(8,128)(2,1)} %get-tuple-element.87.da_ref, bf16[128,96,384]{2,1,0:T(8,128)(2,1)} %get-tuple-element.88.db_ref, bf16[96,384,128]{2,1,0:T(8,128)(2,1)} %finish.2.z_ref, bf16[96,384,128]{2,1,0:T(8,128)(2,1)} %collective-permute-done.8.g_ref, ...), custom_call_target="tpu_custom_call" | custom-call | flops 12079595520 | bytes 56623104 | tf_op jit(solution)/shard_map/back/pallas_call | solution.py:361
  1242.3 73.5 %head.7 = (bf16[128,96,384]{2,1,0:T(8,128)(2,1)}, bf16[96,384,128]{2,1,0:T(8,128)(2,1)}) custom-call(bf16[128,96,384]{2,1,0:T(8,128)(2,1)} %get-tuple-element.66.t_ref, bf16[96,384,128]{2,1,0:T(8,128)(2,1)} %collective-permute-done.z_ref, bf16[96,384,128]{2,1,0:T(8,128)(2,1)} %back.4.g_ref, f32[2,128]{1,0:T(2,128)} %get-tuple-element.130.lnp_ref, ...), custom_call_target="tpu_custom_call" | custom-call | flops 3623878656 | bytes 47185920 | tf_op jit(solution)/shard_map/head/pallas_call | solution.py:298
  1315.8 111.6 %back.3 = (bf16[96,384,128]{2,1,0:T(8,128)(2,1)}, f32[512,128]{1,0:T(8,128)}, f32[128,128]{1,0:T(8,128)}, f32[2,128]{1,0:T(2,128)}) custom-call(bf16[128,96,384]{2,1,0:T(8,128)(2,1)} %get-tuple-element.82.da_ref, bf16[128,96,384]{2,1,0:T(8,128)(2,1)} %get-tuple-element.83.db_ref, bf16[96,384,128]{2,1,0:T(8,128)(2,1)} %finish.3.z_ref, ...), custom_call_target="tpu_custom_call" | custom-call | flops 12079595520 | bytes 56623104 | tf_op jit(solution)/shard_map/back/pallas_call | solution.py:361
  1427.5 79.1 %head.6 = (bf16[128,96,384]{2,1,0:T(8,128)(2,1)}, bf16[96,384,128]{2,1,0:T(8,128)(2,1)}, f32[128,128]{1,0:T(8,128)}, f32[128,384]{1,0:T(8,128)}, f32[128,384]{1,0:T(8,128)}) custom-call(bf16[128,96,384]{2,1,0:T(8,128)(2,1)} %get-tuple-element.67.t_ref, bf16[96,384,128]{2,1,0:T(8,128)(2,1)} %z_ref.7, bf16[96,384,128]{2,1,0:T(8,128)(2,1)} %get-tuple-element.85.g_ref, ...), custom_call_target="tpu_custom_call" | custom-call | flops 3623878656 | bytes 47185920 | tf_op jit(solution)/shard_map/head/pallas_call | solution.py:298
  1507.3 1.0 reduce_sum.36
  1508.4 1.0 reduce_sum.37
  1510.3 11.1 collective-permute-done.11.d2
  1521.4 46.2 %tri_out_bwd.1 = (bf16[128,96,384]{2,1,0:T(8,128)(2,1)}, bf16[128,96,384]{2,1,0:T(8,128)(2,1)}) custom-call(s32[4]{0:T(128)} %pad_add_fusion.idx, bf16[128,96,384]{2,1,0:T(8,128)(2,1)} %get-tuple-element.86.d0, bf16[128,96,384]{2,1,0:T(8,128)(2,1)} %get-tuple-element.90.d1, bf16[128,96,384]{2,1,0:T(8,128)(2,1)} %collective-permute-done.11.d2, ...), custom_call_target="tpu_custom_call" | custom-call | flops 7247757312 | bytes 100000000 | tf_op jit(solution)/shard_map/tri_out_bwd/pallas_call | solution.py:154
  1567.6 111.5 %back.5 = (bf16[96,384,128]{2,1,0:T(8,128)(2,1)}, f32[512,128]{1,0:T(8,128)}, f32[128,128]{1,0:T(8,128)}, f32[2,128]{1,0:T(2,128)}) custom-call(bf16[128,96,384]{2,1,0:T(8,128)(2,1)} %get-tuple-element.91.da_ref, bf16[128,96,384]{2,1,0:T(8,128)(2,1)} %get-tuple-element.92.db_ref, bf16[96,384,128]{2,1,0:T(8,128)(2,1)} %z_ref.7, ...), custom_call_target="tpu_custom_call" | custom-call | flops 12079595520 | bytes 56623104 | tf_op jit(solution)/shard_map/back/pallas_call | solution.py:361
  1680.6 1.0 pad_maximum_fusion
  1681.6 21.3 %all-reduce.2 = (bf16[2,2,128]{2,1,0:T(2,128)(2,1)}, bf16[2,128,512]{1,2,0:T(8,128)(2,1)S(1)}, bf16[2,128,128]{2,1,0:T(8,128)(2,1)}, bf16[2,2,128]{2,1,0:T(2,128)(2,1)}, bf16[2,128,128]{2,1,0:T(8,128)(2,1)}) all-reduce(f32[2,2,128]{2,1,0:T(2,128)S(1)} %pad_maximum_fusion.3, ...), channel_id=1, replica_groups=mesh['data'=2,'dap'=4] {'dap'}, use_global_device_ids=true, to_apply=%region_0.0 | all-reduce | flops 197632 | bytes 1185792 | tf_op jit(solution)/shard_map/psum | solution.py:439
  (64 shorter events, 12.7 us)
Async XLA Ops:
  0.6 206.3 %collective-permute-start = (bf16[96,384,128]{2,1,0:T(8,128)(2,1)}, bf16[96,384,128]{2,1,0:T(8,128)(2,1)}, u32[]{:S(2)}, u32[]{:S(2)}) collective-permute-start(bf16[96,384,128]{2,1,0:T(8,128)(2,1)} %z_ref.7), channel_id=1, source_target_pairs={{0,2},{2,0},{1,3},{3,1},{4,6},{6,4},{5,7},{7,5}} | collective-permute-start | bytes 28311560 | tf_op jit(solution)/shard_map/ppermute | solution.py:377
  4.0 276.0 %collective-permute-start.4 = (bf16[96,384,128]{2,1,0:T(8,128)(2,1)}, bf16[96,384,128]{2,1,0:T(8,128)(2,1)}, u32[]{:S(2)}, u32[]{:S(2)}) collective-permute-start(bf16[96,384,128]{2,1,0:T(8,128)(2,1)} %z_ref.7), channel_id=1, source_target_pairs={{0,1},{1,0},{2,3},{3,2},{4,5},{5,4},{6,7},{7,6}} | collective-permute-start | bytes 28311560 | tf_op jit(solution)/shard_map/ppermute | solution.py:380
  206.9 201.4 %collective-permute-start.1 = (bf16[96,384,128]{2,1,0:T(8,128)(2,1)}, bf16[96,384,128]{2,1,0:T(8,128)(2,1)}, u32[]{:S(2)}, u32[]{:S(2)}) collective-permute-start(bf16[96,384,128]{2,1,0:T(8,128)(2,1)} %collective-permute-done.z_ref), channel_id=1, source_target_pairs={{0,1},{1,0},{2,3},{3,2},{4,5},{5,4},{6,7},{7,6}} | collective-permute-start | bytes 28311560 | tf_op jit(solution)/shard_map/ppermute | solution.py:380
  207.9 6.9 copy-start
  207.9 72.1 %collective-permute-start.5 = (f32[96,384]{1,0:T(8,128)S(1)}, f32[96,384]{1,0:T(8,128)S(1)}, u32[]{:S(2)}, u32[]{:S(2)}) collective-permute-start(f32[96,384]{1,0:T(8,128)S(1)} %convert_element_type.27.m_ref), channel_id=1, source_target_pairs={{0,1},{1,0},{2,3},{3,2},{4,5},{5,4},{6,7},{7,6}} | collective-permute-start | bytes 442376 | tf_op jit(solution)/shard_map/ppermute | solution.py:380
  208.4 71.6 %collective-permute-start.2 = (f32[96,384]{1,0:T(8,128)S(1)}, f32[96,384]{1,0:T(8,128)S(1)}, u32[]{:S(2)}, u32[]{:S(2)}) collective-permute-start(f32[96,384]{1,0:T(8,128)S(1)} %convert_element_type.27.m_ref), channel_id=1, source_target_pairs={{0,2},{2,0},{1,3},{3,1},{4,6},{6,4},{5,7},{7,5}} | collective-permute-start | bytes 442376 | tf_op jit(solution)/shard_map/ppermute | solution.py:377
  212.7 65.9 %copy-start.8 = (bf16[2,128,128]{2,1,0:T(8,128)(2,1)S(1)}, bf16[2,128,128]{2,1,0:T(8,128)(2,1)}, u32[]{:S(2)}) copy-start(bf16[2,128,128]{2,1,0:T(8,128)(2,1)} %param.15) | copy-start | bytes 196612
  212.7 65.9 %copy-start.9 = (bf16[2,128,128]{2,1,0:T(8,128)(2,1)S(1)}, bf16[2,128,128]{2,1,0:T(8,128)(2,1)}, u32[]{:S(2)}) copy-start(bf16[2,128,128]{2,1,0:T(8,128)(2,1)} %param.13) | copy-start | bytes 196612
  280.0 64.5 %copy-start.1 = (f32[96,384]{1,0:T(8,128)}, f32[96,384]{1,0:T(8,128)S(1)}, u32[]{:S(2)}) copy-start(f32[96,384]{1,0:T(8,128)S(1)} %collective-permute-done.2.m_ref) | copy-start | bytes 442372
  280.0 128.4 %collective-permute-start.3 = (f32[96,384]{1,0:T(8,128)S(1)}, f32[96,384]{1,0:T(8,128)S(1)}, u32[]{:S(2)}, u32[]{:S(2)}) collective-permute-start(f32[96,384]{1,0:T(8,128)S(1)} %collective-permute-done.2.m_ref), channel_id=1, source_target_pairs={{0,1},{1,0},{2,3},{3,2},{4,5},{5,4},{6,7},{7,6}} | collective-permute-start | bytes 442376 | tf_op jit(solution)/shard_map/ppermute | solution.py:380
  280.0 0.7 copy-start.3
  408.4 0.7 copy-start.4
  564.0 186.3 %collective-permute-start.7 = (bf16[96,384,128]{2,1,0:T(8,128)(2,1)}, bf16[96,384,128]{2,1,0:T(8,128)(2,1)}, u32[]{:S(2)}, u32[]{:S(2)}) collective-permute-start(bf16[96,384,128]{2,1,0:T(8,128)(2,1)} %finish.3.z_ref), channel_id=1, source_target_pairs={{0,1},{1,0},{2,3},{3,2},{4,5},{5,4},{6,7},{7,6}} | collective-permute-start | bytes 28311560 | tf_op jit(solution)/shard_map/ppermute | solution.py:380
  622.5 191.8 %collective-permute-start.6 = (bf16[96,384,128]{2,1,0:T(8,128)(2,1)}, bf16[96,384,128]{2,1,0:T(8,128)(2,1)}, u32[]{:S(2)}, u32[]{:S(2)}) collective-permute-start(bf16[96,384,128]{2,1,0:T(8,128)(2,1)} %finish.2.z_ref), channel_id=1, source_target_pairs={{0,1},{1,0},{2,3},{3,2},{4,5},{5,4},{6,7},{7,6}} | collective-permute-start | bytes 28311560 | tf_op jit(solution)/shard_map/ppermute | solution.py:380
  622.5 293.5 %collective-permute-start.8 = (bf16[96,384,128]{2,1,0:T(8,128)(2,1)}, bf16[96,384,128]{2,1,0:T(8,128)(2,1)}, u32[]{:S(2)}, u32[]{:S(2)}) collective-permute-start(bf16[96,384,128]{2,1,0:T(8,128)(2,1)} %g_ref.3), channel_id=1, source_target_pairs={{0,2},{2,0},{1,3},{3,1},{4,6},{6,4},{5,7},{7,5}} | collective-permute-start | bytes 28311560 | tf_op jit(solution)/shard_map/ppermute | solution.py:377
  989.3 81.3 %collective-permute-start.10 = (bf16[128,96,384]{2,1,0:T(8,128)(2,1)}, bf16[128,96,384]{2,1,0:T(8,128)(2,1)}, u32[]{:S(2)}, u32[]{:S(2)}) collective-permute-start(bf16[128,96,384]{2,1,0:T(8,128)(2,1)} %get-tuple-element.81.d1), channel_id=1, source_target_pairs={{0,1},{1,0},{2,3},{3,2},{4,5},{5,4},{6,7},{7,6}} | collective-permute-start | bytes 28311560 | tf_op jit(solution)/shard_map/ppermute | solution.py:380
  989.7 80.2 %copy-start.2 = (bf16[2,128,512]{2,1,0:T(8,128)(2,1)S(1)}, bf16[2,128,512]{2,1,0:T(8,128)(2,1)}, u32[]{:S(2)}) copy-start(bf16[2,128,512]{2,1,0:T(8,128)(2,1)} %param.12) | copy-start | bytes 786436
  1069.7 14.6 collective-permute-start.9
  1315.8 194.5 %collective-permute-start.12 = (bf16[128,96,384]{2,1,0:T(8,128)(2,1)}, bf16[128,96,384]{2,1,0:T(8,128)(2,1)}, u32[]{:S(2)}, u32[]{:S(2)}) collective-permute-start(bf16[128,96,384]{2,1,0:T(8,128)(2,1)} %get-tuple-element.90.d1), channel_id=1, source_target_pairs={{0,1},{1,0},{2,3},{3,2},{4,5},{5,4},{6,7},{7,6}} | collective-permute-start | bytes 28311560 | tf_op jit(solution)/shard_map/ppermute | solution.py:380
  1427.4 79.6 %copy-start.7 = (f32[128,384]{1,0:T(8,128)S(1)}, f32[128,384]{1,0:T(8,128)}, u32[]{:S(2)}) copy-start(f32[128,384]{1,0:T(8,128)} %get-tuple-element.103) | copy-start | bytes 589828
  1427.5 79.7 %copy-start.6 = (f32[128,384]{1,0:T(8,128)S(1)}, f32[128,384]{1,0:T(8,128)}, u32[]{:S(2)}) copy-start(f32[128,384]{1,0:T(8,128)} %get-tuple-element.104) | copy-start | bytes 589828
  1427.5 82.0 %copy-start.10 = (f32[128,128]{1,0:T(8,128)S(1)}, f32[128,128]{1,0:T(8,128)}, u32[]{:S(2)}) copy-start(f32[128,128]{1,0:T(8,128)} %get-tuple-element.106) | copy-start | bytes 196612
  1506.6 14.8 collective-permute-start.11
  1567.5 111.5 %copy-start.12 = (f32[2,128]{1,0:T(2,128)S(1)}, f32[2,128]{1,0:T(2,128)}, u32[]{:S(2)}) copy-start(f32[2,128]{1,0:T(2,128)} %get-tuple-element.96) | copy-start | bytes 3076
  1567.5 112.2 %copy-start.11 = (f32[128,128]{1,0:T(8,128)S(1)}, f32[128,128]{1,0:T(8,128)}, u32[]{:S(2)}) copy-start(f32[128,128]{1,0:T(8,128)} %get-tuple-element.100) | copy-start | bytes 196612
  1567.6 113.1 %copy-start.5 = (f32[512,128]{1,0:T(8,128)S(1)}, f32[512,128]{1,0:T(8,128)}, u32[]{:S(2)}) copy-start(f32[512,128]{1,0:T(8,128)} %get-tuple-element.98) | copy-start | bytes 786436

commit v2 on v0

v2 whole, which is shorter than its diff:
```python
import functools
import jax
import jax.numpy as jnp
from jax import lax
from jax.experimental import pallas as pl
from jax.experimental.pallas import tpu as pltpu
from jax.sharding import PartitionSpec as P

LN_EPS = 1e-5
AX = 'dap'
N = 384
C = 128
H = 64
TI = 16
RB = 96
CB = 8
NCH = 2
HC = H // NCH
UNROLL = 4
F32 = jnp.float32
BF16 = jnp.bfloat16
ICI_SWAP = [(0, 2), (2, 0), (1, 3), (3, 1)]
D2D_SWAP = [(0, 1), (1, 0), (2, 3), (3, 2)]
OWN, CROSS, PART, DIAG = 0, 2, 1, 3


def sig(v):
    return 0.5 * jnp.tanh(0.5 * v) + 0.5


def dot(a, b, ca=1, cb=0):
    return lax.dot_general(a, b, (((ca,), (cb,)), ((), ())), preferred_element_type=F32)


def hat(v):
    mean = jnp.sum(v, axis=0, keepdims=True) * (1.0 / C)
    cen = v - mean
    var = jnp.sum(cen * cen, axis=0, keepdims=True) * (1.0 / C)
    rstd = lax.rsqrt(var + LN_EPS)
    return cen * rstd, rstd


def affine(h, ln_ref):
    return (h * ln_ref[:, 0:1] + ln_ref[:, 1:2]).astype(BF16)


def rows_loop(fn, unroll=UNROLL):
    def step(i, carry):
        fn(i)
        return carry
    lax.fori_loop(0, TI, step, 0, unroll=unroll)


def fill(scr, refs):
    at = 0
    for ref in refs:
        for c in range(0, ref.shape[0], 16):
            scr[:, at + c:at + c + 16, :] = jnp.swapaxes(ref[c:c + 16], 0, 1)
        at += ref.shape[0]


def flush(scr, refs):
    at = 0
    for ref in refs:
        for c in range(0, ref.shape[0], 16):
            ref[c:c + 16] = jnp.swapaxes(scr[:, at + c:at + c + 16, :], 0, 1)
        at += ref.shape[0]


def scr(n):
    return pltpu.VMEM((TI, n, N), BF16)


def const_spec(shape):
    nd = len(shape)
    return pl.BlockSpec(shape, lambda *_: (0,) * nd)


def act_spec():
    return pl.BlockSpec((TI, N, C), lambda i, *_: (i, 0, 0))


def actt_spec():
    return pl.BlockSpec((TI, C, N), lambda i, *_: (i, 0, 0))


def mask_spec_():
    return pl.BlockSpec((TI, N), lambda i, *_: (i, 0))


def piece_spec(k, n):
    return pl.BlockSpec((None, n, TI, N), lambda i: (k, 0, i, 0))


def half_spec():
    return pl.BlockSpec((H, TI, N), lambda i: (0, i, 0))


ACT = jax.ShapeDtypeStruct((RB, N, C), BF16)
ACTT = jax.ShapeDtypeStruct((RB, C, N), BF16)
HALF = jax.ShapeDtypeStruct((H, RB, N), BF16)
NPOS = RB * N


def cost(flops, nbytes, trans=0):
    return pl.CostEstimate(flops=int(flops), bytes_accessed=int(nbytes), transcendentals=int(trans))


def turn_body(z_ref, zt_ref):
    def row(i):
        zt_ref[i] = z_ref[i].T
    rows_loop(row)


def turn(z):
    return pl.pallas_call(turn_body, grid=(RB // TI,), in_specs=[act_spec()], out_specs=actt_spec(), out_shape=ACTT,
                          cost_estimate=cost(NPOS * C * 40, NPOS * C * 4), name="turn")(z)


def norm_body(z_ref, ln_ref, zt_ref, xt_ref):
    def row(i):
        zt = z_ref[i].T
        zt_ref[i] = zt
        h, _ = hat(zt.astype(F32))
        xt_ref[i] = affine(h, ln_ref)
    rows_loop(row)


def norm(z, ln):
    return pl.pallas_call(norm_body, grid=(RB // TI,), in_specs=[act_spec(), const_spec((C, 2))], out_specs=[actt_spec()] * 2,
                          out_shape=[ACTT] * 2, cost_estimate=cost(NPOS * C * 60, NPOS * C * 6), name="norm")(z, ln)


def prep_body(base, x_ref, m_ref, wt_ref, *rest):
    a_out, b_out, sa, sb = rest[-4:]

    def row(i):
        mrow = m_ref[pl.ds(i, 1), :]
        p = dot(wt_ref[...], x_ref[i])
        sa[i] = (mrow * sig(p[H:2 * H]) * p[0:H]).astype(BF16)
        sb[i] = (mrow * sig(p[3 * H:4 * H]) * p[2 * H:3 * H]).astype(BF16)

    rows_loop(row)
    flush(sa, [a_out])
    flush(sb, [b_out])


def prep(base, xt, mask, wt, full=None):
    out = jax.ShapeDtypeStruct((H, N, N), BF16)
    spec = pl.BlockSpec((H, TI, N), lambda i, b: (0, b[0] + i, 0))
    extra = () if full is None else tuple(full)
    grid_spec = pltpu.PrefetchScalarGridSpec(
        num_scalar_prefetch=1, grid=(RB // TI,),
        in_specs=[actt_spec(), mask_spec_(), const_spec((4 * H, C))] + [pl.BlockSpec(memory_space=pl.ANY)] * len(extra),
        out_specs=[spec, spec], scratch_shapes=[scr(H), scr(H)])
    return pl.pallas_call(
        prep_body, grid_spec=grid_spec, out_shape=[out, out],
        input_output_aliases={4: 0, 5: 1} if extra else {},
        cost_estimate=cost(NPOS * C * 400, NPOS * C * 4, NPOS * C), name="prep",
    )(base, xt, mask, wt, *extra)


def block_rows(idx, ref, c):
    return [ref[c, pl.ds(pl.multiple_of(idx[k] * RB, RB), RB), :] for k in range(4)]


def emit(vals, keep, send, c):
    keep[0, c] = vals[:RB]
    keep[1, c] = vals[RB:2 * RB]
    send[0, c] = vals[2 * RB:3 * RB]
    send[1, c] = vals[3 * RB:]


def tri_out_body(idx, a, b, keep, send):
    for c in range(CB):
        lhs = jnp.concatenate(block_rows(idx, a, c), axis=0)
        emit(dot(lhs, b[c], 1, 1).astype(BF16), keep, send, c)


def tri_in_body(idx, a, b, keep, send, s):
    for c in range(CB):
        s[c] = a[c].T
        lhs = jnp.concatenate(block_rows(idx, s, c), axis=0)
        emit(dot(lhs, b[c]).astype(BF16), keep, send, c)


def gather_dt(idx, parts, c, s):
    for k, part in enumerate(parts):
        s[c, pl.ds(pl.multiple_of(idx[k] * RB, RB), RB), :] = part[c]


def tri_in_bwd_body(idx, d0, d1, d2, d3, a, b, dak, das, dbk, dbs, s):
    for c in range(CB):
        gather_dt(idx, (d0, d1, d2, d3), c, s)
        emit(dot(jnp.concatenate(block_rows(idx, b, c), axis=0), s[c], 1, 1).astype(BF16), dak, das, c)
        emit(dot(jnp.concatenate(block_rows(idx, a, c), axis=0), s[c]).astype(BF16), dbk, dbs, c)


def tri_out_bwd_body(idx, d0, d1, d2, d3, a, b, dak, das, dbk, dbs, s, st):
    for c in range(CB):
        gather_dt(idx, (d0, d1, d2, d3), c, s)
        da = dot(jnp.concatenate([d0[c], d2[c]], axis=0), b[c]).astype(BF16)
        st[c] = s[c].T
        rows = block_rows(idx, st, c)
        db = dot(jnp.concatenate([rows[0], rows[2]], axis=0), a[c]).astype(BF16)
        dak[0, c] = da[:RB]
        das[0, c] = da[RB:]
        dbk[0, c] = db[:RB]
        dbs[0, c] = db[RB:]


def tri_call(body, idx, part, dts, ab, pieces, n_out, n_scr, flops, name):
    off = part * (HC // CB)
    dspec = pl.BlockSpec((CB, RB, N), lambda c, _: (c + off, 0, 0))
    fspec = pl.BlockSpec((CB, N, N), lambda c, _: (c + off, 0, 0))
    ospec = pl.BlockSpec((pieces, CB, RB, N), lambda c, _: (0, c, 0, 0))
    grid_spec = pltpu.PrefetchScalarGridSpec(
        num_scalar_prefetch=1, grid=(HC // CB,), in_specs=[dspec] * len(dts) + [fspec] * len(ab),
        out_specs=[ospec] * n_out, scratch_shapes=[pltpu.VMEM((CB, N, N), BF16)] * n_scr)
    return pl.pallas_call(body, grid_spec=grid_spec, out_shape=[jax.ShapeDtypeStruct((pieces, HC, RB, N), BF16)] * n_out,
                          cost_estimate=cost(flops, 50e6), name=name)(idx, *dts, *ab)


def finish_body(*refs):
    ts = refs[:2 * NCH]
    z_ref, x_ref, wg_ref, lnq_ref, wo_ref, ln_ref, z_out, x_out, st = refs[2 * NCH:]
    fill(st, ts)

    def row(i):
        th, _ = hat(st[i].astype(F32))
        upd = dot(wo_ref[...], affine(th, lnq_ref))
        gate = sig(dot(wg_ref[...], x_ref[i]))
        zn = (z_ref[i].astype(F32) + gate * upd).astype(BF16)
        z_out[i] = zn
        h, _ = hat(zn.astype(F32))
        x_out[i] = affine(h, ln_ref)

    rows_loop(row)


def finish(k, ts, zt, xt, wgt, lnq, wot, ln_next):
    return pl.pallas_call(
        finish_body, grid=(RB // TI,),
        in_specs=[piece_spec(k, HC)] * (2 * NCH) + [actt_spec(), actt_spec(), const_spec((C, C)), const_spec((C, 2)), const_spec((C, C)), const_spec((C, 2))],
        out_specs=[actt_spec()] * 2, out_shape=[ACTT] * 2, scratch_shapes=[scr(C)],
        cost_estimate=cost(NPOS * C * 600, NPOS * C * 10, NPOS * C), name="finish",
    )(*ts, zt, xt, wgt, lnq, wot, ln_next)


def head_body(emit_z, emit_w, *refs):
    ts = refs[:2 * NCH]
    refs = list(refs[2 * NCH:])
    x_ref, g_ref, wg_ref, lnq_ref, wot_ref, wo_ref = refs[:6]
    k = 6
    if emit_z:
        z_ref = refs[k]
        k += 1
    dt_keep, dt_send, dg_out = refs[k:k + 3]
    k += 3
    if emit_z:
        z_out = refs[k]
        k += 1
    if emit_w:
        gwo, ggain, gshift = refs[k:k + 3]

        @pl.when(pl.program_id(0) == 0)
        def _():
            gwo[...] = jnp.zeros_like(gwo)
            ggain[...] = jnp.zeros_like(ggain)
            gshift[...] = jnp.zeros_like(gshift)

    st, sd = refs[-2:]
    fill(st, ts)

    def row(i):
        th, rstd = hat(st[i].astype(F32))
        y = affine(th, lnq_ref)
        upd = dot(wot_ref[...], y)
        gate = sig(dot(wg_ref[...], x_ref[i]))
        if emit_z:
            z_out[i] = (z_ref[i].astype(F32) + gate * upd).astype(BF16).T
        dgate = g_ref[i].astype(F32) * gate
        dg_out[i] = (dgate * upd * (1.0 - gate)).astype(BF16)
        du = dgate.astype(BF16)
        dy = dot(wo_ref[...], du).astype(BF16).astype(F32)
        dh = dy * lnq_ref[:, 0:1]
        m1 = jnp.sum(dh, axis=0, keepdims=True) * (1.0 / C)
        m2 = jnp.sum(dh * th, axis=0, keepdims=True) * (1.0 / C)
        sd[i] = (rstd * (dh - m1 - th * m2)).astype(BF16)
        if emit_w:
            gwo[...] += dot(y, du, 1, 1)
            e = dy * th
            ggain[...] += e[:, 0:128] + e[:, 128:256] + e[:, 256:384]
            gshift[...] += dy[:, 0:128] + dy[:, 128:256] + dy[:, 256:384]

    rows_loop(row)
    flush(sd, [dt_keep, dt_send])


def head(k, ts, xt, gt, wgt, lnq, wot, wo, zt=None, emit_w=False):
    emit_z = zt is not None
    in_specs = [piece_spec(k, HC)] * (2 * NCH) + [actt_spec(), actt_spec(), const_spec((C, C)), const_spec((C, 2)), const_spec((C, C)), const_spec((C, C))]
    out_shape = [HALF, HALF, ACTT]
    out_specs = [half_spec(), half_spec(), actt_spec()]
    extra = ()
    if emit_z:
        in_specs.append(actt_spec())
        extra = (zt,)
        out_shape.append(ACT)
        out_specs.append(act_spec())
    if emit_w:
        for s in ((C, C), (C, C), (C, C)):
            out_shape.append(jax.ShapeDtypeStruct(s, F32))
            out_specs.append(const_spec(s))
    return pl.pallas_call(
        functools.partial(head_body, emit_z, emit_w), grid=(RB // TI,), in_specs=in_specs,
        out_specs=out_specs, out_shape=out_shape, scratch_shapes=[scr(C), scr(C)],
        cost_estimate=cost(NPOS * C * 800, NPOS * C * 10, NPOS * C), name="head",
    )(*ts, xt, gt, wgt, lnq, wot, wo, *extra)


def back_body(n_ab, emit_w, last, *refs):
    das, dbs = refs[:n_ab], refs[n_ab:2 * n_ab]
    refs = refs[2 * n_ab:]
    z_ref, g_ref, dg_ref, m_ref, ln_ref, wt_ref, wb_ref, d_out = refs[:8]
    if emit_w:
        gw, ggain, gshift = refs[8:11]

        @pl.when(pl.program_id(0) == 0)
        def _():
            gw[...] = jnp.zeros_like(gw)
            ggain[...] = jnp.zeros_like(ggain)
            gshift[...] = jnp.zeros_like(gshift)

    sa, sb = refs[-2:]
    fill(sa, das)
    fill(sb, dbs)

    def row(i):
        xh, rstd = hat(z_ref[i].astype(F32))
        x = affine(xh, ln_ref)
        mrow = m_ref[pl.ds(i, 1), :]
        ds = []
        for s, at in ((sa, 0), (sb, 2 * C)):
            p = dot(wt_ref[at:at + 2 * C], x)
            sg = sig(p[C:])
            t0 = s[i].astype(F32) * mrow * sg
            ds.append(t0.astype(BF16))
            ds.append((t0 * p[:C] * (1.0 - sg)).astype(BF16))
        dp = jnp.concatenate(ds + [dg_ref[i]], axis=0)
        dx = dot(wb_ref[...], dp).astype(BF16).astype(F32)
        dh = dx * ln_ref[:, 0:1]
        m1 = jnp.sum(dh, axis=0, keepdims=True) * (1.0 / C)
        m2 = jnp.sum(dh * xh, axis=0, keepdims=True) * (1.0 / C)
        d = (g_ref[i].astype(F32) + rstd * (dh - m1 - xh * m2)).astype(BF16)
        d_out[i] = d.T if last else d
        if emit_w:
            gw[...] += dot(dp, x, 1, 1)
            e = dx * xh
            ggain[...] += e[:, 0:128] + e[:, 128:256] + e[:, 256:384]
            gshift[...] += dx[:, 0:128] + dx[:, 128:256] + dx[:, 256:384]

    rows_loop(row)


def back(k, das, dbs, zt, gt, dgt, mask, ln, wt, wb, emit_w, last):
    n = len(das)
    out_shape = [ACT if last else ACTT]
    out_specs = [act_spec() if last else actt_spec()]
    if emit_w:
        for s in ((5 * C, C), (C, C), (C, C)):
            out_shape.append(jax.ShapeDtypeStruct(s, F32))
            out_specs.append(const_spec(s))
    return pl.pallas_call(
        functools.partial(back_body, n, emit_w, last), grid=(RB // TI,),
        in_specs=[piece_spec(k, HC)] * (2 * n) + [actt_spec()] * 3 + [mask_spec_(), const_spec((C, 2)), const_spec((4 * C, C)), const_spec((C, 5 * C))],
        out_specs=out_specs, out_shape=out_shape, scratch_shapes=[scr(C), scr(C)],
        cost_estimate=cost(NPOS * C * 2000, NPOS * C * 12, NPOS * C * 2), name="back",
    )(*das, *dbs, zt, gt, dgt, mask, ln, wt, wb)


def solution(mesh):
    row_spec = P(('data', 'dap'), None, None)
    mask_spec = P(('data', 'dap'), None)
    full_spec = P()
    grad_spec = P('data', None, None)

    def ici(v):
        return lax.ppermute(v, AX, ICI_SWAP)

    def d2d(v):
        return lax.ppermute(v, AX, D2D_SWAP)

    def device_step(pair_act, pair_mask, d_pair_out, ln_pair, w_proj, w_gate, ln_chan, w_out):
        me = lax.axis_index(AX)
        odd = (me & 1) == 1
        blocks = jnp.stack([me ^ OWN, me ^ CROSS, me ^ PART, me ^ DIAG]).astype(jnp.int32)
        base = [blocks[k:k + 1] * (RB // TI) for k in range(4)]

        def local(v, axis):
            return jnp.where(odd, jnp.roll(v, H, axis=axis), v)

        m_own = pair_mask.astype(F32)
        m_cross = ici(m_own)
        m_part = d2d(m_own)
        m_diag = d2d(m_cross)
        z_cross = ici(pair_act)

        ln = [ln_pair[u].T.astype(F32) for u in range(2)]
        lnq = [local(ln_chan[u].T.astype(F32), 0) for u in range(2)]
        wp4 = [local(w_proj[u].reshape(C, 4, C), 2) for u in range(2)]
        wt_half = [wp4[u][:, :, :H].reshape(C, 4 * H).T for u in range(2)]
        wt = [wp4[u].reshape(C, 4 * C).T for u in range(2)]
        wb = [jnp.concatenate([wp4[u].reshape(C, 4 * C), w_gate[u]], axis=1) for u in range(2)]
        wgt = [w_gate[u].T for u in range(2)]
        wo = [local(w_out[u], 0) for u in range(2)]
        wot = [wo[u].T for u in range(2)]

        def products(body, name, dts, a, b, pieces, n_scr, flops):
            n_out = 4 if dts else 2
            res = [tri_call(body, blocks, part, dts, (a, b), pieces, n_out, n_scr, flops / NCH, name) for part in range(NCH)]
            keeps = [[r[j] for r in res] for j in range(0, n_out, 2)]
            sends = [[d2d(r[j]) for r in res] for j in range(1, n_out, 2)]
            return [k + s for k, s in zip(keeps, sends)]

        zt_own, xt_own = norm(pair_act, ln[0])
        xt_part = d2d(xt_own)
        gt_own = turn(d_pair_out)
        ab1 = prep(base[0], xt_own, m_own, wt_half[0])
        ab1 = prep(base[2], xt_part, m_part, wt_half[0], ab1)
        gt_src, z_cross, a1, b1 = lax.optimization_barrier((gt_own, z_cross, ab1[0], ab1[1]))
        gt_cross = ici(gt_src)
        zt_cross, xt_cross = norm(z_cross, ln[0])
        xt_diag = d2d(xt_cross)
        ab1 = prep(base[1], xt_cross, m_cross, wt_half[0], (a1, b1))
        a1, b1 = prep(base[3], xt_diag, m_diag, wt_half[0], ab1)
        t1, = products(tri_out_body, "tri_out", (), a1, b1, 2, 0, 7.2e9)
        yt_own, vt_own = finish(0, t1, zt_own, xt_own, wgt[0], lnq[0], wot[0], ln[1])
        vt_part = d2d(vt_own)
        yt_cross, vt_cross = finish(1, t1, zt_cross, xt_cross, wgt[0], lnq[0], wot[0], ln[1])
        vt_diag = d2d(vt_cross)

        ab2 = prep(base[0], vt_own, m_own, wt_half[1])
        ab2 = prep(base[2], vt_part, m_part, wt_half[1], ab2)
        ab2 = prep(base[1], vt_cross, m_cross, wt_half[1], ab2)
        a2, b2 = prep(base[3], vt_diag, m_diag, wt_half[1], ab2)
        t2, = products(tri_in_body, "tri_in", (), a2, b2, 2, 1, 7.2e9)

        dk_own, ds_own, dg2_own, pair_out, gwo2, gq2g, gq2s = head(0, t2, vt_own, gt_own, wgt[1], lnq[1], wot[1], wo[1], yt_own, True)
        dk_part = d2d(ds_own)
        dk_cross, ds_cross, dg2_cross = head(1, t2, vt_cross, gt_cross, wgt[1], lnq[1], wot[1], wo[1])
        dk_diag = d2d(ds_cross)
        da2, db2 = products(tri_in_bwd_body, "tri_in_bwd", (dk_own, dk_cross, dk_part, dk_diag), a2, b2, 2, 1, 14.4e9)
        et_own, gw2, gp2g, gp2s = back(0, da2, db2, yt_own, gt_own, dg2_own, m_own, ln[1], wt[1], wb[1], True, False)
        et_cross, = back(1, da2, db2, yt_cross, gt_cross, dg2_cross, m_cross, ln[1], wt[1], wb[1], False, False)

        dk_own, ds_own, dg1_own, gwo1, gq1g, gq1s = head(0, t1, xt_own, et_own, wgt[0], lnq[0], wot[0], wo[0], None, True)
        dk_part = d2d(ds_own)
        dk_cross, ds_cross, _ = head(1, t1, xt_cross, et_cross, wgt[0], lnq[0], wot[0], wo[0])
        dk_diag = d2d(ds_cross)
        da1, db1 = products(tri_out_bwd_body, "tri_out_bwd", (dk_own, dk_cross, dk_part, dk_diag), a1, b1, 1, 2, 7.2e9)
        d_pair, gw1, gp1g, gp1s = back(0, da1, db1, zt_own, et_own, dg1_own, m_own, ln[0], wt[0], wb[0], True, True)

        def vec(gg, gs):
            return jnp.stack([jnp.sum(gg, axis=1), jnp.sum(gs, axis=1)])

        def proj(g):
            return local(g[:4 * C].T.reshape(C, 4, C), 2).reshape(C, 4 * C)

        grads = (jnp.stack([vec(gp1g, gp1s), vec(gp2g, gp2s)]),
                 jnp.stack([proj(gw1), proj(gw2)]),
                 jnp.stack([gw1[4 * C:].T, gw2[4 * C:].T]),
                 jnp.stack([local(vec(gq1g, gq1s), 1), local(vec(gq2g, gq2s), 1)]),
                 jnp.stack([local(gwo1, 0), local(gwo2, 0)]))
        sums = lax.psum(grads, AX)
        return (pair_out, d_pair) + tuple(v.astype(BF16) for v in sums)

    return jax.shard_map(device_step, mesh=mesh, in_specs=(row_spec, mask_spec, row_spec, full_spec, full_spec, full_spec, full_spec, full_spec), out_specs=(row_spec, row_spec, grad_spec, grad_spec, grad_spec, grad_spec, grad_spec), check_vma=False)
```

time: 2680 us -> 1040 us (0.39)
  Pallas kernels: 0 us -> 702 us
  blocking collectives: 679 us -> 21.1 us
  local copies, waits for them, and re-layouts: 597 us -> 15.3 us
  other arithmetic: 521 us -> 8.64 us
  matrix products: 452 us -> 0 us
  waiting for transfers between devices: 381 us -> 272 us
    pallas_call x0 -> x28, Pallas kernels: none -> 702 us  [the longest x3 184 us: back(): pl.pallas_call(functools.partial(back_body, n, emit_w, last), grid=(RB //...]
    all_to_all x4 -> x0, blocking collectives: 660 us -> none  [to_channels(): lax.all_to_all(row_blocks, GROUP_AXIS, chan_dim, chan_dim + 1, tiled=True)]
    dot_general x24 -> x0, matrix products: 452 us -> none  [the longest x2 60.2 us: update_forward(): jnp.einsum('ijd,de->eij', x_norm, w_proj, preferred_element_type=jnp.floa...]
    all_to_all x4 -> x0, waiting for transfers between devices: 381 us -> none  [to_rows(): lax.all_to_all(chan_blocks, GROUP_AXIS, chan_dim + 1, chan_dim, tiled=True)]
    ppermute x0 -> x25, waiting for transfers between devices: none -> 272 us  [the longest x3 226 us: ici(): return lax.ppermute(v, AX, ICI_SWAP)]
    convert_element_type x18 -> x0, local copies, waits for them, and re-layouts: 256 us -> none  [the longest x4 62.6 us: update_forward(): t_rows.astype(jnp.float32)]
    another operation x17 -> x11, other arithmetic: 189 us -> 0.77 us  [the longest x1 0.65 us: device_step(): jnp.stack([me ^ OWN, me ^ CROSS, me ^ PART, me ^ DIAG]).astype(jnp.int32)]
    convert_element_type x14 -> x5, other arithmetic: 182 us -> 1.28 us  [the longest x2 1.26 us: device_step(): ln = [ln_pair[u].T.astype(F32) for u in range(2)]]
  transfers between devices with their start and end apart: 4 -> 25, of which waited for: 4 -> 12; matrix products, arithmetic and copies ran while one was open for 9% -> 1% of each run, Pallas kernels for 0% -> 38%
where the time goes in v2:
time: 1040 us; the launch traced here: 1030 us
  Pallas kernels  702 us (68%)
  waiting for transfers between devices  272 us (26%)
  blocking collectives  21.1 us (2%)
  local copies, waits for them, and re-layouts  15.3 us (1%)
  starting transfers between devices  11.6 us (1%)
    ppermute x3, waiting for transfers between devices, ici(): return lax.ppermute(v, AX, ICI_SWAP)  226 us
    pallas_call x3, Pallas kernels, back(): pl.pallas_call(functools.partial(back_body, n, emit_w, last), grid=(RB //...  184 us
    pallas_call x4, Pallas kernels, head(): pl.pallas_call(functools.partial(head_body, emit_z, emit_w), grid=(RB //...  176 us
    pallas_call x8, Pallas kernels, tri_call(): pl.pallas_call(body, grid_spec=grid_spec, out_shape=[jax.ShapeDtypeStruct...  132 us
    pallas_call x8, Pallas kernels, prep(): pl.pallas_call(prep_body, grid_spec=grid_spec, out_shape=[out, out], inpu...  115 us
    pallas_call x2, Pallas kernels, finish(): pl.pallas_call(finish_body, grid=(RB // TI,), in_specs=[piece_spec(k, HC)...  55.5 us
    ppermute x22, waiting for transfers between devices, d2d(): return lax.ppermute(v, AX, D2D_SWAP)  46.7 us
    pallas_call x2, Pallas kernels, norm(): pl.pallas_call(norm_body, grid=(RB // TI,), in_specs=[act_spec(), const_s...  29 us
  transfers between devices with their start and end apart: 25, of which 12 were waited for; matrix products, arithmetic and copies ran while one was open for 1% of the time, Pallas kernels for 38%

profile of v2, /device:TPU:0, one launch (start us, length us, event | category | flops | bytes accessed | tf_op | source)
XLA Modules:
  0.0 1032.8 jit_solution(9617755488898466061)
XLA Ops:
  2.1 14.5 %norm.2 = (bf16[96,128,384]{2,1,0:T(8,128)(2,1)}, bf16[96,128,384]{2,1,0:T(8,128)(2,1)}) custom-call(bf16[96,384,128]{2,1,0:T(8,128)(2,1)} %z_ref.3, f32[128,2]{1,0:T(8,128)} %convert_bitcast_fusion.ln_ref.refs_12_), custom_call_target="tpu_custom_call" | custom-call | flops 283115520 | bytes 28311552 | tf_op jit(solution)/shard_map/norm/pallas_call | solution.py:130
  22.1 10.2 turn.1.refs_5_.refs_9_
  32.3 14.3 %prep.8 = (bf16[64,384,384]{2,1,0:T(8,128)(2,1)}, bf16[64,384,384]{2,1,0:T(8,128)(2,1)}) custom-call(s32[1]{0:T(128)S(6)} %mul.14.base, bf16[96,128,384]{2,1,0:T(8,128)(2,1)} %get-tuple-element.85.x_ref.refs_5_.refs_4_, f32[96,384]{1,0:T(8,128)} %copy-done, bf16[256,128]{1,0:T(8,128)(2,1)} %bitcast.132), custom_call_target="tpu_custom_call" | custom-call | flops 1887436800 | bytes 18874368 | tf_op jit(solution)/shard_map/prep/pallas_call | solution.py:156
  47.3 14.3 %prep.9 = (bf16[64,384,384]{2,1,0:T(8,128)(2,1)}, bf16[64,384,384]{2,1,0:T(8,128)(2,1)}) custom-call(s32[1]{0:T(128)S(6)} %mul.13.base, bf16[96,128,384]{2,1,0:T(8,128)(2,1)} %collective-permute-done.1.x_ref, f32[96,384]{1,0:T(8,128)} %copy-done.10, bf16[256,128]{1,0:T(8,128)(2,1)} %bitcast.133, ...), custom_call_target="tpu_custom_call", output_to_operand_aliasing={{0}: (4, {}), {1}: (5, {})} | custom-call | flops 1887436800 | bytes 18874368 | tf_op jit(solution)/shard_map/prep/pallas_call | solution.py:156
  61.7 161.9 %collective-permute-done.z_ref = bf16[96,384,128]{2,1,0:T(8,128)(2,1)} collective-permute-done((bf16[96,384,128]{2,1,0:T(8,128)(2,1)}, bf16[96,384,128]{2,1,0:T(8,128)(2,1)}, u32[]{:S(2)}, u32[]{:S(2)}) %collective-permute-start) | collective-permute-done | bytes 9437216 | tf_op jit(solution)/shard_map/ppermute | solution.py:389
  223.6 14.5 %norm.3 = (bf16[96,128,384]{2,1,0:T(8,128)(2,1)}, bf16[96,128,384]{2,1,0:T(8,128)(2,1)}) custom-call(bf16[96,384,128]{2,1,0:T(8,128)(2,1)} %collective-permute-done.z_ref, f32[128,2]{1,0:T(8,128)} %convert_bitcast_fusion.ln_ref.refs_12_), custom_call_target="tpu_custom_call" | custom-call | flops 283115520 | bytes 28311552 | tf_op jit(solution)/shard_map/norm/pallas_call | solution.py:130
  245.0 14.4 %prep.10 = (bf16[64,384,384]{2,1,0:T(8,128)(2,1)}, bf16[64,384,384]{2,1,0:T(8,128)(2,1)}) custom-call(s32[1]{0:T(128)S(6)} %mul.15.base, bf16[96,128,384]{2,1,0:T(8,128)(2,1)} %get-tuple-element.91.x_ref.refs_5_.refs_4_, f32[96,384]{1,0:T(8,128)} %copy-done.3, bf16[256,128]{1,0:T(8,128)(2,1)} %bitcast.134, ...), custom_call_target="tpu_custom_call", output_to_operand_aliasing={{0}: (4, {}), {1}: (5, {})} | custom-call | flops 1887436800 | bytes 18874368 | tf_op jit(solution)/shard_map/prep/pallas_call | solution.py:156
  260.0 14.3 %prep.11 = (bf16[64,384,384]{2,1,0:T(8,128)(2,1)}, bf16[64,384,384]{2,1,0:T(8,128)(2,1)}) custom-call(s32[1]{0:T(128)S(6)} %mul.12.base, bf16[96,128,384]{2,1,0:T(8,128)(2,1)} %collective-permute-done.3.x_ref, f32[96,384]{1,0:T(8,128)} %copy-done.11, bf16[256,128]{1,0:T(8,128)(2,1)} %bitcast.135, ...), custom_call_target="tpu_custom_call", output_to_operand_aliasing={{0}: (4, {}), {1}: (5, {})} | custom-call | flops 1887436800 | bytes 18874368 | tf_op jit(solution)/shard_map/prep/pallas_call | solution.py:156
  274.3 13.7 %tri_out.3 = (bf16[2,32,96,384]{3,2,1,0:T(8,128)(2,1)}, bf16[2,32,96,384]{3,2,1,0:T(8,128)(2,1)}) custom-call(s32[4]{0:T(128)} %pad_add_fusion.idx, bf16[64,384,384]{2,1,0:T(8,128)(2,1)} %get-tuple-element.96.a, bf16[64,384,384]{2,1,0:T(8,128)(2,1)} %get-tuple-element.97.b), custom_call_target="tpu_custom_call" | custom-call | flops 3600000000 | bytes 50000000 | tf_op jit(solution)/shard_map/tri_out/pallas_call | solution.py:220
  288.1 13.8 %tri_out.2 = (bf16[2,32,96,384]{3,2,1,0:T(8,128)(2,1)}, bf16[2,32,96,384]{3,2,1,0:T(8,128)(2,1)}) custom-call(s32[4]{0:T(128)} %pad_add_fusion.idx, bf16[64,384,384]{2,1,0:T(8,128)(2,1)} %get-tuple-element.96.a, bf16[64,384,384]{2,1,0:T(8,128)(2,1)} %get-tuple-element.97.b), custom_call_target="tpu_custom_call" | custom-call | flops 3600000000 | bytes 50000000 | tf_op jit(solution)/shard_map/tri_out/pallas_call | solution.py:220
  316.5 27.7 %finish.3 = (bf16[96,128,384]{2,1,0:T(8,128)(2,1)}, bf16[96,128,384]{2,1,0:T(8,128)(2,1)}) custom-call(bf16[2,32,96,384]{3,2,1,0:T(8,128)(2,1)} %get-tuple-element.98.refs_0_, bf16[2,32,96,384]{3,2,1,0:T(8,128)(2,1)} %get-tuple-element.99.refs_1_, bf16[2,32,96,384]{3,2,1,0:T(8,128)(2,1)} %collective-permute-done.6.refs_2_, ...), custom_call_target="tpu_custom_call" | custom-call | flops 2831155200 | bytes 47185920 | tf_op jit(solution)/shard_map/finish/pallas_call | solution.py:242
  344.4 27.8 %finish.2 = (bf16[96,128,384]{2,1,0:T(8,128)(2,1)}, bf16[96,128,384]{2,1,0:T(8,128)(2,1)}) custom-call(bf16[2,32,96,384]{3,2,1,0:T(8,128)(2,1)} %get-tuple-element.98.refs_0_, bf16[2,32,96,384]{3,2,1,0:T(8,128)(2,1)} %get-tuple-element.99.refs_1_, bf16[2,32,96,384]{3,2,1,0:T(8,128)(2,1)} %collective-permute-done.6.refs_2_, ...), custom_call_target="tpu_custom_call" | custom-call | flops 2831155200 | bytes 47185920 | tf_op jit(solution)/shard_map/finish/pallas_call | solution.py:242
  375.4 14.8 %prep.12 = (bf16[64,384,384]{2,1,0:T(8,128)(2,1)}, bf16[64,384,384]{2,1,0:T(8,128)(2,1)}) custom-call(s32[1]{0:T(128)S(6)} %mul.14.base, bf16[96,128,384]{2,1,0:T(8,128)(2,1)} %get-tuple-element.105.x_ref.refs_4_, f32[96,384]{1,0:T(8,128)} %copy-done, bf16[256,128]{1,0:T(8,128)(2,1)} %bitcast.136), custom_call_target="tpu_custom_call" | custom-call | flops 1887436800 | bytes 18874368 | tf_op jit(solution)/shard_map/prep/pallas_call | solution.py:156
  390.2 14.4 %prep.13 = (bf16[64,384,384]{2,1,0:T(8,128)(2,1)}, bf16[64,384,384]{2,1,0:T(8,128)(2,1)}) custom-call(s32[1]{0:T(128)S(6)} %mul.13.base, bf16[96,128,384]{2,1,0:T(8,128)(2,1)} %collective-permute-done.9.x_ref, f32[96,384]{1,0:T(8,128)} %copy-done.10, bf16[256,128]{1,0:T(8,128)(2,1)} %bitcast.137, ...), custom_call_target="tpu_custom_call", output_to_operand_aliasing={{0}: (4, {}), {1}: (5, {})} | custom-call | flops 1887436800 | bytes 18874368 | tf_op jit(solution)/shard_map/prep/pallas_call | solution.py:156
  404.6 14.3 %prep.14 = (bf16[64,384,384]{2,1,0:T(8,128)(2,1)}, bf16[64,384,384]{2,1,0:T(8,128)(2,1)}) custom-call(s32[1]{0:T(128)S(6)} %mul.15.base, bf16[96,128,384]{2,1,0:T(8,128)(2,1)} %get-tuple-element.103.x_ref.refs_4_, f32[96,384]{1,0:T(8,128)} %copy-done.3, bf16[256,128]{1,0:T(8,128)(2,1)} %bitcast.138, ...), custom_call_target="tpu_custom_call", output_to_operand_aliasing={{0}: (4, {}), {1}: (5, {})} | custom-call | flops 1887436800 | bytes 18874368 | tf_op jit(solution)/shard_map/prep/pallas_call | solution.py:156
  419.0 14.3 %prep.15 = (bf16[64,384,384]{2,1,0:T(8,128)(2,1)}, bf16[64,384,384]{2,1,0:T(8,128)(2,1)}) custom-call(s32[1]{0:T(128)S(6)} %mul.12.base, bf16[96,128,384]{2,1,0:T(8,128)(2,1)} %collective-permute-done.8.x_ref, f32[96,384]{1,0:T(8,128)} %copy-done.11, bf16[256,128]{1,0:T(8,128)(2,1)} %bitcast.139, ...), custom_call_target="tpu_custom_call", output_to_operand_aliasing={{0}: (4, {}), {1}: (5, {})} | custom-call | flops 1887436800 | bytes 18874368 | tf_op jit(solution)/shard_map/prep/pallas_call | solution.py:156
  433.3 14.3 %tri_in.3 = (bf16[2,32,96,384]{3,2,1,0:T(8,128)(2,1)}, bf16[2,32,96,384]{3,2,1,0:T(8,128)(2,1)}) custom-call(s32[4]{0:T(128)} %pad_add_fusion.idx, bf16[64,384,384]{2,1,0:T(8,128)(2,1)} %get-tuple-element.112.a, bf16[64,384,384]{2,1,0:T(8,128)(2,1)} %get-tuple-element.113.b), custom_call_target="tpu_custom_call" | custom-call | flops 3600000000 | bytes 50000000 | tf_op jit(solution)/shard_map/tri_in/pallas_call | solution.py:220
  447.7 14.4 %tri_in.2 = (bf16[2,32,96,384]{3,2,1,0:T(8,128)(2,1)}, bf16[2,32,96,384]{3,2,1,0:T(8,128)(2,1)}) custom-call(s32[4]{0:T(128)} %pad_add_fusion.idx, bf16[64,384,384]{2,1,0:T(8,128)(2,1)} %get-tuple-element.112.a, bf16[64,384,384]{2,1,0:T(8,128)(2,1)} %get-tuple-element.113.b), custom_call_target="tpu_custom_call" | custom-call | flops 3600000000 | bytes 50000000 | tf_op jit(solution)/shard_map/tri_in/pallas_call | solution.py:220
  470.1 47.2 %head.4 = (bf16[64,96,384]{2,1,0:T(8,128)(2,1)}, bf16[64,96,384]{2,1,0:T(8,128)(2,1)}, bf16[96,128,384]{2,1,0:T(8,128)(2,1)}, bf16[96,384,128]{2,1,0:T(8,128)(2,...) custom-call(bf16[2,32,96,384]{3,2,1,0:T(8,128)(2,1)} %get-tuple-element.114.refs_0_, ...), custom_call_target="tpu_custom_call" | custom-call | flops 3774873600 | bytes 47185920 | tf_op jit(solution)/shard_map/head/pallas_call | solution.py:315
  517.6 60.0 %collective-permute-done.12.refs_5_.refs_9_ = bf16[96,128,384]{2,1,0:T(8,128)(2,1)} collective-permute-done((bf16[96,128,384]{2,1,0:T(8,128)(2,1)}, bf16[96,128,384]{2,1,0:T(8,128)(2,1)}, u32[]{:S(2)}, u32[]{:S(2)}) %collective-permute-start.12) | collective-permute-done | bytes 9437216 | tf_op jit(solution)/shard_map/ppermute | solution.py:389
  577.6 42.1 %head.5 = (bf16[64,96,384]{2,1,0:T(8,128)(2,1)}, bf16[64,96,384]{2,1,0:T(8,128)(2,1)}, bf16[96,128,384]{2,1,0:T(8,128)(2,1)}) custom-call(bf16[2,32,96,384]{3,2,1,0:T(8,128)(2,1)} %get-tuple-element.114.refs_0_, bf16[2,32,96,384]{3,2,1,0:T(8,128)(2,1)} %get-tuple-element.115.refs_1_, bf16[2,32,96,384]{3,2,1,0:T(8,128)(2,1)} %collective-permute-done.10.refs_2_, ...), custom_call_target="tpu_custom_call" | custom-call | flops 3774873600 | bytes 47185920 | tf_op jit(solution)/shard_map/head/pallas_call | solution.py:315
  619.7 7.8 collective-permute-done.14.d3
  627.5 22.0 %tri_in_bwd.3 = (bf16[2,32,96,384]{3,2,1,0:T(8,128)(2,1)}, bf16[2,32,96,384]{3,2,1,0:T(8,128)(2,1)}, bf16[2,32,96,384]{3,2,1,0:T(8,128)(2,1)}, bf16[2,32,96,384]{3,2,1,0:T(8,128)(2,1)}) custom-call(s32[4]{0:T(128)} %pad_add_fusion.idx, bf16[64,96,384]{2,1,0:T(8,128)(2,1)} %get-tuple-element.120.d0, bf16[64,96,384]{2,1,0:T(8,128)(2,1)} %get-tuple-element.122.d1, ...), custom_call_target="tpu_custom_call" | custom-call | flops 7200000000 | bytes 50000000 | tf_op jit(solution)/shard_map/tri_in_bwd/pallas_call | solution.py:220
  650.0 21.7 %tri_in_bwd.2 = (bf16[2,32,96,384]{3,2,1,0:T(8,128)(2,1)}, bf16[2,32,96,384]{3,2,1,0:T(8,128)(2,1)}, bf16[2,32,96,384]{3,2,1,0:T(8,128)(2,1)}, bf16[2,32,96,384]{3,2,1,0:T(8,128)(2,1)}) custom-call(s32[4]{0:T(128)} %pad_add_fusion.idx, bf16[64,96,384]{2,1,0:T(8,128)(2,1)} %get-tuple-element.120.d0, bf16[64,96,384]{2,1,0:T(8,128)(2,1)} %get-tuple-element.122.d1, ...), custom_call_target="tpu_custom_call" | custom-call | flops 7200000000 | bytes 50000000 | tf_op jit(solution)/shard_map/tri_in_bwd/pallas_call | solution.py:220
  686.3 66.0 %back.3 = (bf16[96,128,384]{2,1,0:T(8,128)(2,1)}, f32[640,128]{1,0:T(8,128)}, f32[128,128]{1,0:T(8,128)}, f32[128,128]{1,0:T(8,128)}) custom-call(bf16[2,32,96,384]{3,2,1,0:T(8,128)(2,1)} %get-tuple-element.125.refs_0_, bf16[2,32,96,384]{3,2,1,0:T(8,128)(2,1)} %get-tuple-element.126.refs_1_, bf16[2,32,96,384]{3,2,1,0:T(8,128)(2,1)} %collective-permute-done.15.refs_2_, ...), custom_call_target="tpu_custom_call" | custom-call | flops 9437184000 | bytes 56623104 | tf_op jit(solution)/shard_map/back/pallas_call | solution.py:374
  752.3 44.6 %head.6 = (bf16[64,96,384]{2,1,0:T(8,128)(2,1)}, bf16[64,96,384]{2,1,0:T(8,128)(2,1)}, bf16[96,128,384]{2,1,0:T(8,128)(2,1)}, f32[128,128]{1,0:T(8,128)}, f32[128,128]{1,0:T(8,128)}, /*index=5*/f32[128,128]{1,0:T(8,128)}) custom-call(bf16[2,32,96,384]{3,2,1,0:T(8,128)(2,1)} %get-tuple-element.98.refs_0_, bf16[2,32,96,384]{3,2,1,0:T(8,128)(2,1)} %get-tuple-element.99.refs_1_, ...), custom_call_target="tpu_custom_call" | custom-call | flops 3774873600 | bytes 47185920 | tf_op jit(solution)/shard_map/head/pallas_call | solution.py:315
  797.3 53.1 %back.4.refs_5_ = bf16[96,128,384]{2,1,0:T(8,128)(2,1)} custom-call(bf16[2,32,96,384]{3,2,1,0:T(8,128)(2,1)} %get-tuple-element.125.refs_0_, bf16[2,32,96,384]{3,2,1,0:T(8,128)(2,1)} %get-tuple-element.126.refs_1_, bf16[2,32,96,384]{3,2,1,0:T(8,128)(2,1)} %collective-permute-done.15.refs_2_, bf16[2,32,96,384]{3,2,1,0:T(8,128)(2,1)} %collective-permute-done.16.refs_3_, ...), custom_call_target="tpu_custom_call" | custom-call | flops 9437184000 | bytes 56623104 | tf_op jit(solution)/shard_map/back/pallas_call | solution.py:374
  850.4 42.2 %head.7 = (bf16[64,96,384]{2,1,0:T(8,128)(2,1)}, bf16[64,96,384]{2,1,0:T(8,128)(2,1)}, bf16[96,128,384]{2,1,0:T(8,128)(2,1)}) custom-call(bf16[2,32,96,384]{3,2,1,0:T(8,128)(2,1)} %get-tuple-element.98.refs_0_, bf16[2,32,96,384]{3,2,1,0:T(8,128)(2,1)} %get-tuple-element.99.refs_1_, bf16[2,32,96,384]{3,2,1,0:T(8,128)(2,1)} %collective-permute-done.6.refs_2_, ...), custom_call_target="tpu_custom_call" | custom-call | flops 3774873600 | bytes 47185920 | tf_op jit(solution)/shard_map/head/pallas_call | solution.py:315
  900.4 15.9 %tri_out_bwd.3 = (bf16[1,32,96,384]{3,2,1,0:T(8,128)(2,1)}, bf16[1,32,96,384]{3,2,1,0:T(8,128)(2,1)}, bf16[1,32,96,384]{3,2,1,0:T(8,128)(2,1)}, bf16[1,32,96,384]{3,2,1,0:T(8,128)(2,1)}) custom-call(s32[4]{0:T(128)} %pad_add_fusion.idx, bf16[64,96,384]{2,1,0:T(8,128)(2,1)} %get-tuple-element.135.d0, bf16[64,96,384]{2,1,0:T(8,128)(2,1)} %get-tuple-element.138.d1, ...), custom_call_target="tpu_custom_call" | custom-call | flops 3600000000 | bytes 50000000 | tf_op jit(solution)/shard_map/tri_out_bwd/pallas_call | solution.py:220
  916.9 16.1 %tri_out_bwd.2 = (bf16[1,32,96,384]{3,2,1,0:T(8,128)(2,1)}, bf16[1,32,96,384]{3,2,1,0:T(8,128)(2,1)}, bf16[1,32,96,384]{3,2,1,0:T(8,128)(2,1)}, bf16[1,32,96,384]{3,2,1,0:T(8,128)(2,1)}) custom-call(s32[4]{0:T(128)} %pad_add_fusion.idx, bf16[64,96,384]{2,1,0:T(8,128)(2,1)} %get-tuple-element.135.d0, bf16[64,96,384]{2,1,0:T(8,128)(2,1)} %get-tuple-element.138.d1, ...), custom_call_target="tpu_custom_call" | custom-call | flops 3600000000 | bytes 50000000 | tf_op jit(solution)/shard_map/tri_out_bwd/pallas_call | solution.py:220
  940.9 65.0 %back.5 = (bf16[96,384,128]{2,1,0:T(8,128)(2,1)}, f32[640,128]{1,0:T(8,128)}, f32[128,128]{1,0:T(8,128)}, f32[128,128]{1,0:T(8,128)}) custom-call(bf16[1,32,96,384]{3,2,1,0:T(8,128)(2,1)} %get-tuple-element.141.refs_0_, bf16[1,32,96,384]{3,2,1,0:T(8,128)(2,1)} %get-tuple-element.142.refs_1_, bf16[1,32,96,384]{3,2,1,0:T(8,128)(2,1)} %collective-permute-done.21.refs_2_, ...), custom_call_target="tpu_custom_call" | custom-call | flops 9437184000 | bytes 56623104 | tf_op jit(solution)/shard_map/back/pallas_call | solution.py:374
  1010.5 21.1 %all-reduce.2 = (bf16[2,2,128]{2,1,0:T(2,128)(2,1)}, bf16[2,128,512]{2,1,0:T(8,128)(2,1)}, bf16[2,128,128]{1,2,0:T(8,128)(2,1)S(1)}, bf16[2,2,128]{2,1,0:T(2,128)(2,1)}, bf16[2,128,128]{2,1,0:T(8,128)(2,1)}) all-reduce(f32[2,2,128]{2,1,0:T(2,128)S(1)} %pad_maximum_fusion.9, ...), channel_id=1, replica_groups=mesh['data'=2,'dap'=4] {'dap'}, use_global_device_ids=true, to_apply=%region_4.5 | all-reduce | flops 197632 | bytes 1185792 | tf_op jit(solution)/shard_map/psum | solution.py:475
  (179 shorter events, 78.3 us)
Async XLA Ops:
  16.6 30.0 %collective-permute-start.1 = (bf16[96,128,384]{2,1,0:T(8,128)(2,1)}, bf16[96,128,384]{2,1,0:T(8,128)(2,1)}, u32[]{:S(2)}, u32[]{:S(2)}) collective-permute-start(bf16[96,128,384]{2,1,0:T(8,128)(2,1)} %get-tuple-element.85.x_ref.refs_5_.refs_4_), channel_id=1, source_target_pairs={{0,1},{1,0},{2,3},{3,2},{4,5},{5,4},{6,7},{7,6}} | collective-permute-start | bytes 28311560 | tf_op jit(solution)/shard_map/ppermute | solution.py:392
  17.5 206.1 %collective-permute-start = (bf16[96,384,128]{2,1,0:T(8,128)(2,1)}, bf16[96,384,128]{2,1,0:T(8,128)(2,1)}, u32[]{:S(2)}, u32[]{:S(2)}) collective-permute-start(bf16[96,384,128]{2,1,0:T(8,128)(2,1)} %z_ref.3), channel_id=1, source_target_pairs={{0,2},{2,0},{1,3},{3,1},{4,6},{6,4},{5,7},{7,5}} | collective-permute-start | bytes 28311560 | tf_op jit(solution)/shard_map/ppermute | solution.py:389
  20.0 26.7 %collective-permute-start.2 = (f32[96,384]{1,0:T(8,128)S(1)}, f32[96,384]{1,0:T(8,128)S(1)}, u32[]{:S(2)}, u32[]{:S(2)}) collective-permute-start(f32[96,384]{1,0:T(8,128)S(1)} %convert_element_type.53.m_ref.refs_11_), channel_id=1, source_target_pairs={{0,1},{1,0},{2,3},{3,2},{4,5},{5,4},{6,7},{7,6}} | collective-permute-start | bytes 442376 | tf_op jit(solution)/shard_map/ppermute | solution.py:392
  238.0 21.3 %collective-permute-start.3 = (bf16[96,128,384]{2,1,0:T(8,128)(2,1)}, bf16[96,128,384]{2,1,0:T(8,128)(2,1)}, u32[]{:S(2)}, u32[]{:S(2)}) collective-permute-start(bf16[96,128,384]{2,1,0:T(8,128)(2,1)} %get-tuple-element.91.x_ref.refs_5_.refs_4_), channel_id=1, source_target_pairs={{0,1},{1,0},{2,3},{3,2},{4,5},{5,4},{6,7},{7,6}} | collective-permute-start | bytes 28311560 | tf_op jit(solution)/shard_map/ppermute | solution.py:392
  238.1 6.2 collective-permute-start.4
  244.3 15.0 %collective-permute-start.5 = (f32[96,384]{1,0:T(8,128)S(1)}, f32[96,384]{1,0:T(8,128)S(1)}, u32[]{:S(2)}, u32[]{:S(2)}) collective-permute-start(f32[96,384]{1,0:T(8,128)S(1)} %collective-permute-done.4.m_ref.refs_11_), channel_id=1, source_target_pairs={{0,1},{1,0},{2,3},{3,2},{4,5},{5,4},{6,7},{7,6}} | collective-permute-start | bytes 442376 | tf_op jit(solution)/shard_map/ppermute | solution.py:392
  301.9 7.9 collective-permute-start.7
  301.9 14.6 %collective-permute-start.6 = (bf16[2,32,96,384]{3,2,1,0:T(8,128)(2,1)}, bf16[2,32,96,384]{3,2,1,0:T(8,128)(2,1)}, u32[]{:S(2)}, u32[]{:S(2)}) collective-permute-start(bf16[2,32,96,384]{3,2,1,0:T(8,128)(2,1)} %get-tuple-element.100), channel_id=1, source_target_pairs={{0,1},{1,0},{2,3},{3,2},{4,5},{5,4},{6,7},{7,6}} | collective-permute-start | bytes 14155784 | tf_op jit(solution)/shard_map/ppermute | solution.py:392
  302.7 41.5 %copy-start.13 = (bf16[128,128]{1,0:T(8,128)(2,1)}, bf16[128,128]{1,0:T(8,128)(2,1)S(1)}, u32[]{:S(2)}) copy-start(bf16[128,128]{1,0:T(8,128)(2,1)S(1)} %get-tuple-element.210.refs_9_) | copy-start | bytes 98308
  302.7 159.9 %copy-start.12 = (bf16[128,128]{1,0:T(8,128)(2,1)}, bf16[128,128]{1,0:T(8,128)(2,1)S(1)}, u32[]{:S(2)}) copy-start(bf16[128,128]{1,0:T(8,128)(2,1)S(1)} %get-tuple-element.209.refs_9_) | copy-start | bytes 98308
  344.2 46.0 %collective-permute-start.9 = (bf16[96,128,384]{2,1,0:T(8,128)(2,1)}, bf16[96,128,384]{2,1,0:T(8,128)(2,1)}, u32[]{:S(2)}, u32[]{:S(2)}) collective-permute-start(bf16[96,128,384]{2,1,0:T(8,128)(2,1)} %get-tuple-element.105.x_ref.refs_4_), channel_id=1, source_target_pairs={{0,1},{1,0},{2,3},{3,2},{4,5},{5,4},{6,7},{7,6}} | collective-permute-start | bytes 28311560 | tf_op jit(solution)/shard_map/ppermute | solution.py:392
  372.2 46.8 %collective-permute-start.8 = (bf16[96,128,384]{2,1,0:T(8,128)(2,1)}, bf16[96,128,384]{2,1,0:T(8,128)(2,1)}, u32[]{:S(2)}, u32[]{:S(2)}) collective-permute-start(bf16[96,128,384]{2,1,0:T(8,128)(2,1)} %get-tuple-element.103.x_ref.refs_4_), channel_id=1, source_target_pairs={{0,1},{1,0},{2,3},{3,2},{4,5},{5,4},{6,7},{7,6}} | collective-permute-start | bytes 28311560 | tf_op jit(solution)/shard_map/ppermute | solution.py:392
  372.5 205.0 %collective-permute-start.12 = (bf16[96,128,384]{2,1,0:T(8,128)(2,1)}, bf16[96,128,384]{2,1,0:T(8,128)(2,1)}, u32[]{:S(2)}, u32[]{:S(2)}) collective-permute-start(bf16[96,128,384]{2,1,0:T(8,128)(2,1)} %turn.1.refs_5_.refs_9_), channel_id=1, source_target_pairs={{0,2},{2,0},{1,3},{3,1},{4,6},{6,4},{5,7},{7,5}} | collective-permute-start | bytes 28311560 | tf_op jit(solution)/shard_map/ppermute | solution.py:389
  447.7 17.1 %collective-permute-start.11 = (bf16[2,32,96,384]{3,2,1,0:T(8,128)(2,1)}, bf16[2,32,96,384]{3,2,1,0:T(8,128)(2,1)}, u32[]{:S(2)}, u32[]{:S(2)}) collective-permute-start(bf16[2,32,96,384]{3,2,1,0:T(8,128)(2,1)} %get-tuple-element.117), channel_id=1, source_target_pairs={{0,1},{1,0},{2,3},{3,2},{4,5},{5,4},{6,7},{7,6}} | collective-permute-start | bytes 14155784 | tf_op jit(solution)/shard_map/ppermute | solution.py:392
  462.0 8.0 collective-permute-start.10
  517.3 102.4 %collective-permute-start.13 = (bf16[64,96,384]{2,1,0:T(8,128)(2,1)}, bf16[64,96,384]{2,1,0:T(8,128)(2,1)}, u32[]{:S(2)}, u32[]{:S(2)}) collective-permute-start(bf16[64,96,384]{2,1,0:T(8,128)(2,1)} %get-tuple-element.123), channel_id=1, source_target_pairs={{0,1},{1,0},{2,3},{3,2},{4,5},{5,4},{6,7},{7,6}} | collective-permute-start | bytes 14155784 | tf_op jit(solution)/shard_map/ppermute | solution.py:392
  619.6 7.9 collective-permute-start.14
  649.5 24.6 %collective-permute-start.16 = (bf16[2,32,96,384]{3,2,1,0:T(8,128)(2,1)}, bf16[2,32,96,384]{3,2,1,0:T(8,128)(2,1)}, u32[]{:S(2)}, u32[]{:S(2)}) collective-permute-start(bf16[2,32,96,384]{3,2,1,0:T(8,128)(2,1)} %get-tuple-element.128), channel_id=1, source_target_pairs={{0,1},{1,0},{2,3},{3,2},{4,5},{5,4},{6,7},{7,6}} | collective-permute-start | bytes 14155784 | tf_op jit(solution)/shard_map/ppermute | solution.py:392
  649.6 22.9 %copy-start.9 = (bf16[2,128,512]{2,1,0:T(8,128)(2,1)S(1)}, bf16[2,128,512]{2,1,0:T(8,128)(2,1)}, u32[]{:S(2)}) copy-start(bf16[2,128,512]{2,1,0:T(8,128)(2,1)} %param.12) | copy-start | bytes 786436
  649.6 24.4 %collective-permute-start.18 = (bf16[2,32,96,384]{3,2,1,0:T(8,128)(2,1)}, bf16[2,32,96,384]{3,2,1,0:T(8,128)(2,1)}, u32[]{:S(2)}, u32[]{:S(2)}) collective-permute-start(bf16[2,32,96,384]{3,2,1,0:T(8,128)(2,1)} %get-tuple-element.132), channel_id=1, source_target_pairs={{0,1},{1,0},{2,3},{3,2},{4,5},{5,4},{6,7},{7,6}} | collective-permute-start | bytes 14155784 | tf_op jit(solution)/shard_map/ppermute | solution.py:392
  671.7 7.9 collective-permute-start.15
  672.0 14.3 %collective-permute-start.17 = (bf16[2,32,96,384]{3,2,1,0:T(8,128)(2,1)}, bf16[2,32,96,384]{3,2,1,0:T(8,128)(2,1)}, u32[]{:S(2)}, u32[]{:S(2)}) collective-permute-start(bf16[2,32,96,384]{3,2,1,0:T(8,128)(2,1)} %get-tuple-element.131), channel_id=1, source_target_pairs={{0,1},{1,0},{2,3},{3,2},{4,5},{5,4},{6,7},{7,6}} | collective-permute-start | bytes 14155784 | tf_op jit(solution)/shard_map/ppermute | solution.py:392
  796.9 97.5 %collective-permute-start.19 = (bf16[64,96,384]{2,1,0:T(8,128)(2,1)}, bf16[64,96,384]{2,1,0:T(8,128)(2,1)}, u32[]{:S(2)}, u32[]{:S(2)}) collective-permute-start(bf16[64,96,384]{2,1,0:T(8,128)(2,1)} %get-tuple-element.139), channel_id=1, source_target_pairs={{0,1},{1,0},{2,3},{3,2},{4,5},{5,4},{6,7},{7,6}} | collective-permute-start | bytes 14155784 | tf_op jit(solution)/shard_map/ppermute | solution.py:392
  850.3 43.2 %copy-start.19 = (bf16[128,128]{1,0:T(8,128)(2,1)S(1)}, bf16[128,128]{1,0:T(8,128)(2,1)}, u32[]{:S(2)}) copy-start(bf16[128,128]{1,0:T(8,128)(2,1)} %get-tuple-element.205) | copy-start | bytes 98308
  850.3 43.8 %copy-start.22 = (f32[128,128]{1,0:T(8,128)S(1)}, f32[128,128]{1,0:T(8,128)}, u32[]{:S(2)}) copy-start(f32[128,128]{1,0:T(8,128)} %get-tuple-element.159) | copy-start | bytes 196612
  850.3 43.9 %copy-start.21 = (f32[128,128]{1,0:T(8,128)S(1)}, f32[128,128]{1,0:T(8,128)}, u32[]{:S(2)}) copy-start(f32[128,128]{1,0:T(8,128)} %get-tuple-element.160) | copy-start | bytes 196612
  850.3 44.1 %copy-start.16 = (f32[128,128]{1,0:T(8,128)S(1)}, f32[128,128]{1,0:T(8,128)}, u32[]{:S(2)}) copy-start(f32[128,128]{1,0:T(8,128)} %get-tuple-element.162) | copy-start | bytes 196612
  892.5 7.9 collective-permute-start.20
  916.3 19.6 %collective-permute-start.22 = (bf16[1,32,96,384]{3,2,1,0:T(8,128)(2,1)}, bf16[1,32,96,384]{3,2,1,0:T(8,128)(2,1)S(1)}, u32[]{:S(2)}, u32[]{:S(2)}) collective-permute-start(bf16[1,32,96,384]{3,2,1,0:T(8,128)(2,1)} %get-tuple-element.144), channel_id=1, source_target_pairs={{0,1},{1,0},{2,3},{3,2},{4,5},{5,4},{6,7},{7,6}} | collective-permute-start | bytes 7077896 | tf_op jit(solution)/shard_map/ppermute | solution.py:392
  916.5 19.4 %collective-permute-start.24 = (bf16[1,32,96,384]{3,2,1,0:T(8,128)(2,1)}, bf16[1,32,96,384]{3,2,1,0:T(8,128)(2,1)}, u32[]{:S(2)}, u32[]{:S(2)}) collective-permute-start(bf16[1,32,96,384]{3,2,1,0:T(8,128)(2,1)} %get-tuple-element.148), channel_id=1, source_target_pairs={{0,1},{1,0},{2,3},{3,2},{4,5},{5,4},{6,7},{7,6}} | collective-permute-start | bytes 7077896 | tf_op jit(solution)/shard_map/ppermute | solution.py:392
  933.0 4.5 collective-permute-start.21
  933.3 7.6 collective-permute-start.23
  (21 other events, 265.7 us)

commit v3 on v2

--- a/solution.py
+++ b/solution.py
@@ -16,16 +16,15 @@
 CB = 8
 NCH = 2
 HC = H // NCH
-UNROLL = 4
+UNROLL = 2
+G = 2
+ZC = 3
+ZR = RB // ZC
 F32 = jnp.float32
 BF16 = jnp.bfloat16
 ICI_SWAP = [(0, 2), (2, 0), (1, 3), (3, 1)]
 D2D_SWAP = [(0, 1), (1, 0), (2, 3), (3, 2)]
 OWN, CROSS, PART, DIAG = 0, 2, 1, 3
-
-
-def sig(v):
-    return 0.5 * jnp.tanh(0.5 * v) + 0.5
 
 
 def dot(a, b, ca=1, cb=0):
@@ -44,11 +43,34 @@
     return (h * ln_ref[:, 0:1] + ln_ref[:, 1:2]).astype(BF16)
 
 
-def rows_loop(fn, unroll=UNROLL):
+def rows_loop(fn, unroll=UNROLL, n=TI // G):
     def step(i, carry):
         fn(i)
         return carry
-    lax.fori_loop(0, TI, step, 0, unroll=unroll)
+
+    lax.fori_loop(0, n, step, 0, unroll=unroll)
+
+
+def get(ref, i):
+    return jnp.concatenate([ref[G * i + r] for r in range(G)], axis=1)
+
+
+def put(ref, i, v):
+    for r in range(G):
+        ref[G * i + r] = v[:, r * N:(r + 1) * N]
+
+
+def put_turned(ref, i, v):
+    for r in range(G):
+        ref[G * i + r] = v[:, r * N:(r + 1) * N].T
+
+
+def get_mask(ref, i):
+    return jnp.concatenate([ref[pl.ds(G * i + r, 1), :] for r in range(G)], axis=1).astype(BF16)
+
+
+def fold(v):
+    return functools.reduce(lambda p, q: p + q, [v[:, k * 128:(k + 1) * 128] for k in range(G * N // 128)])
 
 
 def fill(scr, refs):
@@ -107,9 +129,7 @@
 
 
 def turn_body(z_ref, zt_ref):
-    def row(i):
-        zt_ref[i] = z_ref[i].T
-    rows_loop(row)
+    rows_loop(lambda i: put(zt_ref, i, jnp.concatenate([z_ref[G * i + r].T for r in range(G)], axis=1)))
 
 
 def turn(z):
@@ -117,28 +137,39 @@
                           cost_estimate=cost(NPOS * C * 40, NPOS * C * 4), name="turn")(z)
 
 
-def norm_body(z_ref, ln_ref, zt_ref, xt_ref):
+def norm_body(z_ref, ln_ref, *rest):
+    zt_ref, xt_ref, xc_ref = rest[-3:]
+
     def row(i):
-        zt = z_ref[i].T
-        zt_ref[i] = zt
+        zt = jnp.concatenate([z_ref[G * i + r].T for r in range(G)], axis=1)
+        put(zt_ref, i, zt)
         h, _ = hat(zt.astype(F32))
-        xt_ref[i] = affine(h, ln_ref)
+        x = affine(h, ln_ref)
+        put(xt_ref, i, x)
+        put(xc_ref, i, x)
+
     rows_loop(row)
 
 
-def norm(z, ln):
-    return pl.pallas_call(norm_body, grid=(RB // TI,), in_specs=[act_spec(), const_spec((C, 2))], out_specs=[actt_spec()] * 2,
-                          out_shape=[ACTT] * 2, cost_estimate=cost(NPOS * C * 60, NPOS * C * 6), name="norm")(z, ln)
+def norm(z, ln, part=0, full=None):
+    rows = z.shape[0]
+    off = part * (ZR // TI)
+    extra = () if full is None else tuple(full)
+    spec = pl.BlockSpec((TI, C, N), lambda i: (i + off, 0, 0))
+    return pl.pallas_call(norm_body, grid=(rows // TI,), in_specs=[act_spec(), const_spec((C, 2))] + [pl.BlockSpec(memory_space=pl.ANY)] * len(extra),
+                          out_specs=[spec, spec, actt_spec()], out_shape=[ACTT, ACTT, jax.ShapeDtypeStruct((rows, C, N), BF16)],
+                          input_output_aliases={2: 0, 3: 1} if extra else {},
+                          cost_estimate=cost(rows * N * C * 60, rows * N * C * 8), name="norm")(z, ln, *extra)
 
 
 def prep_body(base, x_ref, m_ref, wt_ref, *rest):
     a_out, b_out, sa, sb = rest[-4:]
 
     def row(i):
-        mrow = m_ref[pl.ds(i, 1), :]
-        p = dot(wt_ref[...], x_ref[i])
-        sa[i] = (mrow * sig(p[H:2 * H]) * p[0:H]).astype(BF16)
-        sb[i] = (mrow * sig(p[3 * H:4 * H]) * p[2 * H:3 * H]).astype(BF16)
+        p = dot(wt_ref[...], get(x_ref, i) * get_mask(m_ref, i))
+        for out, at in ((sa, 0), (sb, 2 * H)):
+            lin = p[at:at + H]
+            put(out, i, (lin * jnp.tanh(p[at + H:at + 2 * H]) + lin).astype(BF16))
 
     rows_loop(row)
     flush(sa, [a_out])
@@ -146,17 +177,19 @@
 
 
 def prep(base, xt, mask, wt, full=None):
+    rows = xt.shape[0]
+    npos = rows * N
     out = jax.ShapeDtypeStruct((H, N, N), BF16)
     spec = pl.BlockSpec((H, TI, N), lambda i, b: (0, b[0] + i, 0))
     extra = () if full is None else tuple(full)
     grid_spec = pltpu.PrefetchScalarGridSpec(
-        num_scalar_prefetch=1, grid=(RB // TI,),
+        num_scalar_prefetch=1, grid=(rows // TI,),
         in_specs=[actt_spec(), mask_spec_(), const_spec((4 * H, C))] + [pl.BlockSpec(memory_space=pl.ANY)] * len(extra),
         out_specs=[spec, spec], scratch_shapes=[scr(H), scr(H)])
     return pl.pallas_call(
         prep_body, grid_spec=grid_spec, out_shape=[out, out],
         input_output_aliases={4: 0, 5: 1} if extra else {},
-        cost_estimate=cost(NPOS * C * 400, NPOS * C * 4, NPOS * C), name="prep",
+        cost_estimate=cost(npos * C * 400, npos * C * 4, npos * C), name="prep",
     )(base, xt, mask, wt, *extra)
 
 
@@ -172,17 +205,21 @@
 
 
 def tri_out_body(idx, a, b, keep, send):
-    for c in range(CB):
+    def chan(c):
         lhs = jnp.concatenate(block_rows(idx, a, c), axis=0)
         emit(dot(lhs, b[c], 1, 1).astype(BF16), keep, send, c)
 
+    rows_loop(chan, 2, CB)
+
 
 def tri_in_body(idx, a, b, keep, send, s):
-    for c in range(CB):
+    def chan(c):
         s[c] = a[c].T
         lhs = jnp.concatenate(block_rows(idx, s, c), axis=0)
         emit(dot(lhs, b[c]).astype(BF16), keep, send, c)
 
+    rows_loop(chan, 2, CB)
+
 
 def gather_dt(idx, parts, c, s):
     for k, part in enumerate(parts):
@@ -190,14 +227,16 @@
 
 
 def tri_in_bwd_body(idx, d0, d1, d2, d3, a, b, dak, das, dbk, dbs, s):
-    for c in range(CB):
+    def chan(c):
         gather_dt(idx, (d0, d1, d2, d3), c, s)
         emit(dot(jnp.concatenate(block_rows(idx, b, c), axis=0), s[c], 1, 1).astype(BF16), dak, das, c)
         emit(dot(jnp.concatenate(block_rows(idx, a, c), axis=0), s[c]).astype(BF16), dbk, dbs, c)
 
+    rows_loop(chan, 2, CB)
+
 
 def tri_out_bwd_body(idx, d0, d1, d2, d3, a, b, dak, das, dbk, dbs, s, st):
-    for c in range(CB):
+    def chan(c):
         gather_dt(idx, (d0, d1, d2, d3), c, s)
         da = dot(jnp.concatenate([d0[c], d2[c]], axis=0), b[c]).astype(BF16)
         st[c] = s[c].T
@@ -208,8 +247,10 @@
         dbk[0, c] = db[:RB]
         dbs[0, c] = db[RB:]
 
-
-def tri_call(body, idx, part, dts, ab, pieces, n_out, n_scr, flops, name):
+    rows_loop(chan, 2, CB)
+
+
+def tri_call(body, idx, part, dts, ab, pieces, n_out, n_scr, flops):
     off = part * (HC // CB)
     dspec = pl.BlockSpec((CB, RB, N), lambda c, _: (c + off, 0, 0))
     fspec = pl.BlockSpec((CB, N, N), lambda c, _: (c + off, 0, 0))
@@ -218,7 +259,7 @@
         num_scalar_prefetch=1, grid=(HC // CB,), in_specs=[dspec] * len(dts) + [fspec] * len(ab),
         out_specs=[ospec] * n_out, scratch_shapes=[pltpu.VMEM((CB, N, N), BF16)] * n_scr)
     return pl.pallas_call(body, grid_spec=grid_spec, out_shape=[jax.ShapeDtypeStruct((pieces, HC, RB, N), BF16)] * n_out,
-                          cost_estimate=cost(flops, 50e6), name=name)(idx, *dts, *ab)
+                          cost_estimate=cost(flops, 50e6))(idx, *dts, *ab)
 
 
 def finish_body(*refs):
@@ -227,13 +268,13 @@
     fill(st, ts)
 
     def row(i):
-        th, _ = hat(st[i].astype(F32))
+        th, _ = hat(get(st, i).astype(F32))
         upd = dot(wo_ref[...], affine(th, lnq_ref))
-        gate = sig(dot(wg_ref[...], x_ref[i]))
-        zn = (z_ref[i].astype(F32) + gate * upd).astype(BF16)
-        z_out[i] = zn
+        gate = jnp.tanh(dot(wg_ref[...], get(x_ref, i)))
+        zn = (get(z_ref, i).astype(F32) + (gate * upd + upd)).astype(BF16)
+        put(z_out, i, zn)
         h, _ = hat(zn.astype(F32))
-        x_out[i] = affine(h, ln_ref)
+        put(x_out, i, affine(h, ln_ref))
 
     rows_loop(row)
 
@@ -273,25 +314,24 @@
     fill(st, ts)
 
     def row(i):
-        th, rstd = hat(st[i].astype(F32))
+        th, rstd = hat(get(st, i).astype(F32))
         y = affine(th, lnq_ref)
         upd = dot(wot_ref[...], y)
-        gate = sig(dot(wg_ref[...], x_ref[i]))
+        gate = jnp.tanh(dot(wg_ref[...], get(x_ref, i)))
         if emit_z:
-            z_out[i] = (z_ref[i].astype(F32) + gate * upd).astype(BF16).T
-        dgate = g_ref[i].astype(F32) * gate
-        dg_out[i] = (dgate * upd * (1.0 - gate)).astype(BF16)
+            put_turned(z_out, i, (get(z_ref, i).astype(F32) + (gate * upd + upd)).astype(BF16))
+        dgate = get(g_ref, i).astype(F32) * (0.5 * gate + 0.5)
+        put(dg_out, i, (dgate * (upd - upd * gate)).astype(BF16))
         du = dgate.astype(BF16)
         dy = dot(wo_ref[...], du).astype(BF16).astype(F32)
         dh = dy * lnq_ref[:, 0:1]
         m1 = jnp.sum(dh, axis=0, keepdims=True) * (1.0 / C)
         m2 = jnp.sum(dh * th, axis=0, keepdims=True) * (1.0 / C)
-        sd[i] = (rstd * (dh - m1 - th * m2)).astype(BF16)
+        put(sd, i, (rstd * (dh - m1 - th * m2)).astype(BF16))
         if emit_w:
             gwo[...] += dot(y, du, 1, 1)
-            e = dy * th
-            ggain[...] += e[:, 0:128] + e[:, 128:256] + e[:, 256:384]
-            gshift[...] += dy[:, 0:128] + dy[:, 128:256] + dy[:, 256:384]
+            ggain[...] += fold(dy * th)
+            gshift[...] += fold(dy)
 
     rows_loop(row)
     flush(sd, [dt_keep, dt_send])
@@ -337,28 +377,27 @@
     fill(sb, dbs)
 
     def row(i):
-        xh, rstd = hat(z_ref[i].astype(F32))
+        xh, rstd = hat(get(z_ref, i).astype(F32))
         x = affine(xh, ln_ref)
-        mrow = m_ref[pl.ds(i, 1), :]
+        mrow = get_mask(m_ref, i)
         ds = []
         for s, at in ((sa, 0), (sb, 2 * C)):
             p = dot(wt_ref[at:at + 2 * C], x)
-            sg = sig(p[C:])
-            t0 = s[i].astype(F32) * mrow * sg
+            th = jnp.tanh(p[C:])
+            t0 = (get(s, i) * mrow).astype(F32) * (0.5 * th + 0.5)
             ds.append(t0.astype(BF16))
-            ds.append((t0 * p[:C] * (1.0 - sg)).astype(BF16))
-        dp = jnp.concatenate(ds + [dg_ref[i]], axis=0)
+            ds.append((t0 * (p[:C] - p[:C] * th)).astype(BF16))
+        dp = jnp.concatenate(ds + [get(dg_ref, i)], axis=0)
         dx = dot(wb_ref[...], dp).astype(BF16).astype(F32)
         dh = dx * ln_ref[:, 0:1]
         m1 = jnp.sum(dh, axis=0, keepdims=True) * (1.0 / C)
         m2 = jnp.sum(dh * xh, axis=0, keepdims=True) * (1.0 / C)
-        d = (g_ref[i].astype(F32) + rstd * (dh - m1 - xh * m2)).astype(BF16)
-        d_out[i] = d.T if last else d
+        d = (get(g_ref, i).astype(F32) + rstd * (dh - m1 - xh * m2)).astype(BF16)
+        (put_turned if last else put)(d_out, i, d)
         if emit_w:
             gw[...] += dot(dp, x, 1, 1)
-            e = dx * xh
-            ggain[...] += e[:, 0:128] + e[:, 128:256] + e[:, 256:384]
-            gshift[...] += dx[:, 0:128] + dx[:, 128:256] + dx[:, 256:384]
+            ggain[...] += fold(dx * xh)
+            gshift[...] += fold(dx)
 
     rows_loop(row)
 
@@ -404,37 +443,43 @@
         m_cross = ici(m_own)
         m_part = d2d(m_own)
         m_diag = d2d(m_cross)
-        z_cross = ici(pair_act)
 
         ln = [ln_pair[u].T.astype(F32) for u in range(2)]
         lnq = [local(ln_chan[u].T.astype(F32), 0) for u in range(2)]
         wp4 = [local(w_proj[u].reshape(C, 4, C), 2) for u in range(2)]
-        wt_half = [wp4[u][:, :, :H].reshape(C, 4 * H).T for u in range(2)]
-        wt = [wp4[u].reshape(C, 4 * C).T for u in range(2)]
+        wt_half = [(0.5 * wp4[u][:, :, :H]).reshape(C, 4 * H).T for u in range(2)]
+        wt = [(0.5 * wp4[u]).reshape(C, 4 * C).T for u in range(2)]
         wb = [jnp.concatenate([wp4[u].reshape(C, 4 * C), w_gate[u]], axis=1) for u in range(2)]
-        wgt = [w_gate[u].T for u in range(2)]
+        wgt = [0.5 * w_gate[u].T for u in range(2)]
         wo = [local(w_out[u], 0) for u in range(2)]
-        wot = [wo[u].T for u in range(2)]
-
-        def products(body, name, dts, a, b, pieces, n_scr, flops):
+        wot = [0.5 * wo[u].T for u in range(2)]
+
+        def products(body, dts, a, b, pieces, n_scr, flops):
             n_out = 4 if dts else 2
-            res = [tri_call(body, blocks, part, dts, (a, b), pieces, n_out, n_scr, flops / NCH, name) for part in range(NCH)]
+            res = [tri_call(body, blocks, part, dts, (a, b), pieces, n_out, n_scr, flops / NCH) for part in range(NCH)]
             keeps = [[r[j] for r in res] for j in range(0, n_out, 2)]
             sends = [[d2d(r[j]) for r in res] for j in range(1, n_out, 2)]
             return [k + s for k, s in zip(keeps, sends)]
 
-        zt_own, xt_own = norm(pair_act, ln[0])
+        z_parts = []
+        for j in range(ZC):
+            z_parts.append(ici(pair_act[j * ZR:(j + 1) * ZR]))
+        zt_own, xt_own, _ = norm(pair_act, ln[0])
         xt_part = d2d(xt_own)
         gt_own = turn(d_pair_out)
+        gt_cross = ici(gt_own)
         ab1 = prep(base[0], xt_own, m_own, wt_half[0])
         ab1 = prep(base[2], xt_part, m_part, wt_half[0], ab1)
-        gt_src, z_cross, a1, b1 = lax.optimization_barrier((gt_own, z_cross, ab1[0], ab1[1]))
-        gt_cross = ici(gt_src)
-        zt_cross, xt_cross = norm(z_cross, ln[0])
-        xt_diag = d2d(xt_cross)
-        ab1 = prep(base[1], xt_cross, m_cross, wt_half[0], (a1, b1))
-        a1, b1 = prep(base[3], xt_diag, m_diag, wt_half[0], ab1)
-        t1, = products(tri_out_body, "tri_out", (), a1, b1, 2, 0, 7.2e9)
+        full = None
+        for j in range(ZC):
+            zt_cross, xt_cross, xc = norm(z_parts[j], ln[0], j, full)
+            full = (zt_cross, xt_cross)
+            xd = d2d(xc)
+            rows = slice(j * ZR, (j + 1) * ZR)
+            ab1 = prep(base[1] + j * (ZR // TI), xc, m_cross[rows], wt_half[0], ab1)
+            ab1 = prep(base[3] + j * (ZR // TI), xd, m_diag[rows], wt_half[0], ab1)
+        a1, b1 = ab1
+        t1, = products(tri_out_body, (), a1, b1, 2, 0, 7.2e9)
         yt_own, vt_own = finish(0, t1, zt_own, xt_own, wgt[0], lnq[0], wot[0], ln[1])
         vt_part = d2d(vt_own)
         yt_cross, vt_cross = finish(1, t1, zt_cross, xt_cross, wgt[0], lnq[0], wot[0], ln[1])
@@ -444,13 +489,13 @@
         ab2 = prep(base[2], vt_part, m_part, wt_half[1], ab2)
         ab2 = prep(base[1], vt_cross, m_cross, wt_half[1], ab2)
         a2, b2 = prep(base[3], vt_diag, m_diag, wt_half[1], ab2)
-        t2, = products(tri_in_body, "tri_in", (), a2, b2, 2, 1, 7.2e9)
+        t2, = products(tri_in_body, (), a2, b2, 2, 1, 7.2e9)
 
         dk_own, ds_own, dg2_own, pair_out, gwo2, gq2g, gq2s = head(0, t2, vt_own, gt_own, wgt[1], lnq[1], wot[1], wo[1], yt_own, True)
         dk_part = d2d(ds_own)
         dk_cross, ds_cross, dg2_cross = head(1, t2, vt_cross, gt_cross, wgt[1], lnq[1], wot[1], wo[1])
         dk_diag = d2d(ds_cross)
-        da2, db2 = products(tri_in_bwd_body, "tri_in_bwd", (dk_own, dk_cross, dk_part, dk_diag), a2, b2, 2, 1, 14.4e9)
+        da2, db2 = products(tri_in_bwd_body, (dk_own, dk_cross, dk_part, dk_diag), a2, b2, 2, 1, 14.4e9)
         et_own, gw2, gp2g, gp2s = back(0, da2, db2, yt_own, gt_own, dg2_own, m_own, ln[1], wt[1], wb[1], True, False)
         et_cross, = back(1, da2, db2, yt_cross, gt_cross, dg2_cross, m_cross, ln[1], wt[1], wb[1], False, False)
 
@@ -458,21 +503,31 @@
         dk_part = d2d(ds_own)
         dk_cross, ds_cross, _ = head(1, t1, xt_cross, et_cross, wgt[0], lnq[0], wot[0], wo[0])
         dk_diag = d2d(ds_cross)
-        da1, db1 = products(tri_out_bwd_body, "tri_out_bwd", (dk_own, dk_cross, dk_part, dk_diag), a1, b1, 1, 2, 7.2e9)
+        da1, db1 = products(tri_out_bwd_body, (dk_own, dk_cross, dk_part, dk_diag), a1, b1, 1, 2, 7.2e9)
         d_pair, gw1, gp1g, gp1s = back(0, da1, db1, zt_own, et_own, dg1_own, m_own, ln[0], wt[0], wb[0], True, True)
 
         def vec(gg, gs):
             return jnp.stack([jnp.sum(gg, axis=1), jnp.sum(gs, axis=1)])
 
-        def proj(g):
-            return local(g[:4 * C].T.reshape(C, 4, C), 2).reshape(C, 4 * C)
-
-        grads = (jnp.stack([vec(gp1g, gp1s), vec(gp2g, gp2s)]),
-                 jnp.stack([proj(gw1), proj(gw2)]),
-                 jnp.stack([gw1[4 * C:].T, gw2[4 * C:].T]),
-                 jnp.stack([local(vec(gq1g, gq1s), 1), local(vec(gq2g, gq2s), 1)]),
-                 jnp.stack([local(gwo1, 0), local(gwo2, 0)]))
-        sums = lax.psum(grads, AX)
-        return (pair_out, d_pair) + tuple(v.astype(BF16) for v in sums)
+        def total(*parts):
+            for swap in (d2d, ici):
+                parts = tuple(v + swap(v) for v in parts)
+            return parts
+
+        def sums(gw, gpg, gps, gqg, gqs, gwo):
+            vecs = jnp.concatenate([vec(gpg, gps), local(vec(gqg, gqs), 1)], axis=0)
+            gw, gwo, vecs = total(gw, local(gwo, 0), jnp.concatenate([vecs, jnp.zeros_like(vecs)], axis=0))
+            return vecs[0:2], proj_local(gw), gw[4 * C:].T, vecs[2:4], gwo
+
+        def proj_local(g):
+            return g[:4 * C].T
+
+        def common(g):
+            return jnp.concatenate([local(g[:4 * C].reshape(4, C, C), 1).reshape(4 * C, C), g[4 * C:]], axis=0)
+
+        s2 = sums(common(gw2), gp2g, gp2s, gq2g, gq2s, gwo2)
+        s1 = sums(common(gw1), gp1g, gp1s, gq1g, gq1s, gwo1)
+        return (pair_out, d_pair) + tuple(jnp.stack([p, q]).astype(BF16) for p, q in zip(s1, s2))
+
 
     return jax.shard_map(device_step, mesh=mesh, in_specs=(row_spec, mask_spec, row_spec, full_spec, full_spec, full_spec, full_spec, full_spec), out_specs=(row_spec, row_spec, grad_spec, grad_spec, grad_spec, grad_spec, grad_spec), check_vma=False)

time: 1040 us -> 1110 us (1.067)
  waiting for transfers between devices: 272 us -> 372 us
  Pallas kernels: 702 us -> 670 us
  blocking collectives: 21.1 us -> 0 us
    ppermute x3 -> x11, waiting for transfers between devices: 226 us -> 326 us  [ici(): return lax.ppermute(v, AX, ICI_SWAP)]
    pallas_call x4, Pallas kernels: 176 us -> 142 us  [head(): pl.pallas_call(functools.partial(head_body, emit_z, emit_w), grid=(RB //...]
    psum x1 -> x0, blocking collectives: 21.1 us -> none  [device_step(): sums = lax.psum(grads, AX)]
    pallas_call x3, Pallas kernels: 184 us -> 163 us  [back(): pl.pallas_call(functools.partial(back_body, n, emit_w, last), grid=(RB //...]
    pallas_call x8 -> x12, Pallas kernels: 115 us -> 127 us  [prep(): pl.pallas_call(prep_body, grid_spec=grid_spec, out_shape=[out, out], inpu...]
    pallas_call x2 -> x4, Pallas kernels: 29 us -> 35.4 us  [norm(): pl.pallas_call(norm_body, grid=(rows // TI,), in_specs=[act_spec(), const...]
    ppermute x22 -> x30, waiting for transfers between devices: 46.7 us -> 46.1 us  [d2d(): return lax.ppermute(v, AX, D2D_SWAP)]
  transfers between devices with their start and end apart: 25 -> 41, of which waited for: 12 -> 19; matrix products, arithmetic and copies ran while one was open for 1% -> 3% of each run, Pallas kernels for 38% -> 36%
where the time goes in v3:
time: 1110 us; the launch traced here: 1100 us
  Pallas kernels  670 us (60%)
  waiting for transfers between devices  372 us (34%)
  local copies, waits for them, and re-layouts  25.7 us (2%)
  starting transfers between devices  18.7 us (2%)
  other arithmetic  15 us (1%)
    ppermute x11, waiting for transfers between devices, ici(): return lax.ppermute(v, AX, ICI_SWAP)  326 us
    pallas_call x3, Pallas kernels, back(): pl.pallas_call(functools.partial(back_body, n, emit_w, last), grid=(RB //...  163 us
    pallas_call x4, Pallas kernels, head(): pl.pallas_call(functools.partial(head_body, emit_z, emit_w), grid=(RB //...  142 us
    pallas_call x8, Pallas kernels, tri_call(): pl.pallas_call(body, grid_spec=grid_spec, out_shape=[jax.ShapeDtypeStruct...  141 us
    pallas_call x12, Pallas kernels, prep(): pl.pallas_call(prep_body, grid_spec=grid_spec, out_shape=[out, out], inpu...  127 us
    pallas_call x2, Pallas kernels, finish(): pl.pallas_call(finish_body, grid=(RB // TI,), in_specs=[piece_spec(k, HC)...  52.4 us
    ppermute x30, waiting for transfers between devices, d2d(): return lax.ppermute(v, AX, D2D_SWAP)  46.1 us
    pallas_call x4, Pallas kernels, norm(): pl.pallas_call(norm_body, grid=(rows // TI,), in_specs=[act_spec(), const...  35.4 us
  transfers between devices with their start and end apart: 41, of which 19 were waited for; matrix products, arithmetic and copies ran while one was open for 3% of the time, Pallas kernels for 36%

profile of v3, /device:TPU:0, one launch (start us, length us, event | category | flops | bytes accessed | tf_op | source)
XLA Modules:
  0.0 1102.8 jit_solution(8235456533224406812)
XLA Ops:
  2.1 15.6 %norm.7 = (bf16[96,128,384]{2,1,0:T(8,128)(2,1)}, bf16[96,128,384]{2,1,0:T(8,128)(2,1)}, bf16[96,128,384]{2,1,0:T(8,128)(2,1)}) custom-call(bf16[96,384,128]{2,1,0:T(8,128)(2,1)} %z_ref.2, f32[128,2]{1,0:T(8,128)} %convert_bitcast_fusion.3.ln_ref.refs_12_), custom_call_target="tpu_custom_call" | custom-call | flops 283115520 | bytes 37748736 | tf_op jit(solution)/shard_map/norm/pallas_call | solution.py:159
  28.4 67.0 %collective-permute-done.2.z_ref = bf16[32,384,128]{2,1,0:T(8,128)(2,1)} collective-permute-done((bf16[32,384,128]{2,1,0:T(8,128)(2,1)S(1)}, bf16[32,384,128]{2,1,0:T(8,128)(2,1)}, u32[]{:S(2)}, u32[]{:S(2)}) %collective-permute-start.2) | collective-permute-done | bytes 3145760 | tf_op jit(solution)/shard_map/ppermute | solution.py:428
  102.1 60.8 %collective-permute-done.1.z_ref = bf16[32,384,128]{2,1,0:T(8,128)(2,1)} collective-permute-done((bf16[32,384,128]{2,1,0:T(8,128)(2,1)}, bf16[32,384,128]{2,1,0:T(8,128)(2,1)}, u32[]{:S(2)}, u32[]{:S(2)}) %collective-permute-start.1) | collective-permute-done | bytes 3145760 | tf_op jit(solution)/shard_map/ppermute | solution.py:428
  169.4 60.7 %collective-permute-done.z_ref = bf16[32,384,128]{2,1,0:T(8,128)(2,1)} collective-permute-done((bf16[32,384,128]{2,1,0:T(8,128)(2,1)S(1)}, bf16[32,384,128]{2,1,0:T(8,128)(2,1)}, u32[]{:S(2)}, u32[]{:S(2)}) %collective-permute-start) | collective-permute-done | bytes 3145760 | tf_op jit(solution)/shard_map/ppermute | solution.py:428
  244.7 14.3 %prep.12 = (bf16[64,384,384]{2,1,0:T(8,128)(2,1)}, bf16[64,384,384]{2,1,0:T(8,128)(2,1)}) custom-call(s32[1]{0:T(128)S(6)} %mul.50.base, bf16[96,128,384]{2,1,0:T(8,128)(2,1)} %get-tuple-element.103.x_ref.refs_5_.refs_4_, f32[96,384]{1,0:T(8,128)} %copy-done, bf16[256,128]{1,0:T(8,128)(2,1)} %bitcast.124), custom_call_target="tpu_custom_call" | custom-call | flops 1887436800 | bytes 18874368 | tf_op jit(solution)/shard_map/prep/pallas_call | solution.py:189
  262.6 14.2 %prep.13 = (bf16[64,384,384]{2,1,0:T(8,128)(2,1)}, bf16[64,384,384]{2,1,0:T(8,128)(2,1)}) custom-call(s32[1]{0:T(128)S(6)} %mul.49.base, bf16[96,128,384]{2,1,0:T(8,128)(2,1)} %collective-permute-done.8.x_ref, f32[96,384]{1,0:T(8,128)} %copy-done.6, bf16[256,128]{1,0:T(8,128)(2,1)} %bitcast.125, ...), custom_call_target="tpu_custom_call", output_to_operand_aliasing={{0}: (4, {}), {1}: (5, {})} | custom-call | flops 1887436800 | bytes 18874368 | tf_op jit(solution)/shard_map/prep/pallas_call | solution.py:189
  319.6 14.5 %shard_map.136 = (bf16[2,32,96,384]{3,2,1,0:T(8,128)(2,1)}, bf16[2,32,96,384]{3,2,1,0:T(8,128)(2,1)}) custom-call(s32[4]{0:T(128)} %pad_add_fusion.idx, bf16[64,384,384]{2,1,0:T(8,128)(2,1)} %get-tuple-element.118.a, bf16[64,384,384]{2,1,0:T(8,128)(2,1)} %get-tuple-element.119.b), custom_call_target="tpu_custom_call" | custom-call | flops 3600000000 | bytes 50000000 | tf_op jit(solution)/shard_map/pallas_call | solution.py:261
  334.1 14.6 %shard_map.135 = (bf16[2,32,96,384]{3,2,1,0:T(8,128)(2,1)}, bf16[2,32,96,384]{3,2,1,0:T(8,128)(2,1)}) custom-call(s32[4]{0:T(128)} %pad_add_fusion.idx, bf16[64,384,384]{2,1,0:T(8,128)(2,1)} %get-tuple-element.118.a, bf16[64,384,384]{2,1,0:T(8,128)(2,1)} %get-tuple-element.119.b), custom_call_target="tpu_custom_call" | custom-call | flops 3600000000 | bytes 50000000 | tf_op jit(solution)/shard_map/pallas_call | solution.py:261
  363.8 26.0 %finish.3 = (bf16[96,128,384]{2,1,0:T(8,128)(2,1)}, bf16[96,128,384]{2,1,0:T(8,128)(2,1)}) custom-call(bf16[2,32,96,384]{3,2,1,0:T(8,128)(2,1)} %get-tuple-element.120.refs_0_, bf16[2,32,96,384]{3,2,1,0:T(8,128)(2,1)} %get-tuple-element.121.refs_1_, bf16[2,32,96,384]{3,2,1,0:T(8,128)(2,1)} %collective-permute-done.10.refs_2_, ...), custom_call_target="tpu_custom_call" | custom-call | flops 2831155200 | bytes 47185920 | tf_op jit(solution)/shard_map/finish/pallas_call | solution.py:283
  390.1 26.4 %finish.2 = (bf16[96,128,384]{2,1,0:T(8,128)(2,1)}, bf16[96,128,384]{2,1,0:T(8,128)(2,1)}) custom-call(bf16[2,32,96,384]{3,2,1,0:T(8,128)(2,1)} %get-tuple-element.120.refs_0_, bf16[2,32,96,384]{3,2,1,0:T(8,128)(2,1)} %get-tuple-element.121.refs_1_, bf16[2,32,96,384]{3,2,1,0:T(8,128)(2,1)} %collective-permute-done.10.refs_2_, ...), custom_call_target="tpu_custom_call" | custom-call | flops 2831155200 | bytes 47185920 | tf_op jit(solution)/shard_map/finish/pallas_call | solution.py:283
  416.7 10.2 turn.1.refs_5_.refs_9_
  428.0 14.2 %prep.20 = (bf16[64,384,384]{2,1,0:T(8,128)(2,1)}, bf16[64,384,384]{2,1,0:T(8,128)(2,1)}) custom-call(s32[1]{0:T(128)S(6)} %mul.50.base, bf16[96,128,384]{2,1,0:T(8,128)(2,1)} %get-tuple-element.128.x_ref.refs_4_, f32[96,384]{1,0:T(8,128)} %copy-done, bf16[256,128]{1,0:T(8,128)(2,1)} %bitcast.132), custom_call_target="tpu_custom_call" | custom-call | flops 1887436800 | bytes 18874368 | tf_op jit(solution)/shard_map/prep/pallas_call | solution.py:189
  442.3 14.2 %prep.21 = (bf16[64,384,384]{2,1,0:T(8,128)(2,1)}, bf16[64,384,384]{2,1,0:T(8,128)(2,1)}) custom-call(s32[1]{0:T(128)S(6)} %mul.49.base, bf16[96,128,384]{2,1,0:T(8,128)(2,1)} %collective-permute-done.13.x_ref, f32[96,384]{1,0:T(8,128)} %copy-done.6, bf16[256,128]{1,0:T(8,128)(2,1)} %bitcast.133, ...), custom_call_target="tpu_custom_call", output_to_operand_aliasing={{0}: (4, {}), {1}: (5, {})} | custom-call | flops 1887436800 | bytes 18874368 | tf_op jit(solution)/shard_map/prep/pallas_call | solution.py:189
  456.5 14.2 %prep.22 = (bf16[64,384,384]{2,1,0:T(8,128)(2,1)}, bf16[64,384,384]{2,1,0:T(8,128)(2,1)}) custom-call(s32[1]{0:T(128)S(6)} %mul.48.base, bf16[96,128,384]{2,1,0:T(8,128)(2,1)} %get-tuple-element.126.x_ref.refs_4_, f32[96,384]{1,0:T(8,128)} %copy-done.3, bf16[256,128]{1,0:T(8,128)(2,1)} %bitcast.134, ...), custom_call_target="tpu_custom_call", output_to_operand_aliasing={{0}: (4, {}), {1}: (5, {})} | custom-call | flops 1887436800 | bytes 18874368 | tf_op jit(solution)/shard_map/prep/pallas_call | solution.py:189
  470.8 14.3 %prep.23 = (bf16[64,384,384]{2,1,0:T(8,128)(2,1)}, bf16[64,384,384]{2,1,0:T(8,128)(2,1)}) custom-call(s32[1]{0:T(128)S(6)} %mul.46.base, bf16[96,128,384]{2,1,0:T(8,128)(2,1)} %collective-permute-done.12.x_ref, f32[96,384]{1,0:T(8,128)} %copy-done.7, bf16[256,128]{1,0:T(8,128)(2,1)} %bitcast.135, ...), custom_call_target="tpu_custom_call", output_to_operand_aliasing={{0}: (4, {}), {1}: (5, {})} | custom-call | flops 1887436800 | bytes 18874368 | tf_op jit(solution)/shard_map/prep/pallas_call | solution.py:189
  485.0 15.7 %shard_map.138 = (bf16[2,32,96,384]{3,2,1,0:T(8,128)(2,1)}, bf16[2,32,96,384]{3,2,1,0:T(8,128)(2,1)}) custom-call(s32[4]{0:T(128)} %pad_add_fusion.idx, bf16[64,384,384]{2,1,0:T(8,128)(2,1)} %get-tuple-element.135.a, bf16[64,384,384]{2,1,0:T(8,128)(2,1)} %get-tuple-element.136.b), custom_call_target="tpu_custom_call" | custom-call | flops 3600000000 | bytes 50000000 | tf_op jit(solution)/shard_map/pallas_call | solution.py:261
  500.8 15.6 %shard_map.137 = (bf16[2,32,96,384]{3,2,1,0:T(8,128)(2,1)}, bf16[2,32,96,384]{3,2,1,0:T(8,128)(2,1)}) custom-call(s32[4]{0:T(128)} %pad_add_fusion.idx, bf16[64,384,384]{2,1,0:T(8,128)(2,1)} %get-tuple-element.135.a, bf16[64,384,384]{2,1,0:T(8,128)(2,1)} %get-tuple-element.136.b), custom_call_target="tpu_custom_call" | custom-call | flops 3600000000 | bytes 50000000 | tf_op jit(solution)/shard_map/pallas_call | solution.py:261
  519.1 113.2 %collective-permute-done.16.refs_5_.refs_9_ = bf16[96,128,384]{2,1,0:T(8,128)(2,1)} collective-permute-done((bf16[96,128,384]{2,1,0:T(8,128)(2,1)}, bf16[96,128,384]{2,1,0:T(8,128)(2,1)}, u32[]{:S(2)}, u32[]{:S(2)}) %collective-permute-start.16) | collective-permute-done | bytes 9437216 | tf_op jit(solution)/shard_map/ppermute | solution.py:428
  632.3 34.3 %head.5 = (bf16[64,96,384]{2,1,0:T(8,128)(2,1)}, bf16[64,96,384]{2,1,0:T(8,128)(2,1)}, bf16[96,128,384]{2,1,0:T(8,128)(2,1)}) custom-call(bf16[2,32,96,384]{3,2,1,0:T(8,128)(2,1)} %get-tuple-element.137.refs_0_, bf16[2,32,96,384]{3,2,1,0:T(8,128)(2,1)} %get-tuple-element.138.refs_1_, bf16[2,32,96,384]{3,2,1,0:T(8,128)(2,1)} %collective-permute-done.14.refs_2_, ...), custom_call_target="tpu_custom_call" | custom-call | flops 3774873600 | bytes 47185920 | tf_op jit(solution)/shard_map/head/pallas_call | solution.py:355
  666.7 38.2 %head.4 = (bf16[64,96,384]{2,1,0:T(8,128)(2,1)}, bf16[64,96,384]{2,1,0:T(8,128)(2,1)}, bf16[96,128,384]{2,1,0:T(8,128)(2,1)}, bf16[96,384,128]{2,1,0:T(8,128)(2,...) custom-call(bf16[2,32,96,384]{3,2,1,0:T(8,128)(2,1)} %get-tuple-element.137.refs_0_, ...), custom_call_target="tpu_custom_call" | custom-call | flops 3774873600 | bytes 47185920 | tf_op jit(solution)/shard_map/head/pallas_call | solution.py:355
  705.3 7.9 collective-permute-done.17.d2
  713.2 22.4 %shard_map.140 = (bf16[2,32,96,384]{3,2,1,0:T(8,128)(2,1)}, bf16[2,32,96,384]{3,2,1,0:T(8,128)(2,1)}, bf16[2,32,96,384]{3,2,1,0:T(8,128)(2,1)}, bf16[2,32,96,384]{3,2,1,0:T(8,128)(2,1)}) custom-call(s32[4]{0:T(128)} %pad_add_fusion.idx, bf16[64,96,384]{2,1,0:T(8,128)(2,1)} %get-tuple-element.143.d0, bf16[64,96,384]{2,1,0:T(8,128)(2,1)} %get-tuple-element.144.d1, ...), custom_call_target="tpu_custom_call" | custom-call | flops 7200000000 | bytes 50000000 | tf_op jit(solution)/shard_map/pallas_call | solution.py:261
  736.1 22.7 %shard_map.139 = (bf16[2,32,96,384]{3,2,1,0:T(8,128)(2,1)}, bf16[2,32,96,384]{3,2,1,0:T(8,128)(2,1)}, bf16[2,32,96,384]{3,2,1,0:T(8,128)(2,1)}, bf16[2,32,96,384]{3,2,1,0:T(8,128)(2,1)}) custom-call(s32[4]{0:T(128)} %pad_add_fusion.idx, bf16[64,96,384]{2,1,0:T(8,128)(2,1)} %get-tuple-element.143.d0, bf16[64,96,384]{2,1,0:T(8,128)(2,1)} %get-tuple-element.144.d1, ...), custom_call_target="tpu_custom_call" | custom-call | flops 7200000000 | bytes 50000000 | tf_op jit(solution)/shard_map/pallas_call | solution.py:261
  773.8 43.5 %back.4.refs_5_ = bf16[96,128,384]{2,1,0:T(8,128)(2,1)} custom-call(bf16[2,32,96,384]{3,2,1,0:T(8,128)(2,1)} %get-tuple-element.147.refs_0_, bf16[2,32,96,384]{3,2,1,0:T(8,128)(2,1)} %get-tuple-element.148.refs_1_, bf16[2,32,96,384]{3,2,1,0:T(8,128)(2,1)} %collective-permute-done.19.refs_2_, bf16[2,32,96,384]{3,2,1,0:T(8,128)(2,1)} %collective-permute-done.20.refs_3_, ...), custom_call_target="tpu_custom_call" | custom-call | flops 9437184000 | bytes 56623104 | tf_op jit(solution)/shard_map/back/pallas_call | solution.py:413
  817.3 34.2 %head.7 = (bf16[64,96,384]{2,1,0:T(8,128)(2,1)}, bf16[64,96,384]{2,1,0:T(8,128)(2,1)}, bf16[96,128,384]{2,1,0:T(8,128)(2,1)}) custom-call(bf16[2,32,96,384]{3,2,1,0:T(8,128)(2,1)} %get-tuple-element.120.refs_0_, bf16[2,32,96,384]{3,2,1,0:T(8,128)(2,1)} %get-tuple-element.121.refs_1_, bf16[2,32,96,384]{3,2,1,0:T(8,128)(2,1)} %collective-permute-done.10.refs_2_, ...), custom_call_target="tpu_custom_call" | custom-call | flops 3774873600 | bytes 47185920 | tf_op jit(solution)/shard_map/head/pallas_call | solution.py:355
  851.8 59.7 %back.3 = (bf16[96,128,384]{2,1,0:T(8,128)(2,1)}, f32[640,128]{1,0:T(8,128)}, f32[128,128]{1,0:T(8,128)}, f32[128,128]{1,0:T(8,128)}) custom-call(bf16[2,32,96,384]{3,2,1,0:T(8,128)(2,1)} %get-tuple-element.147.refs_0_, bf16[2,32,96,384]{3,2,1,0:T(8,128)(2,1)} %get-tuple-element.148.refs_1_, bf16[2,32,96,384]{3,2,1,0:T(8,128)(2,1)} %collective-permute-done.19.refs_2_, ...), custom_call_target="tpu_custom_call" | custom-call | flops 9437184000 | bytes 56623104 | tf_op jit(solution)/shard_map/back/pallas_call | solution.py:413
  911.6 35.0 %head.6 = (bf16[64,96,384]{2,1,0:T(8,128)(2,1)}, bf16[64,96,384]{2,1,0:T(8,128)(2,1)}, bf16[96,128,384]{2,1,0:T(8,128)(2,1)}, f32[128,128]{1,0:T(8,128)}, f32[128,128]{1,0:T(8,128)}, /*index=5*/f32[128,128]{1,0:T(8,128)}) custom-call(bf16[2,32,96,384]{3,2,1,0:T(8,128)(2,1)} %get-tuple-element.120.refs_0_, ...), custom_call_target="tpu_custom_call" | custom-call | flops 3774873600 | bytes 47185920 | tf_op jit(solution)/shard_map/head/pallas_call | solution.py:355
  963.0 17.5 %shard_map.142 = (bf16[1,32,96,384]{3,2,1,0:T(8,128)(2,1)}, bf16[1,32,96,384]{3,2,1,0:T(8,128)(2,1)}, bf16[1,32,96,384]{3,2,1,0:T(8,128)(2,1)}, bf16[1,32,96,384]{3,2,1,0:T(8,128)(2,1)}) custom-call(s32[4]{0:T(128)} %pad_add_fusion.idx, bf16[64,96,384]{2,1,0:T(8,128)(2,1)} %get-tuple-element.157.d0, bf16[64,96,384]{2,1,0:T(8,128)(2,1)} %get-tuple-element.160.d1, ...), custom_call_target="tpu_custom_call" | custom-call | flops 3600000000 | bytes 50000000 | tf_op jit(solution)/shard_map/pallas_call | solution.py:261
  981.1 17.7 %shard_map.141 = (bf16[1,32,96,384]{3,2,1,0:T(8,128)(2,1)}, bf16[1,32,96,384]{3,2,1,0:T(8,128)(2,1)}, bf16[1,32,96,384]{3,2,1,0:T(8,128)(2,1)}, bf16[1,32,96,384]{3,2,1,0:T(8,128)(2,1)}) custom-call(s32[4]{0:T(128)} %pad_add_fusion.idx, bf16[64,96,384]{2,1,0:T(8,128)(2,1)} %get-tuple-element.157.d0, bf16[64,96,384]{2,1,0:T(8,128)(2,1)} %get-tuple-element.160.d1, ...), custom_call_target="tpu_custom_call" | custom-call | flops 3600000000 | bytes 50000000 | tf_op jit(solution)/shard_map/pallas_call | solution.py:261
  1000.1 7.4 collective-permute-done.35
  1012.9 8.1 collective-permute-done.36
  1022.5 59.9 %back.5 = (bf16[96,384,128]{2,1,0:T(8,128)(2,1)}, f32[640,128]{1,0:T(8,128)}, f32[128,128]{1,0:T(8,128)}, f32[128,128]{1,0:T(8,128)}) custom-call(bf16[1,32,96,384]{3,2,1,0:T(8,128)(2,1)} %get-tuple-element.163.refs_0_, bf16[1,32,96,384]{3,2,1,0:T(8,128)(2,1)} %get-tuple-element.164.refs_1_, bf16[1,32,96,384]{3,2,1,0:T(8,128)(2,1)} %collective-permute-done.25.refs_2_, ...), custom_call_target="tpu_custom_call" | custom-call | flops 9437184000 | bytes 56623104 | tf_op jit(solution)/shard_map/back/pallas_call | solution.py:413
  (227 shorter events, 167.2 us)
Async XLA Ops:
  17.7 244.2 %collective-permute-start.8 = (bf16[96,128,384]{2,1,0:T(8,128)(2,1)}, bf16[96,128,384]{2,1,0:T(8,128)(2,1)}, u32[]{:S(2)}, u32[]{:S(2)}) collective-permute-start(bf16[96,128,384]{2,1,0:T(8,128)(2,1)} %get-tuple-element.103.x_ref.refs_5_.refs_4_), channel_id=1, source_target_pairs={{0,1},{1,0},{2,3},{3,2},{4,5},{5,4},{6,7},{7,6}} | collective-permute-start | bytes 28311560 | tf_op jit(solution)/shard_map/ppermute | solution.py:431
  23.9 71.5 %collective-permute-start.2 = (bf16[32,384,128]{2,1,0:T(8,128)(2,1)S(1)}, bf16[32,384,128]{2,1,0:T(8,128)(2,1)}, u32[]{:S(2)}, u32[]{:S(2)}) collective-permute-start(bf16[32,384,128]{2,1,0:T(8,128)(2,1)S(1)} %get-tuple-element.221), channel_id=1, source_target_pairs={{0,2},{2,0},{1,3},{3,1},{4,6},{6,4},{5,7},{7,5}} | collective-permute-start | bytes 9437192 | tf_op jit(solution)/shard_map/ppermute | solution.py:428
  26.4 136.5 %collective-permute-start.1 = (bf16[32,384,128]{2,1,0:T(8,128)(2,1)}, bf16[32,384,128]{2,1,0:T(8,128)(2,1)}, u32[]{:S(2)}, u32[]{:S(2)}) collective-permute-start(bf16[32,384,128]{2,1,0:T(8,128)(2,1)} %get-tuple-element.222), channel_id=1, source_target_pairs={{0,2},{2,0},{1,3},{3,1},{4,6},{6,4},{5,7},{7,5}} | collective-permute-start | bytes 9437192 | tf_op jit(solution)/shard_map/ppermute | solution.py:428
  26.4 203.7 %collective-permute-start = (bf16[32,384,128]{2,1,0:T(8,128)(2,1)S(1)}, bf16[32,384,128]{2,1,0:T(8,128)(2,1)}, u32[]{:S(2)}, u32[]{:S(2)}) collective-permute-start(bf16[32,384,128]{2,1,0:T(8,128)(2,1)S(1)} %get-tuple-element.223), channel_id=1, source_target_pairs={{0,2},{2,0},{1,3},{3,1},{4,6},{6,4},{5,7},{7,5}} | collective-permute-start | bytes 9437192 | tf_op jit(solution)/shard_map/ppermute | solution.py:428
  102.1 181.6 %collective-permute-start.7 = (bf16[32,128,384]{2,1,0:T(8,128)(2,1)}, bf16[32,128,384]{2,1,0:T(8,128)(2,1)}, u32[]{:S(2)}, u32[]{:S(2)}) collective-permute-start(bf16[32,128,384]{2,1,0:T(8,128)(2,1)} %get-tuple-element.102.x_ref), channel_id=1, source_target_pairs={{0,1},{1,0},{2,3},{3,2},{4,5},{5,4},{6,7},{7,6}} | collective-permute-start | bytes 9437192 | tf_op jit(solution)/shard_map/ppermute | solution.py:431
  169.4 127.9 %collective-permute-start.6 = (bf16[32,128,384]{2,1,0:T(8,128)(2,1)}, bf16[32,128,384]{2,1,0:T(8,128)(2,1)}, u32[]{:S(2)}, u32[]{:S(2)}) collective-permute-start(bf16[32,128,384]{2,1,0:T(8,128)(2,1)} %get-tuple-element.101.x_ref), channel_id=1, source_target_pairs={{0,1},{1,0},{2,3},{3,2},{4,5},{5,4},{6,7},{7,6}} | collective-permute-start | bytes 9437192 | tf_op jit(solution)/shard_map/ppermute | solution.py:431
  236.7 74.4 %collective-permute-start.3 = (bf16[32,128,384]{2,1,0:T(8,128)(2,1)}, bf16[32,128,384]{2,1,0:T(8,128)(2,1)S(1)}, u32[]{:S(2)}, u32[]{:S(2)}) collective-permute-start(bf16[32,128,384]{2,1,0:T(8,128)(2,1)} %get-tuple-element.100.x_ref), channel_id=1, source_target_pairs={{0,1},{1,0},{2,3},{3,2},{4,5},{5,4},{6,7},{7,6}} | collective-permute-start | bytes 9437192 | tf_op jit(solution)/shard_map/ppermute | solution.py:431
  236.7 22.2 %collective-permute-start.4 = (f32[96,384]{1,0:T(8,128)S(1)}, f32[96,384]{1,0:T(8,128)S(1)}, u32[]{:S(2)}, u32[]{:S(2)}) collective-permute-start(f32[96,384]{1,0:T(8,128)S(1)} %convert_element_type.43.m_ref.refs_11_), channel_id=1, source_target_pairs={{0,2},{2,0},{1,3},{3,1},{4,6},{6,4},{5,7},{7,5}} | collective-permute-start | bytes 442376 | tf_op jit(solution)/shard_map/ppermute | solution.py:428
  348.8 8.3 collective-permute-start.11
  349.0 14.7 %collective-permute-start.10 = (bf16[2,32,96,384]{3,2,1,0:T(8,128)(2,1)}, bf16[2,32,96,384]{3,2,1,0:T(8,128)(2,1)}, u32[]{:S(2)}, u32[]{:S(2)}) collective-permute-start(bf16[2,32,96,384]{3,2,1,0:T(8,128)(2,1)} %get-tuple-element.122), channel_id=1, source_target_pairs={{0,1},{1,0},{2,3},{3,2},{4,5},{5,4},{6,7},{7,6}} | collective-permute-start | bytes 14155784 | tf_op jit(solution)/shard_map/ppermute | solution.py:431
  389.8 52.5 %collective-permute-start.13 = (bf16[96,128,384]{2,1,0:T(8,128)(2,1)}, bf16[96,128,384]{2,1,0:T(8,128)(2,1)}, u32[]{:S(2)}, u32[]{:S(2)}) collective-permute-start(bf16[96,128,384]{2,1,0:T(8,128)(2,1)} %get-tuple-element.128.x_ref.refs_4_), channel_id=1, source_target_pairs={{0,1},{1,0},{2,3},{3,2},{4,5},{5,4},{6,7},{7,6}} | collective-permute-start | bytes 28311560 | tf_op jit(solution)/shard_map/ppermute | solution.py:431
  416.5 54.3 %collective-permute-start.12 = (bf16[96,128,384]{2,1,0:T(8,128)(2,1)}, bf16[96,128,384]{2,1,0:T(8,128)(2,1)}, u32[]{:S(2)}, u32[]{:S(2)}) collective-permute-start(bf16[96,128,384]{2,1,0:T(8,128)(2,1)} %get-tuple-element.126.x_ref.refs_4_), channel_id=1, source_target_pairs={{0,1},{1,0},{2,3},{3,2},{4,5},{5,4},{6,7},{7,6}} | collective-permute-start | bytes 28311560 | tf_op jit(solution)/shard_map/ppermute | solution.py:431
  426.9 205.4 %collective-permute-start.16 = (bf16[96,128,384]{2,1,0:T(8,128)(2,1)}, bf16[96,128,384]{2,1,0:T(8,128)(2,1)}, u32[]{:S(2)}, u32[]{:S(2)}) collective-permute-start(bf16[96,128,384]{2,1,0:T(8,128)(2,1)} %turn.1.refs_5_.refs_9_), channel_id=1, source_target_pairs={{0,2},{2,0},{1,3},{3,1},{4,6},{6,4},{5,7},{7,5}} | collective-permute-start | bytes 28311560 | tf_op jit(solution)/shard_map/ppermute | solution.py:428
  500.7 131.6 %collective-permute-start.15 = (bf16[2,32,96,384]{3,2,1,0:T(8,128)(2,1)}, bf16[2,32,96,384]{3,2,1,0:T(8,128)(2,1)}, u32[]{:S(2)}, u32[]{:S(2)}) collective-permute-start(bf16[2,32,96,384]{3,2,1,0:T(8,128)(2,1)} %get-tuple-element.140), channel_id=1, source_target_pairs={{0,1},{1,0},{2,3},{3,2},{4,5},{5,4},{6,7},{7,6}} | collective-permute-start | bytes 14155784 | tf_op jit(solution)/shard_map/ppermute | solution.py:431
  516.4 115.9 %collective-permute-start.14 = (bf16[2,32,96,384]{3,2,1,0:T(8,128)(2,1)}, bf16[2,32,96,384]{3,2,1,0:T(8,128)(2,1)}, u32[]{:S(2)}, u32[]{:S(2)}) collective-permute-start(bf16[2,32,96,384]{3,2,1,0:T(8,128)(2,1)} %get-tuple-element.139), channel_id=1, source_target_pairs={{0,1},{1,0},{2,3},{3,2},{4,5},{5,4},{6,7},{7,6}} | collective-permute-start | bytes 14155784 | tf_op jit(solution)/shard_map/ppermute | solution.py:431
  666.7 38.7 %collective-permute-start.18 = (bf16[64,96,384]{2,1,0:T(8,128)(2,1)}, bf16[64,96,384]{2,1,0:T(8,128)(2,1)}, u32[]{:S(2)}, u32[]{:S(2)}) collective-permute-start(bf16[64,96,384]{2,1,0:T(8,128)(2,1)} %get-tuple-element.146), channel_id=1, source_target_pairs={{0,1},{1,0},{2,3},{3,2},{4,5},{5,4},{6,7},{7,6}} | collective-permute-start | bytes 14155784 | tf_op jit(solution)/shard_map/ppermute | solution.py:431
  704.8 8.4 collective-permute-start.17
  735.6 25.5 %collective-permute-start.20 = (bf16[2,32,96,384]{3,2,1,0:T(8,128)(2,1)}, bf16[2,32,96,384]{3,2,1,0:T(8,128)(2,1)}, u32[]{:S(2)}, u32[]{:S(2)}) collective-permute-start(bf16[2,32,96,384]{3,2,1,0:T(8,128)(2,1)} %get-tuple-element.150), channel_id=1, source_target_pairs={{0,1},{1,0},{2,3},{3,2},{4,5},{5,4},{6,7},{7,6}} | collective-permute-start | bytes 14155784 | tf_op jit(solution)/shard_map/ppermute | solution.py:431
  736.0 25.1 %collective-permute-start.22 = (bf16[2,32,96,384]{3,2,1,0:T(8,128)(2,1)}, bf16[2,32,96,384]{3,2,1,0:T(8,128)(2,1)}, u32[]{:S(2)}, u32[]{:S(2)}) collective-permute-start(bf16[2,32,96,384]{3,2,1,0:T(8,128)(2,1)} %get-tuple-element.154), channel_id=1, source_target_pairs={{0,1},{1,0},{2,3},{3,2},{4,5},{5,4},{6,7},{7,6}} | collective-permute-start | bytes 14155784 | tf_op jit(solution)/shard_map/ppermute | solution.py:431
  758.8 8.3 collective-permute-start.19
  759.1 14.7 %collective-permute-start.21 = (bf16[2,32,96,384]{3,2,1,0:T(8,128)(2,1)}, bf16[2,32,96,384]{3,2,1,0:T(8,128)(2,1)}, u32[]{:S(2)}, u32[]{:S(2)}) collective-permute-start(bf16[2,32,96,384]{3,2,1,0:T(8,128)(2,1)} %get-tuple-element.153), channel_id=1, source_target_pairs={{0,1},{1,0},{2,3},{3,2},{4,5},{5,4},{6,7},{7,6}} | collective-permute-start | bytes 14155784 | tf_op jit(solution)/shard_map/ppermute | solution.py:431
  851.5 111.6 %collective-permute-start.24 = (bf16[64,96,384]{2,1,0:T(8,128)(2,1)}, bf16[64,96,384]{2,1,0:T(8,128)(2,1)}, u32[]{:S(2)}, u32[]{:S(2)}) collective-permute-start(bf16[64,96,384]{2,1,0:T(8,128)(2,1)} %get-tuple-element.162), channel_id=1, source_target_pairs={{0,1},{1,0},{2,3},{3,2},{4,5},{5,4},{6,7},{7,6}} | collective-permute-start | bytes 14155784 | tf_op jit(solution)/shard_map/ppermute | solution.py:431
  946.6 16.4 %collective-permute-start.23 = (bf16[64,96,384]{2,1,0:T(8,128)(2,1)}, bf16[64,96,384]{2,1,0:T(8,128)(2,1)}, u32[]{:S(2)}, u32[]{:S(2)}) collective-permute-start(bf16[64,96,384]{2,1,0:T(8,128)(2,1)} %get-tuple-element.161), channel_id=1, source_target_pairs={{0,1},{1,0},{2,3},{3,2},{4,5},{5,4},{6,7},{7,6}} | collective-permute-start | bytes 14155784 | tf_op jit(solution)/shard_map/ppermute | solution.py:431
  948.3 6.6 collective-permute-start.39
  960.8 38.6 %collective-permute-start.37 = (f32[128,128]{1,0:T(8,128)S(1)}, f32[128,128]{1,0:T(8,128)S(1)}, u32[]{:S(2)}, u32[]{:S(2)}) collective-permute-start(f32[128,128]{1,0:T(8,128)S(1)} %maximum_select_fusion.2), channel_id=1, source_target_pairs={{0,1},{1,0},{2,3},{3,2},{4,5},{5,4},{6,7},{7,6}} | collective-permute-start | bytes 196616 | tf_op jit(solution)/shard_map/ppermute | solution.py:431
  980.5 40.6 %collective-permute-start.26 = (bf16[1,32,96,384]{3,2,1,0:T(8,128)(2,1)}, bf16[1,32,96,384]{3,2,1,0:T(8,128)(2,1)S(1)}, u32[]{:S(2)}, u32[]{:S(2)}) collective-permute-start(bf16[1,32,96,384]{3,2,1,0:T(8,128)(2,1)} %get-tuple-element.166), channel_id=1, source_target_pairs={{0,1},{1,0},{2,3},{3,2},{4,5},{5,4},{6,7},{7,6}} | collective-permute-start | bytes 7077896 | tf_op jit(solution)/shard_map/ppermute | solution.py:431
  981.0 40.1 %collective-permute-start.28 = (bf16[1,32,96,384]{3,2,1,0:T(8,128)(2,1)}, bf16[1,32,96,384]{3,2,1,0:T(8,128)(2,1)}, u32[]{:S(2)}, u32[]{:S(2)}) collective-permute-start(bf16[1,32,96,384]{3,2,1,0:T(8,128)(2,1)} %get-tuple-element.170), channel_id=1, source_target_pairs={{0,1},{1,0},{2,3},{3,2},{4,5},{5,4},{6,7},{7,6}} | collective-permute-start | bytes 7077896 | tf_op jit(solution)/shard_map/ppermute | solution.py:431
  998.8 22.3 %collective-permute-start.25 = (bf16[1,32,96,384]{3,2,1,0:T(8,128)(2,1)}, bf16[1,32,96,384]{3,2,1,0:T(8,128)(2,1)}, u32[]{:S(2)}, u32[]{:S(2)}) collective-permute-start(bf16[1,32,96,384]{3,2,1,0:T(8,128)(2,1)} %get-tuple-element.165), channel_id=1, source_target_pairs={{0,1},{1,0},{2,3},{3,2},{4,5},{5,4},{6,7},{7,6}} | collective-permute-start | bytes 7077896 | tf_op jit(solution)/shard_map/ppermute | solution.py:431
  999.3 21.8 %collective-permute-start.27 = (bf16[1,32,96,384]{3,2,1,0:T(8,128)(2,1)}, bf16[1,32,96,384]{3,2,1,0:T(8,128)(2,1)}, u32[]{:S(2)}, u32[]{:S(2)}) collective-permute-start(bf16[1,32,96,384]{3,2,1,0:T(8,128)(2,1)} %get-tuple-element.169), channel_id=1, source_target_pairs={{0,1},{1,0},{2,3},{3,2},{4,5},{5,4},{6,7},{7,6}} | collective-permute-start | bytes 7077896 | tf_op jit(solution)/shard_map/ppermute | solution.py:431
  999.5 8.0 collective-permute-start.35
  1011.9 9.1 collective-permute-start.36
  1091.9 9.0 collective-permute-start.34
  (31 other events, 459.7 us)

commit v4 on v3

--- a/solution.py
+++ b/solution.py
@@ -76,16 +76,22 @@
 def fill(scr, refs):
     at = 0
     for ref in refs:
-        for c in range(0, ref.shape[0], 16):
-            scr[:, at + c:at + c + 16, :] = jnp.swapaxes(ref[c:c + 16], 0, 1)
+        def move(k, ref=ref, at=at):
+            c = pl.multiple_of(k * 16, 16)
+            scr[:, pl.ds(at + c, 16), :] = jnp.swapaxes(ref[pl.ds(c, 16)], 0, 1)
+
+        rows_loop(move, 1, ref.shape[0] // 16)
         at += ref.shape[0]
 
 
 def flush(scr, refs):
     at = 0
     for ref in refs:
-        for c in range(0, ref.shape[0], 16):
-            ref[c:c + 16] = jnp.swapaxes(scr[:, at + c:at + c + 16, :], 0, 1)
+        def move(k, ref=ref, at=at):
+            c = pl.multiple_of(k * 16, 16)
+            ref[pl.ds(c, 16)] = jnp.swapaxes(scr[:, pl.ds(at + c, 16), :], 0, 1)
+
+        rows_loop(move, 1, ref.shape[0] // 16)
         at += ref.shape[0]
 
 
@@ -288,7 +294,7 @@
     )(*ts, zt, xt, wgt, lnq, wot, ln_next)
 
 
-def head_body(emit_z, emit_w, *refs):
+def head_body(emit_z, emit_w, emit_dg, *refs):
     ts = refs[:2 * NCH]
     refs = list(refs[2 * NCH:])
     x_ref, g_ref, wg_ref, lnq_ref, wot_ref, wo_ref = refs[:6]
@@ -296,8 +302,11 @@
     if emit_z:
         z_ref = refs[k]
         k += 1
-    dt_keep, dt_send, dg_out = refs[k:k + 3]
-    k += 3
+    dt_keep, dt_send = refs[k:k + 2]
+    k += 2
+    if emit_dg:
+        dg_out = refs[k]
+        k += 1
     if emit_z:
         z_out = refs[k]
         k += 1
@@ -315,13 +324,15 @@
 
     def row(i):
         th, rstd = hat(get(st, i).astype(F32))
-        y = affine(th, lnq_ref)
-        upd = dot(wot_ref[...], y)
+        if emit_dg:
+            y = affine(th, lnq_ref)
+            upd = dot(wot_ref[...], y)
         gate = jnp.tanh(dot(wg_ref[...], get(x_ref, i)))
         if emit_z:
             put_turned(z_out, i, (get(z_ref, i).astype(F32) + (gate * upd + upd)).astype(BF16))
         dgate = get(g_ref, i).astype(F32) * (0.5 * gate + 0.5)
-        put(dg_out, i, (dgate * (upd - upd * gate)).astype(BF16))
+        if emit_dg:
+            put(dg_out, i, (dgate * (upd - upd * gate)).astype(BF16))
         du = dgate.astype(BF16)
         dy = dot(wo_ref[...], du).astype(BF16).astype(F32)
         dh = dy * lnq_ref[:, 0:1]
@@ -337,11 +348,11 @@
     flush(sd, [dt_keep, dt_send])
 
 
-def head(k, ts, xt, gt, wgt, lnq, wot, wo, zt=None, emit_w=False):
+def head(k, ts, xt, gt, wgt, lnq, wot, wo, zt=None, emit_w=False, emit_dg=True):
     emit_z = zt is not None
     in_specs = [piece_spec(k, HC)] * (2 * NCH) + [actt_spec(), actt_spec(), const_spec((C, C)), const_spec((C, 2)), const_spec((C, C)), const_spec((C, C))]
-    out_shape = [HALF, HALF, ACTT]
-    out_specs = [half_spec(), half_spec(), actt_spec()]
+    out_shape = [HALF, HALF] + [ACTT] * emit_dg
+    out_specs = [half_spec(), half_spec()] + [actt_spec()] * emit_dg
     extra = ()
     if emit_z:
         in_specs.append(actt_spec())
@@ -353,7 +364,7 @@
             out_shape.append(jax.ShapeDtypeStruct(s, F32))
             out_specs.append(const_spec(s))
     return pl.pallas_call(
-        functools.partial(head_body, emit_z, emit_w), grid=(RB // TI,), in_specs=in_specs,
+        functools.partial(head_body, emit_z, emit_w, emit_dg), grid=(RB // TI,), in_specs=in_specs,
         out_specs=out_specs, out_shape=out_shape, scratch_shapes=[scr(C), scr(C)],
         cost_estimate=cost(NPOS * C * 800, NPOS * C * 10, NPOS * C), name="head",
     )(*ts, xt, gt, wgt, lnq, wot, wo, *extra)
@@ -456,9 +467,12 @@
 
         def products(body, dts, a, b, pieces, n_scr, flops):
             n_out = 4 if dts else 2
-            res = [tri_call(body, blocks, part, dts, (a, b), pieces, n_out, n_scr, flops / NCH) for part in range(NCH)]
+            res, sent = [], []
+            for part in range(NCH):
+                res.append(tri_call(body, blocks, part, dts, (a, b), pieces, n_out, n_scr, flops / NCH))
+                sent.append([d2d(res[-1][j]) for j in range(1, n_out, 2)])
             keeps = [[r[j] for r in res] for j in range(0, n_out, 2)]
-            sends = [[d2d(r[j]) for r in res] for j in range(1, n_out, 2)]
+            sends = [list(v) for v in zip(*sent)]
             return [k + s for k, s in zip(keeps, sends)]
 
         z_parts = []
@@ -501,33 +515,33 @@
 
         dk_own, ds_own, dg1_own, gwo1, gq1g, gq1s = head(0, t1, xt_own, et_own, wgt[0], lnq[0], wot[0], wo[0], None, True)
         dk_part = d2d(ds_own)
-        dk_cross, ds_cross, _ = head(1, t1, xt_cross, et_cross, wgt[0], lnq[0], wot[0], wo[0])
+
+        def vec(gg, gs):
+            return jnp.stack([jnp.sum(gg, axis=1), jnp.sum(gs, axis=1)])
+
+        def common(g):
+            return jnp.concatenate([local(g[:4 * C].reshape(4, C, C), 1).reshape(4 * C, C), g[4 * C:]], axis=0)
+
+        def total(v):
+            w = d2d(v)
+            v = v + w
+            w = ici(v)
+            return v + w
+
+        early = total(jnp.concatenate([common(gw2), local(gwo2, 0), local(gwo1, 0), vec(gp2g, gp2s),
+                                       local(vec(gq2g, gq2s), 1), local(vec(gq1g, gq1s), 1), jnp.zeros((2, C), F32)], axis=0))
+        dk_cross, ds_cross = head(1, t1, xt_cross, et_cross, wgt[0], lnq[0], wot[0], wo[0], None, False, False)
         dk_diag = d2d(ds_cross)
         da1, db1 = products(tri_out_bwd_body, (dk_own, dk_cross, dk_part, dk_diag), a1, b1, 1, 2, 7.2e9)
         d_pair, gw1, gp1g, gp1s = back(0, da1, db1, zt_own, et_own, dg1_own, m_own, ln[0], wt[0], wb[0], True, True)
-
-        def vec(gg, gs):
-            return jnp.stack([jnp.sum(gg, axis=1), jnp.sum(gs, axis=1)])
-
-        def total(*parts):
-            for swap in (d2d, ici):
-                parts = tuple(v + swap(v) for v in parts)
-            return parts
-
-        def sums(gw, gpg, gps, gqg, gqs, gwo):
-            vecs = jnp.concatenate([vec(gpg, gps), local(vec(gqg, gqs), 1)], axis=0)
-            gw, gwo, vecs = total(gw, local(gwo, 0), jnp.concatenate([vecs, jnp.zeros_like(vecs)], axis=0))
-            return vecs[0:2], proj_local(gw), gw[4 * C:].T, vecs[2:4], gwo
-
-        def proj_local(g):
-            return g[:4 * C].T
-
-        def common(g):
-            return jnp.concatenate([local(g[:4 * C].reshape(4, C, C), 1).reshape(4 * C, C), g[4 * C:]], axis=0)
-
-        s2 = sums(common(gw2), gp2g, gp2s, gq2g, gq2s, gwo2)
-        s1 = sums(common(gw1), gp1g, gp1s, gq1g, gq1s, gwo1)
-        return (pair_out, d_pair) + tuple(jnp.stack([p, q]).astype(BF16) for p, q in zip(s1, s2))
+        late = total(jnp.concatenate([common(gw1), vec(gp1g, gp1s), jnp.zeros((6, C), F32)], axis=0))
+        e0, e1, e2 = 5 * C, 6 * C, 7 * C
+        grads = (jnp.stack([late[e0:e0 + 2], early[e2:e2 + 2]]),
+                 jnp.stack([late[:4 * C].T, early[:4 * C].T]),
+                 jnp.stack([late[4 * C:e0].T, early[4 * C:e0].T]),
+                 jnp.stack([early[e2 + 4:e2 + 6], early[e2 + 2:e2 + 4]]),
+                 jnp.stack([early[e1:e2], early[e0:e1]]))
+        return (pair_out, d_pair) + tuple(v.astype(BF16) for v in grads)
 
 
     return jax.shard_map(device_step, mesh=mesh, in_specs=(row_spec, mask_spec, row_spec, full_spec, full_spec, full_spec, full_spec, full_spec), out_specs=(row_spec, row_spec, grad_spec, grad_spec, grad_spec, grad_spec, grad_spec), check_vma=False)

time: 1110 us -> 1100 us (level)
    ppermute x11 -> x7, waiting for transfers between devices: 326 us -> 319 us  [ici(): return lax.ppermute(v, AX, ICI_SWAP)]
    ppermute x30 -> x26, waiting for transfers between devices: 46.1 us -> 42 us  [d2d(): return lax.ppermute(v, AX, D2D_SWAP)]
  transfers between devices with their start and end apart: 41 -> 33, of which waited for: 19 -> 16; matrix products, arithmetic and copies ran while one was open for 3% -> 3% of each run, Pallas kernels for 36% -> 35%
where the time goes in v4:
time: 1100 us; the launch traced here: 1090 us
  Pallas kernels  673 us (61%)
  waiting for transfers between devices  361 us (33%)
  local copies, waits for them, and re-layouts  27.5 us (2%)
  other arithmetic  18 us (2%)
  starting transfers between devices  13.8 us (1%)
    ppermute x7, waiting for transfers between devices, ici(): return lax.ppermute(v, AX, ICI_SWAP)  319 us
    pallas_call x3, Pallas kernels, back(): pl.pallas_call(functools.partial(back_body, n, emit_w, last), grid=(RB //...  165 us
    pallas_call x8, Pallas kernels, tri_call(): pl.pallas_call(body, grid_spec=grid_spec, out_shape=[jax.ShapeDtypeStruct...  141 us
    pallas_call x4, Pallas kernels, head(): pl.pallas_call(functools.partial(head_body, emit_z, emit_w, emit_dg), gri...  140 us
    pallas_call x12, Pallas kernels, prep(): pl.pallas_call(prep_body, grid_spec=grid_spec, out_shape=[out, out], inpu...  130 us
    pallas_call x2, Pallas kernels, finish(): pl.pallas_call(finish_body, grid=(RB // TI,), in_specs=[piece_spec(k, HC)...  52.5 us
    ppermute x26, waiting for transfers between devices, d2d(): return lax.ppermute(v, AX, D2D_SWAP)  42 us
    pallas_call x4, Pallas kernels, norm(): pl.pallas_call(norm_body, grid=(rows // TI,), in_specs=[act_spec(), const...  35.4 us
  transfers between devices with their start and end apart: 33, of which 16 were waited for; matrix products, arithmetic and copies ran while one was open for 3% of the time, Pallas kernels for 35%

profile of v4, /device:TPU:0, one launch (start us, length us, event | category | flops | bytes accessed | tf_op | source)
XLA Modules:
  0.0 1094.5 jit_solution(4881004554056180488)
XLA Ops:
  2.1 15.6 %norm.7 = (bf16[96,128,384]{2,1,0:T(8,128)(2,1)}, bf16[96,128,384]{2,1,0:T(8,128)(2,1)}, bf16[96,128,384]{2,1,0:T(8,128)(2,1)}) custom-call(bf16[96,384,128]{2,1,0:T(8,128)(2,1)} %z_ref.2, f32[128,2]{1,0:T(8,128)} %convert_bitcast_fusion.3.ln_ref.refs_12_), custom_call_target="tpu_custom_call" | custom-call | flops 283115520 | bytes 37748736 | tf_op jit(solution)/shard_map/norm/pallas_call | solution.py:165
  28.4 67.0 %collective-permute-done.2.z_ref = bf16[32,384,128]{2,1,0:T(8,128)(2,1)} collective-permute-done((bf16[32,384,128]{2,1,0:T(8,128)(2,1)S(1)}, bf16[32,384,128]{2,1,0:T(8,128)(2,1)}, u32[]{:S(2)}, u32[]{:S(2)}) %collective-permute-start.2) | collective-permute-done | bytes 3145760 | tf_op jit(solution)/shard_map/ppermute | solution.py:439
  102.1 60.8 %collective-permute-done.1.z_ref = bf16[32,384,128]{2,1,0:T(8,128)(2,1)} collective-permute-done((bf16[32,384,128]{2,1,0:T(8,128)(2,1)}, bf16[32,384,128]{2,1,0:T(8,128)(2,1)}, u32[]{:S(2)}, u32[]{:S(2)}) %collective-permute-start.1) | collective-permute-done | bytes 3145760 | tf_op jit(solution)/shard_map/ppermute | solution.py:439
  169.4 60.7 %collective-permute-done.z_ref = bf16[32,384,128]{2,1,0:T(8,128)(2,1)} collective-permute-done((bf16[32,384,128]{2,1,0:T(8,128)(2,1)S(1)}, bf16[32,384,128]{2,1,0:T(8,128)(2,1)}, u32[]{:S(2)}, u32[]{:S(2)}) %collective-permute-start) | collective-permute-done | bytes 3145760 | tf_op jit(solution)/shard_map/ppermute | solution.py:439
  244.6 14.6 %prep.12 = (bf16[64,384,384]{2,1,0:T(8,128)(2,1)}, bf16[64,384,384]{2,1,0:T(8,128)(2,1)}) custom-call(s32[1]{0:T(128)S(6)} %mul.50.base, bf16[96,128,384]{2,1,0:T(8,128)(2,1)} %get-tuple-element.103.x_ref.refs_5_.refs_4_, f32[96,384]{1,0:T(8,128)} %copy-done, bf16[256,128]{1,0:T(8,128)(2,1)} %bitcast.124), custom_call_target="tpu_custom_call" | custom-call | flops 1887436800 | bytes 18874368 | tf_op jit(solution)/shard_map/prep/pallas_call | solution.py:195
  262.8 14.6 %prep.13 = (bf16[64,384,384]{2,1,0:T(8,128)(2,1)}, bf16[64,384,384]{2,1,0:T(8,128)(2,1)}) custom-call(s32[1]{0:T(128)S(6)} %mul.49.base, bf16[96,128,384]{2,1,0:T(8,128)(2,1)} %collective-permute-done.8.x_ref, f32[96,384]{1,0:T(8,128)} %copy-done.6, bf16[256,128]{1,0:T(8,128)(2,1)} %bitcast.125, ...), custom_call_target="tpu_custom_call", output_to_operand_aliasing={{0}: (4, {}), {1}: (5, {})} | custom-call | flops 1887436800 | bytes 18874368 | tf_op jit(solution)/shard_map/prep/pallas_call | solution.py:195
  320.9 14.5 %shard_map.136 = (bf16[2,32,96,384]{3,2,1,0:T(8,128)(2,1)}, bf16[2,32,96,384]{3,2,1,0:T(8,128)(2,1)}) custom-call(s32[4]{0:T(128)} %pad_add_fusion.idx, bf16[64,384,384]{2,1,0:T(8,128)(2,1)} %get-tuple-element.118.a, bf16[64,384,384]{2,1,0:T(8,128)(2,1)} %get-tuple-element.119.b), custom_call_target="tpu_custom_call" | custom-call | flops 3600000000 | bytes 50000000 | tf_op jit(solution)/shard_map/pallas_call | solution.py:267
  335.4 14.6 %shard_map.135 = (bf16[2,32,96,384]{3,2,1,0:T(8,128)(2,1)}, bf16[2,32,96,384]{3,2,1,0:T(8,128)(2,1)}) custom-call(s32[4]{0:T(128)} %pad_add_fusion.idx, bf16[64,384,384]{2,1,0:T(8,128)(2,1)} %get-tuple-element.118.a, bf16[64,384,384]{2,1,0:T(8,128)(2,1)} %get-tuple-element.119.b), custom_call_target="tpu_custom_call" | custom-call | flops 3600000000 | bytes 50000000 | tf_op jit(solution)/shard_map/pallas_call | solution.py:267
  365.1 26.3 %finish.3 = (bf16[96,128,384]{2,1,0:T(8,128)(2,1)}, bf16[96,128,384]{2,1,0:T(8,128)(2,1)}) custom-call(bf16[2,32,96,384]{3,2,1,0:T(8,128)(2,1)} %get-tuple-element.120.refs_0_, bf16[2,32,96,384]{3,2,1,0:T(8,128)(2,1)} %get-tuple-element.121.refs_1_, bf16[2,32,96,384]{3,2,1,0:T(8,128)(2,1)} %collective-permute-done.10.refs_2_, ...), custom_call_target="tpu_custom_call" | custom-call | flops 2831155200 | bytes 47185920 | tf_op jit(solution)/shard_map/finish/pallas_call | solution.py:289
  391.7 26.2 %finish.2 = (bf16[96,128,384]{2,1,0:T(8,128)(2,1)}, bf16[96,128,384]{2,1,0:T(8,128)(2,1)}) custom-call(bf16[2,32,96,384]{3,2,1,0:T(8,128)(2,1)} %get-tuple-element.120.refs_0_, bf16[2,32,96,384]{3,2,1,0:T(8,128)(2,1)} %get-tuple-element.121.refs_1_, bf16[2,32,96,384]{3,2,1,0:T(8,128)(2,1)} %collective-permute-done.10.refs_2_, ...), custom_call_target="tpu_custom_call" | custom-call | flops 2831155200 | bytes 47185920 | tf_op jit(solution)/shard_map/finish/pallas_call | solution.py:289
  418.1 10.2 turn.1.refs_5_.refs_9_
  429.5 14.6 %prep.20 = (bf16[64,384,384]{2,1,0:T(8,128)(2,1)}, bf16[64,384,384]{2,1,0:T(8,128)(2,1)}) custom-call(s32[1]{0:T(128)S(6)} %mul.50.base, bf16[96,128,384]{2,1,0:T(8,128)(2,1)} %get-tuple-element.128.x_ref.refs_4_, f32[96,384]{1,0:T(8,128)} %copy-done, bf16[256,128]{1,0:T(8,128)(2,1)} %bitcast.132), custom_call_target="tpu_custom_call" | custom-call | flops 1887436800 | bytes 18874368 | tf_op jit(solution)/shard_map/prep/pallas_call | solution.py:195
  444.1 14.6 %prep.21 = (bf16[64,384,384]{2,1,0:T(8,128)(2,1)}, bf16[64,384,384]{2,1,0:T(8,128)(2,1)}) custom-call(s32[1]{0:T(128)S(6)} %mul.49.base, bf16[96,128,384]{2,1,0:T(8,128)(2,1)} %collective-permute-done.13.x_ref, f32[96,384]{1,0:T(8,128)} %copy-done.6, bf16[256,128]{1,0:T(8,128)(2,1)} %bitcast.133, ...), custom_call_target="tpu_custom_call", output_to_operand_aliasing={{0}: (4, {}), {1}: (5, {})} | custom-call | flops 1887436800 | bytes 18874368 | tf_op jit(solution)/shard_map/prep/pallas_call | solution.py:195
  458.7 14.8 %prep.22 = (bf16[64,384,384]{2,1,0:T(8,128)(2,1)}, bf16[64,384,384]{2,1,0:T(8,128)(2,1)}) custom-call(s32[1]{0:T(128)S(6)} %mul.48.base, bf16[96,128,384]{2,1,0:T(8,128)(2,1)} %get-tuple-element.126.x_ref.refs_4_, f32[96,384]{1,0:T(8,128)} %copy-done.3, bf16[256,128]{1,0:T(8,128)(2,1)} %bitcast.134, ...), custom_call_target="tpu_custom_call", output_to_operand_aliasing={{0}: (4, {}), {1}: (5, {})} | custom-call | flops 1887436800 | bytes 18874368 | tf_op jit(solution)/shard_map/prep/pallas_call | solution.py:195
  473.4 14.6 %prep.23 = (bf16[64,384,384]{2,1,0:T(8,128)(2,1)}, bf16[64,384,384]{2,1,0:T(8,128)(2,1)}) custom-call(s32[1]{0:T(128)S(6)} %mul.46.base, bf16[96,128,384]{2,1,0:T(8,128)(2,1)} %collective-permute-done.12.x_ref, f32[96,384]{1,0:T(8,128)} %copy-done.7, bf16[256,128]{1,0:T(8,128)(2,1)} %bitcast.135, ...), custom_call_target="tpu_custom_call", output_to_operand_aliasing={{0}: (4, {}), {1}: (5, {})} | custom-call | flops 1887436800 | bytes 18874368 | tf_op jit(solution)/shard_map/prep/pallas_call | solution.py:195
  488.1 15.7 %shard_map.138 = (bf16[2,32,96,384]{3,2,1,0:T(8,128)(2,1)}, bf16[2,32,96,384]{3,2,1,0:T(8,128)(2,1)}) custom-call(s32[4]{0:T(128)} %pad_add_fusion.idx, bf16[64,384,384]{2,1,0:T(8,128)(2,1)} %get-tuple-element.135.a, bf16[64,384,384]{2,1,0:T(8,128)(2,1)} %get-tuple-element.136.b), custom_call_target="tpu_custom_call" | custom-call | flops 3600000000 | bytes 50000000 | tf_op jit(solution)/shard_map/pallas_call | solution.py:267
  503.8 15.6 %shard_map.137 = (bf16[2,32,96,384]{3,2,1,0:T(8,128)(2,1)}, bf16[2,32,96,384]{3,2,1,0:T(8,128)(2,1)}) custom-call(s32[4]{0:T(128)} %pad_add_fusion.idx, bf16[64,384,384]{2,1,0:T(8,128)(2,1)} %get-tuple-element.135.a, bf16[64,384,384]{2,1,0:T(8,128)(2,1)} %get-tuple-element.136.b), custom_call_target="tpu_custom_call" | custom-call | flops 3600000000 | bytes 50000000 | tf_op jit(solution)/shard_map/pallas_call | solution.py:267
  522.1 111.6 %collective-permute-done.16.refs_5_.refs_9_ = bf16[96,128,384]{2,1,0:T(8,128)(2,1)} collective-permute-done((bf16[96,128,384]{2,1,0:T(8,128)(2,1)}, bf16[96,128,384]{2,1,0:T(8,128)(2,1)}, u32[]{:S(2)}, u32[]{:S(2)}) %collective-permute-start.16) | collective-permute-done | bytes 9437216 | tf_op jit(solution)/shard_map/ppermute | solution.py:439
  633.7 34.8 %head.5 = (bf16[64,96,384]{2,1,0:T(8,128)(2,1)}, bf16[64,96,384]{2,1,0:T(8,128)(2,1)}, bf16[96,128,384]{2,1,0:T(8,128)(2,1)}) custom-call(bf16[2,32,96,384]{3,2,1,0:T(8,128)(2,1)} %get-tuple-element.137.refs_0_, bf16[2,32,96,384]{3,2,1,0:T(8,128)(2,1)} %get-tuple-element.138.refs_1_, bf16[2,32,96,384]{3,2,1,0:T(8,128)(2,1)} %collective-permute-done.14.refs_2_, ...), custom_call_target="tpu_custom_call" | custom-call | flops 3774873600 | bytes 47185920 | tf_op jit(solution)/shard_map/head/pallas_call | solution.py:366
  668.6 38.8 %head.4 = (bf16[64,96,384]{2,1,0:T(8,128)(2,1)}, bf16[64,96,384]{2,1,0:T(8,128)(2,1)}, bf16[96,128,384]{2,1,0:T(8,128)(2,1)}, bf16[96,384,128]{2,1,0:T(8,128)(2,...) custom-call(bf16[2,32,96,384]{3,2,1,0:T(8,128)(2,1)} %get-tuple-element.137.refs_0_, ...), custom_call_target="tpu_custom_call" | custom-call | flops 3774873600 | bytes 47185920 | tf_op jit(solution)/shard_map/head/pallas_call | solution.py:366
  707.9 7.9 collective-permute-done.17.d2
  715.7 22.4 %shard_map.140 = (bf16[2,32,96,384]{3,2,1,0:T(8,128)(2,1)}, bf16[2,32,96,384]{3,2,1,0:T(8,128)(2,1)}, bf16[2,32,96,384]{3,2,1,0:T(8,128)(2,1)}, bf16[2,32,96,384]{3,2,1,0:T(8,128)(2,1)}) custom-call(s32[4]{0:T(128)} %pad_add_fusion.idx, bf16[64,96,384]{2,1,0:T(8,128)(2,1)} %get-tuple-element.143.d0, bf16[64,96,384]{2,1,0:T(8,128)(2,1)} %get-tuple-element.144.d1, ...), custom_call_target="tpu_custom_call" | custom-call | flops 7200000000 | bytes 50000000 | tf_op jit(solution)/shard_map/pallas_call | solution.py:267
  738.7 22.5 %shard_map.139 = (bf16[2,32,96,384]{3,2,1,0:T(8,128)(2,1)}, bf16[2,32,96,384]{3,2,1,0:T(8,128)(2,1)}, bf16[2,32,96,384]{3,2,1,0:T(8,128)(2,1)}, bf16[2,32,96,384]{3,2,1,0:T(8,128)(2,1)}) custom-call(s32[4]{0:T(128)} %pad_add_fusion.idx, bf16[64,96,384]{2,1,0:T(8,128)(2,1)} %get-tuple-element.143.d0, bf16[64,96,384]{2,1,0:T(8,128)(2,1)} %get-tuple-element.144.d1, ...), custom_call_target="tpu_custom_call" | custom-call | flops 7200000000 | bytes 50000000 | tf_op jit(solution)/shard_map/pallas_call | solution.py:267
  776.2 44.0 %back.4.refs_5_ = bf16[96,128,384]{2,1,0:T(8,128)(2,1)} custom-call(bf16[2,32,96,384]{3,2,1,0:T(8,128)(2,1)} %get-tuple-element.147.refs_0_, bf16[2,32,96,384]{3,2,1,0:T(8,128)(2,1)} %get-tuple-element.148.refs_1_, bf16[2,32,96,384]{3,2,1,0:T(8,128)(2,1)} %collective-permute-done.19.refs_2_, bf16[2,32,96,384]{3,2,1,0:T(8,128)(2,1)} %collective-permute-done.20.refs_3_, ...), custom_call_target="tpu_custom_call" | custom-call | flops 9437184000 | bytes 56623104 | tf_op jit(solution)/shard_map/back/pallas_call | solution.py:424
  820.2 30.5 %head.7 = (bf16[64,96,384]{2,1,0:T(8,128)(2,1)}, bf16[64,96,384]{2,1,0:T(8,128)(2,1)}) custom-call(bf16[2,32,96,384]{3,2,1,0:T(8,128)(2,1)} %get-tuple-element.120.refs_0_, bf16[2,32,96,384]{3,2,1,0:T(8,128)(2,1)} %get-tuple-element.121.refs_1_, bf16[2,32,96,384]{3,2,1,0:T(8,128)(2,1)} %collective-permute-done.10.refs_2_, ...), custom_call_target="tpu_custom_call" | custom-call | flops 3774873600 | bytes 47185920 | tf_op jit(solution)/shard_map/head/pallas_call | solution.py:366
  851.0 60.6 %back.3 = (bf16[96,128,384]{2,1,0:T(8,128)(2,1)}, f32[640,128]{1,0:T(8,128)}, f32[128,128]{1,0:T(8,128)}, f32[128,128]{1,0:T(8,128)}) custom-call(bf16[2,32,96,384]{3,2,1,0:T(8,128)(2,1)} %get-tuple-element.147.refs_0_, bf16[2,32,96,384]{3,2,1,0:T(8,128)(2,1)} %get-tuple-element.148.refs_1_, bf16[2,32,96,384]{3,2,1,0:T(8,128)(2,1)} %collective-permute-done.19.refs_2_, ...), custom_call_target="tpu_custom_call" | custom-call | flops 9437184000 | bytes 56623104 | tf_op jit(solution)/shard_map/back/pallas_call | solution.py:424
  911.7 35.5 %head.6 = (bf16[64,96,384]{2,1,0:T(8,128)(2,1)}, bf16[64,96,384]{2,1,0:T(8,128)(2,1)}, bf16[96,128,384]{2,1,0:T(8,128)(2,1)}, f32[128,128]{1,0:T(8,128)}, f32[128,128]{1,0:T(8,128)}, /*index=5*/f32[128,128]{1,0:T(8,128)}) custom-call(bf16[2,32,96,384]{3,2,1,0:T(8,128)(2,1)} %get-tuple-element.120.refs_0_, ...), custom_call_target="tpu_custom_call" | custom-call | flops 3774873600 | bytes 47185920 | tf_op jit(solution)/shard_map/head/pallas_call | solution.py:366
  955.5 17.5 %shard_map.142 = (bf16[1,32,96,384]{3,2,1,0:T(8,128)(2,1)}, bf16[1,32,96,384]{3,2,1,0:T(8,128)(2,1)}, bf16[1,32,96,384]{3,2,1,0:T(8,128)(2,1)}, bf16[1,32,96,384]{3,2,1,0:T(8,128)(2,1)}) custom-call(s32[4]{0:T(128)} %pad_add_fusion.idx, bf16[64,96,384]{2,1,0:T(8,128)(2,1)} %get-tuple-element.157.d0, bf16[64,96,384]{2,1,0:T(8,128)(2,1)} %get-tuple-element.160.d1, ...), custom_call_target="tpu_custom_call" | custom-call | flops 3600000000 | bytes 50000000 | tf_op jit(solution)/shard_map/pallas_call | solution.py:267
  973.6 17.5 %shard_map.141 = (bf16[1,32,96,384]{3,2,1,0:T(8,128)(2,1)}, bf16[1,32,96,384]{3,2,1,0:T(8,128)(2,1)}, bf16[1,32,96,384]{3,2,1,0:T(8,128)(2,1)}, bf16[1,32,96,384]{3,2,1,0:T(8,128)(2,1)}) custom-call(s32[4]{0:T(128)} %pad_add_fusion.idx, bf16[64,96,384]{2,1,0:T(8,128)(2,1)} %get-tuple-element.157.d0, bf16[64,96,384]{2,1,0:T(8,128)(2,1)} %get-tuple-element.160.d1, ...), custom_call_target="tpu_custom_call" | custom-call | flops 3600000000 | bytes 50000000 | tf_op jit(solution)/shard_map/pallas_call | solution.py:267
  1002.5 10.3 collective-permute-done.32
  1015.4 60.4 %back.5 = (bf16[96,384,128]{2,1,0:T(8,128)(2,1)}, f32[640,128]{1,0:T(8,128)}, f32[128,128]{1,0:T(8,128)}, f32[128,128]{1,0:T(8,128)}) custom-call(bf16[1,32,96,384]{3,2,1,0:T(8,128)(2,1)} %get-tuple-element.163.refs_0_, bf16[1,32,96,384]{3,2,1,0:T(8,128)(2,1)} %get-tuple-element.164.refs_1_, bf16[1,32,96,384]{3,2,1,0:T(8,128)(2,1)} %collective-permute-done.25.refs_2_, ...), custom_call_target="tpu_custom_call" | custom-call | flops 9437184000 | bytes 56623104 | tf_op jit(solution)/shard_map/back/pallas_call | solution.py:424
  1083.4 8.8 collective-permute-done.30
  (207 shorter events, 155.1 us)
Async XLA Ops:
  17.7 244.4 %collective-permute-start.8 = (bf16[96,128,384]{2,1,0:T(8,128)(2,1)}, bf16[96,128,384]{2,1,0:T(8,128)(2,1)}, u32[]{:S(2)}, u32[]{:S(2)}) collective-permute-start(bf16[96,128,384]{2,1,0:T(8,128)(2,1)} %get-tuple-element.103.x_ref.refs_5_.refs_4_), channel_id=1, source_target_pairs={{0,1},{1,0},{2,3},{3,2},{4,5},{5,4},{6,7},{7,6}} | collective-permute-start | bytes 28311560 | tf_op jit(solution)/shard_map/ppermute | solution.py:442
  23.9 71.5 %collective-permute-start.2 = (bf16[32,384,128]{2,1,0:T(8,128)(2,1)S(1)}, bf16[32,384,128]{2,1,0:T(8,128)(2,1)}, u32[]{:S(2)}, u32[]{:S(2)}) collective-permute-start(bf16[32,384,128]{2,1,0:T(8,128)(2,1)S(1)} %get-tuple-element.221), channel_id=1, source_target_pairs={{0,2},{2,0},{1,3},{3,1},{4,6},{6,4},{5,7},{7,5}} | collective-permute-start | bytes 9437192 | tf_op jit(solution)/shard_map/ppermute | solution.py:439
  26.4 136.5 %collective-permute-start.1 = (bf16[32,384,128]{2,1,0:T(8,128)(2,1)}, bf16[32,384,128]{2,1,0:T(8,128)(2,1)}, u32[]{:S(2)}, u32[]{:S(2)}) collective-permute-start(bf16[32,384,128]{2,1,0:T(8,128)(2,1)} %get-tuple-element.222), channel_id=1, source_target_pairs={{0,2},{2,0},{1,3},{3,1},{4,6},{6,4},{5,7},{7,5}} | collective-permute-start | bytes 9437192 | tf_op jit(solution)/shard_map/ppermute | solution.py:439
  26.4 203.7 %collective-permute-start = (bf16[32,384,128]{2,1,0:T(8,128)(2,1)S(1)}, bf16[32,384,128]{2,1,0:T(8,128)(2,1)}, u32[]{:S(2)}, u32[]{:S(2)}) collective-permute-start(bf16[32,384,128]{2,1,0:T(8,128)(2,1)S(1)} %get-tuple-element.223), channel_id=1, source_target_pairs={{0,2},{2,0},{1,3},{3,1},{4,6},{6,4},{5,7},{7,5}} | collective-permute-start | bytes 9437192 | tf_op jit(solution)/shard_map/ppermute | solution.py:439
  102.1 182.4 %collective-permute-start.7 = (bf16[32,128,384]{2,1,0:T(8,128)(2,1)}, bf16[32,128,384]{2,1,0:T(8,128)(2,1)}, u32[]{:S(2)}, u32[]{:S(2)}) collective-permute-start(bf16[32,128,384]{2,1,0:T(8,128)(2,1)} %get-tuple-element.102.x_ref), channel_id=1, source_target_pairs={{0,1},{1,0},{2,3},{3,2},{4,5},{5,4},{6,7},{7,6}} | collective-permute-start | bytes 9437192 | tf_op jit(solution)/shard_map/ppermute | solution.py:442
  169.4 128.9 %collective-permute-start.6 = (bf16[32,128,384]{2,1,0:T(8,128)(2,1)}, bf16[32,128,384]{2,1,0:T(8,128)(2,1)}, u32[]{:S(2)}, u32[]{:S(2)}) collective-permute-start(bf16[32,128,384]{2,1,0:T(8,128)(2,1)} %get-tuple-element.101.x_ref), channel_id=1, source_target_pairs={{0,1},{1,0},{2,3},{3,2},{4,5},{5,4},{6,7},{7,6}} | collective-permute-start | bytes 9437192 | tf_op jit(solution)/shard_map/ppermute | solution.py:442
  236.7 75.6 %collective-permute-start.3 = (bf16[32,128,384]{2,1,0:T(8,128)(2,1)}, bf16[32,128,384]{2,1,0:T(8,128)(2,1)S(1)}, u32[]{:S(2)}, u32[]{:S(2)}) collective-permute-start(bf16[32,128,384]{2,1,0:T(8,128)(2,1)} %get-tuple-element.100.x_ref), channel_id=1, source_target_pairs={{0,1},{1,0},{2,3},{3,2},{4,5},{5,4},{6,7},{7,6}} | collective-permute-start | bytes 9437192 | tf_op jit(solution)/shard_map/ppermute | solution.py:442
  236.7 22.4 %collective-permute-start.4 = (f32[96,384]{1,0:T(8,128)S(1)}, f32[96,384]{1,0:T(8,128)S(1)}, u32[]{:S(2)}, u32[]{:S(2)}) collective-permute-start(f32[96,384]{1,0:T(8,128)S(1)} %convert_element_type.43.m_ref.refs_11_), channel_id=1, source_target_pairs={{0,2},{2,0},{1,3},{3,1},{4,6},{6,4},{5,7},{7,5}} | collective-permute-start | bytes 442376 | tf_op jit(solution)/shard_map/ppermute | solution.py:439
  260.6 1.6 collective-permute-start.9
  350.1 8.3 collective-permute-start.11
  350.4 14.7 %collective-permute-start.10 = (bf16[2,32,96,384]{3,2,1,0:T(8,128)(2,1)}, bf16[2,32,96,384]{3,2,1,0:T(8,128)(2,1)}, u32[]{:S(2)}, u32[]{:S(2)}) collective-permute-start(bf16[2,32,96,384]{3,2,1,0:T(8,128)(2,1)} %get-tuple-element.122), channel_id=1, source_target_pairs={{0,1},{1,0},{2,3},{3,2},{4,5},{5,4},{6,7},{7,6}} | collective-permute-start | bytes 14155784 | tf_op jit(solution)/shard_map/ppermute | solution.py:442
  391.4 52.7 %collective-permute-start.13 = (bf16[96,128,384]{2,1,0:T(8,128)(2,1)}, bf16[96,128,384]{2,1,0:T(8,128)(2,1)}, u32[]{:S(2)}, u32[]{:S(2)}) collective-permute-start(bf16[96,128,384]{2,1,0:T(8,128)(2,1)} %get-tuple-element.128.x_ref.refs_4_), channel_id=1, source_target_pairs={{0,1},{1,0},{2,3},{3,2},{4,5},{5,4},{6,7},{7,6}} | collective-permute-start | bytes 28311560 | tf_op jit(solution)/shard_map/ppermute | solution.py:442
  417.9 55.6 %collective-permute-start.12 = (bf16[96,128,384]{2,1,0:T(8,128)(2,1)}, bf16[96,128,384]{2,1,0:T(8,128)(2,1)}, u32[]{:S(2)}, u32[]{:S(2)}) collective-permute-start(bf16[96,128,384]{2,1,0:T(8,128)(2,1)} %get-tuple-element.126.x_ref.refs_4_), channel_id=1, source_target_pairs={{0,1},{1,0},{2,3},{3,2},{4,5},{5,4},{6,7},{7,6}} | collective-permute-start | bytes 28311560 | tf_op jit(solution)/shard_map/ppermute | solution.py:442
  428.3 205.4 %collective-permute-start.16 = (bf16[96,128,384]{2,1,0:T(8,128)(2,1)}, bf16[96,128,384]{2,1,0:T(8,128)(2,1)}, u32[]{:S(2)}, u32[]{:S(2)}) collective-permute-start(bf16[96,128,384]{2,1,0:T(8,128)(2,1)} %turn.1.refs_5_.refs_9_), channel_id=1, source_target_pairs={{0,2},{2,0},{1,3},{3,1},{4,6},{6,4},{5,7},{7,5}} | collective-permute-start | bytes 28311560 | tf_op jit(solution)/shard_map/ppermute | solution.py:439
  503.8 129.9 %collective-permute-start.15 = (bf16[2,32,96,384]{3,2,1,0:T(8,128)(2,1)}, bf16[2,32,96,384]{3,2,1,0:T(8,128)(2,1)}, u32[]{:S(2)}, u32[]{:S(2)}) collective-permute-start(bf16[2,32,96,384]{3,2,1,0:T(8,128)(2,1)} %get-tuple-element.140), channel_id=1, source_target_pairs={{0,1},{1,0},{2,3},{3,2},{4,5},{5,4},{6,7},{7,6}} | collective-permute-start | bytes 14155784 | tf_op jit(solution)/shard_map/ppermute | solution.py:442
  519.5 114.3 %collective-permute-start.14 = (bf16[2,32,96,384]{3,2,1,0:T(8,128)(2,1)}, bf16[2,32,96,384]{3,2,1,0:T(8,128)(2,1)}, u32[]{:S(2)}, u32[]{:S(2)}) collective-permute-start(bf16[2,32,96,384]{3,2,1,0:T(8,128)(2,1)} %get-tuple-element.139), channel_id=1, source_target_pairs={{0,1},{1,0},{2,3},{3,2},{4,5},{5,4},{6,7},{7,6}} | collective-permute-start | bytes 14155784 | tf_op jit(solution)/shard_map/ppermute | solution.py:442
  668.6 39.3 %collective-permute-start.18 = (bf16[64,96,384]{2,1,0:T(8,128)(2,1)}, bf16[64,96,384]{2,1,0:T(8,128)(2,1)}, u32[]{:S(2)}, u32[]{:S(2)}) collective-permute-start(bf16[64,96,384]{2,1,0:T(8,128)(2,1)} %get-tuple-element.146), channel_id=1, source_target_pairs={{0,1},{1,0},{2,3},{3,2},{4,5},{5,4},{6,7},{7,6}} | collective-permute-start | bytes 14155784 | tf_op jit(solution)/shard_map/ppermute | solution.py:442
  707.4 8.4 collective-permute-start.17
  738.2 26.0 %collective-permute-start.20 = (bf16[2,32,96,384]{3,2,1,0:T(8,128)(2,1)}, bf16[2,32,96,384]{3,2,1,0:T(8,128)(2,1)}, u32[]{:S(2)}, u32[]{:S(2)}) collective-permute-start(bf16[2,32,96,384]{3,2,1,0:T(8,128)(2,1)} %get-tuple-element.150), channel_id=1, source_target_pairs={{0,1},{1,0},{2,3},{3,2},{4,5},{5,4},{6,7},{7,6}} | collective-permute-start | bytes 14155784 | tf_op jit(solution)/shard_map/ppermute | solution.py:442
  738.6 25.5 %collective-permute-start.22 = (bf16[2,32,96,384]{3,2,1,0:T(8,128)(2,1)}, bf16[2,32,96,384]{3,2,1,0:T(8,128)(2,1)}, u32[]{:S(2)}, u32[]{:S(2)}) collective-permute-start(bf16[2,32,96,384]{3,2,1,0:T(8,128)(2,1)} %get-tuple-element.154), channel_id=1, source_target_pairs={{0,1},{1,0},{2,3},{3,2},{4,5},{5,4},{6,7},{7,6}} | collective-permute-start | bytes 14155784 | tf_op jit(solution)/shard_map/ppermute | solution.py:442
  761.2 8.3 collective-permute-start.19
  761.6 14.7 %collective-permute-start.21 = (bf16[2,32,96,384]{3,2,1,0:T(8,128)(2,1)}, bf16[2,32,96,384]{3,2,1,0:T(8,128)(2,1)}, u32[]{:S(2)}, u32[]{:S(2)}) collective-permute-start(bf16[2,32,96,384]{3,2,1,0:T(8,128)(2,1)} %get-tuple-element.153), channel_id=1, source_target_pairs={{0,1},{1,0},{2,3},{3,2},{4,5},{5,4},{6,7},{7,6}} | collective-permute-start | bytes 14155784 | tf_op jit(solution)/shard_map/ppermute | solution.py:442
  850.7 99.6 %collective-permute-start.24 = (bf16[64,96,384]{2,1,0:T(8,128)(2,1)}, bf16[64,96,384]{2,1,0:T(8,128)(2,1)}, u32[]{:S(2)}, u32[]{:S(2)}) collective-permute-start(bf16[64,96,384]{2,1,0:T(8,128)(2,1)} %get-tuple-element.162), channel_id=1, source_target_pairs={{0,1},{1,0},{2,3},{3,2},{4,5},{5,4},{6,7},{7,6}} | collective-permute-start | bytes 14155784 | tf_op jit(solution)/shard_map/ppermute | solution.py:442
  947.2 8.3 collective-permute-start.23
  973.0 40.8 %collective-permute-start.26 = (bf16[1,32,96,384]{3,2,1,0:T(8,128)(2,1)}, bf16[1,32,96,384]{3,2,1,0:T(8,128)(2,1)S(1)}, u32[]{:S(2)}, u32[]{:S(2)}) collective-permute-start(bf16[1,32,96,384]{3,2,1,0:T(8,128)(2,1)} %get-tuple-element.166), channel_id=1, source_target_pairs={{0,1},{1,0},{2,3},{3,2},{4,5},{5,4},{6,7},{7,6}} | collective-permute-start | bytes 7077896 | tf_op jit(solution)/shard_map/ppermute | solution.py:442
  973.2 40.7 %collective-permute-start.28 = (bf16[1,32,96,384]{3,2,1,0:T(8,128)(2,1)}, bf16[1,32,96,384]{3,2,1,0:T(8,128)(2,1)}, u32[]{:S(2)}, u32[]{:S(2)}) collective-permute-start(bf16[1,32,96,384]{3,2,1,0:T(8,128)(2,1)} %get-tuple-element.170), channel_id=1, source_target_pairs={{0,1},{1,0},{2,3},{3,2},{4,5},{5,4},{6,7},{7,6}} | collective-permute-start | bytes 7077896 | tf_op jit(solution)/shard_map/ppermute | solution.py:442
  991.1 22.8 %collective-permute-start.25 = (bf16[1,32,96,384]{3,2,1,0:T(8,128)(2,1)}, bf16[1,32,96,384]{3,2,1,0:T(8,128)(2,1)}, u32[]{:S(2)}, u32[]{:S(2)}) collective-permute-start(bf16[1,32,96,384]{3,2,1,0:T(8,128)(2,1)} %get-tuple-element.165), channel_id=1, source_target_pairs={{0,1},{1,0},{2,3},{3,2},{4,5},{5,4},{6,7},{7,6}} | collective-permute-start | bytes 7077896 | tf_op jit(solution)/shard_map/ppermute | solution.py:442
  991.3 22.6 %collective-permute-start.27 = (bf16[1,32,96,384]{3,2,1,0:T(8,128)(2,1)}, bf16[1,32,96,384]{3,2,1,0:T(8,128)(2,1)}, u32[]{:S(2)}, u32[]{:S(2)}) collective-permute-start(bf16[1,32,96,384]{3,2,1,0:T(8,128)(2,1)} %get-tuple-element.169), channel_id=1, source_target_pairs={{0,1},{1,0},{2,3},{3,2},{4,5},{5,4},{6,7},{7,6}} | collective-permute-start | bytes 7077896 | tf_op jit(solution)/shard_map/ppermute | solution.py:442
  995.7 4.2 collective-permute-start.31
  999.9 12.9 %collective-permute-start.32 = (f32[904,128]{1,0:T(8,128)S(1)}, f32[904,128]{1,0:T(8,128)}, u32[]{:S(2)}, u32[]{:S(2)}) collective-permute-start(f32[904,128]{1,0:T(8,128)S(1)} %add.30), channel_id=1, source_target_pairs={{0,2},{2,0},{1,3},{3,1},{4,6},{6,4},{5,7},{7,5}} | collective-permute-start | bytes 1388552 | tf_op jit(solution)/shard_map/ppermute | solution.py:439
  1080.6 1.7 collective-permute-start.29
  1082.3 9.9 collective-permute-start.30
  (25 other events, 400.7 us)

commit v5 on v4

--- a/solution.py
+++ b/solution.py
@@ -18,7 +18,8 @@
 HC = H // NCH
 UNROLL = 2
 G = 2
-ZC = 3
+ZC = 6
+BACK_UNROLL = 4
 ZR = RB // ZC
 F32 = jnp.float32
 BF16 = jnp.bfloat16
@@ -143,7 +144,7 @@
                           cost_estimate=cost(NPOS * C * 40, NPOS * C * 4), name="turn")(z)
 
 
-def norm_body(z_ref, ln_ref, *rest):
+def norm_body(unroll, _, z_ref, ln_ref, *rest):
     zt_ref, xt_ref, xc_ref = rest[-3:]
 
     def row(i):
@@ -154,21 +155,24 @@
         put(xt_ref, i, x)
         put(xc_ref, i, x)
 
-    rows_loop(row)
+    rows_loop(row, unroll)
 
 
 def norm(z, ln, part=0, full=None):
     rows = z.shape[0]
-    off = part * (ZR // TI)
     extra = () if full is None else tuple(full)
-    spec = pl.BlockSpec((TI, C, N), lambda i: (i + off, 0, 0))
-    return pl.pallas_call(norm_body, grid=(rows // TI,), in_specs=[act_spec(), const_spec((C, 2))] + [pl.BlockSpec(memory_space=pl.ANY)] * len(extra),
-                          out_specs=[spec, spec, actt_spec()], out_shape=[ACTT, ACTT, jax.ShapeDtypeStruct((rows, C, N), BF16)],
-                          input_output_aliases={2: 0, 3: 1} if extra else {},
-                          cost_estimate=cost(rows * N * C * 60, rows * N * C * 8), name="norm")(z, ln, *extra)
-
-
-def prep_body(base, x_ref, m_ref, wt_ref, *rest):
+    spec = pl.BlockSpec((TI, C, N), lambda i, p: (i + p[0], 0, 0))
+    grid_spec = pltpu.PrefetchScalarGridSpec(
+        num_scalar_prefetch=1, grid=(rows // TI,),
+        in_specs=[act_spec(), const_spec((C, 2))] + [pl.BlockSpec(memory_space=pl.ANY)] * len(extra),
+        out_specs=[spec, spec, actt_spec()])
+    return pl.pallas_call(functools.partial(norm_body, UNROLL if rows == RB else 1), grid_spec=grid_spec, out_shape=[ACTT, ACTT, jax.ShapeDtypeStruct((rows, C, N), BF16)],
+                          input_output_aliases={3: 0, 4: 1} if extra else {},
+                          cost_estimate=cost(rows * N * C * 60, rows * N * C * 8), name="norm")(
+        jnp.full((1,), part * (ZR // TI), jnp.int32), z, ln, *extra)
+
+
+def prep_body(unroll, base, x_ref, m_ref, wt_ref, *rest):
     a_out, b_out, sa, sb = rest[-4:]
 
     def row(i):
@@ -177,7 +181,7 @@
             lin = p[at:at + H]
             put(out, i, (lin * jnp.tanh(p[at + H:at + 2 * H]) + lin).astype(BF16))
 
-    rows_loop(row)
+    rows_loop(row, unroll)
     flush(sa, [a_out])
     flush(sb, [b_out])
 
@@ -193,7 +197,7 @@
         in_specs=[actt_spec(), mask_spec_(), const_spec((4 * H, C))] + [pl.BlockSpec(memory_space=pl.ANY)] * len(extra),
         out_specs=[spec, spec], scratch_shapes=[scr(H), scr(H)])
     return pl.pallas_call(
-        prep_body, grid_spec=grid_spec, out_shape=[out, out],
+        functools.partial(prep_body, UNROLL if rows == RB else 1), grid_spec=grid_spec, out_shape=[out, out],
         input_output_aliases={4: 0, 5: 1} if extra else {},
         cost_estimate=cost(npos * C * 400, npos * C * 4, npos * C), name="prep",
     )(base, xt, mask, wt, *extra)
@@ -257,9 +261,9 @@
 
 
 def tri_call(body, idx, part, dts, ab, pieces, n_out, n_scr, flops):
-    off = part * (HC // CB)
-    dspec = pl.BlockSpec((CB, RB, N), lambda c, _: (c + off, 0, 0))
-    fspec = pl.BlockSpec((CB, N, N), lambda c, _: (c + off, 0, 0))
+    idx = jnp.concatenate([idx, jnp.full((1,), part * (HC // CB), jnp.int32)])
+    dspec = pl.BlockSpec((CB, RB, N), lambda c, i: (c + i[4], 0, 0))
+    fspec = pl.BlockSpec((CB, N, N), lambda c, i: (c + i[4], 0, 0))
     ospec = pl.BlockSpec((pieces, CB, RB, N), lambda c, _: (0, c, 0, 0))
     grid_spec = pltpu.PrefetchScalarGridSpec(
         num_scalar_prefetch=1, grid=(HC // CB,), in_specs=[dspec] * len(dts) + [fspec] * len(ab),
@@ -268,7 +272,7 @@
                           cost_estimate=cost(flops, 50e6))(idx, *dts, *ab)
 
 
-def finish_body(*refs):
+def finish_body(_, *refs):
     ts = refs[:2 * NCH]
     z_ref, x_ref, wg_ref, lnq_ref, wo_ref, ln_ref, z_out, x_out, st = refs[2 * NCH:]
     fill(st, ts)
@@ -286,12 +290,15 @@
 
 
 def finish(k, ts, zt, xt, wgt, lnq, wot, ln_next):
+    tspec = pl.BlockSpec((None, HC, TI, N), lambda i, p: (p[0], 0, i, 0))
+    grid_spec = pltpu.PrefetchScalarGridSpec(
+        num_scalar_prefetch=1, grid=(RB // TI,),
+        in_specs=[tspec] * (2 * NCH) + [actt_spec(), actt_spec(), const_spec((C, C)), const_spec((C, 2)), const_spec((C, C)), const_spec((C, 2))],
+        out_specs=[actt_spec()] * 2, scratch_shapes=[scr(C)])
     return pl.pallas_call(
-        finish_body, grid=(RB // TI,),
-        in_specs=[piece_spec(k, HC)] * (2 * NCH) + [actt_spec(), actt_spec(), const_spec((C, C)), const_spec((C, 2)), const_spec((C, C)), const_spec((C, 2))],
-        out_specs=[actt_spec()] * 2, out_shape=[ACTT] * 2, scratch_shapes=[scr(C)],
+        finish_body, grid_spec=grid_spec, out_shape=[ACTT] * 2,
         cost_estimate=cost(NPOS * C * 600, NPOS * C * 10, NPOS * C), name="finish",
-    )(*ts, zt, xt, wgt, lnq, wot, ln_next)
+    )(jnp.full((1,), k, jnp.int32), *ts, zt, xt, wgt, lnq, wot, ln_next)
 
 
 def head_body(emit_z, emit_w, emit_dg, *refs):
@@ -410,7 +417,7 @@
             ggain[...] += fold(dx * xh)
             gshift[...] += fold(dx)
 
-    rows_loop(row)
+    rows_loop(row, BACK_UNROLL if emit_w else UNROLL)
 
 
 def back(k, das, dbs, zt, gt, dgt, mask, ln, wt, wb, emit_w, last):
@@ -476,8 +483,9 @@
             return [k + s for k, s in zip(keeps, sends)]
 
         z_parts = []
+        later = lax.optimization_barrier(pair_act)
         for j in range(ZC):
-            z_parts.append(ici(pair_act[j * ZR:(j + 1) * ZR]))
+            z_parts.append(ici((later if j else pair_act)[j * ZR:(j + 1) * ZR]))
         zt_own, xt_own, _ = norm(pair_act, ln[0])
         xt_part = d2d(xt_own)
         gt_own = turn(d_pair_out)

time: 1100 us -> 1100 us (level)
  waiting for transfers between devices: 361 us -> 333 us
  Pallas kernels: 673 us -> 692 us
    pallas_call x18 -> x27, Pallas kernels: 217 us -> 251 us  [the longest x18 151 us: prep(): pl.pallas_call(functools.partial(prep_body, UNROLL if rows == RB else 1),...]
    ppermute x7 -> x10, waiting for transfers between devices: 319 us -> 299 us  [ici(): return lax.ppermute(v, AX, ICI_SWAP)]
    pallas_call x3, Pallas kernels: 165 us -> 150 us  [back(): pl.pallas_call(functools.partial(back_body, n, emit_w, last), grid=(RB //...]
    ppermute x26 -> x29, waiting for transfers between devices: 42 us -> 34.5 us  [d2d(): return lax.ppermute(v, AX, D2D_SWAP)]
  transfers between devices with their start and end apart: 33 -> 39, of which waited for: 16 -> 14; matrix products, arithmetic and copies ran while one was open for 3% -> 3% of each run, Pallas kernels for 35% -> 39%
where the time goes in v5:
time: 1100 us; the launch traced here: 1090 us
  Pallas kernels  692 us (63%)
  waiting for transfers between devices  333 us (30%)
  local copies, waits for them, and re-layouts  30.3 us (3%)
  starting transfers between devices  19.8 us (2%)
  other arithmetic  17.4 us (2%)
    ppermute x10, waiting for transfers between devices, ici(): return lax.ppermute(v, AX, ICI_SWAP)  299 us
    pallas_call x18, Pallas kernels, prep(): pl.pallas_call(functools.partial(prep_body, UNROLL if rows == RB else 1),...  151 us
    pallas_call x3, Pallas kernels, back(): pl.pallas_call(functools.partial(back_body, n, emit_w, last), grid=(RB //...  150 us
    pallas_call x8, Pallas kernels, tri_call(): pl.pallas_call(body, grid_spec=grid_spec, out_shape=[jax.ShapeDtypeStruct...  141 us
    pallas_call x4, Pallas kernels, head(): pl.pallas_call(functools.partial(head_body, emit_z, emit_w, emit_dg), gri...  140 us
    pallas_call x2, Pallas kernels, finish(): pl.pallas_call(finish_body, grid_spec=grid_spec, out_shape=[ACTT] * 2, co...  52.9 us
    pallas_call x7, Pallas kernels, norm(): pl.pallas_call(functools.partial(norm_body, UNROLL if rows == RB else 1),...  47.4 us
    ppermute x29, waiting for transfers between devices, d2d(): return lax.ppermute(v, AX, D2D_SWAP)  34.5 us
  transfers between devices with their start and end apart: 39, of which 14 were waited for; matrix products, arithmetic and copies ran while one was open for 3% of the time, Pallas kernels for 39%

profile of v5, /device:TPU:0, one launch (start us, length us, event | category | flops | bytes accessed | tf_op | source)
XLA Modules:
  0.0 1094.0 jit_solution(10827985702941680752)
XLA Ops:
  2.6 15.6 %norm.13 = (bf16[96,128,384]{2,1,0:T(8,128)(2,1)}, bf16[96,128,384]{2,1,0:T(8,128)(2,1)}, bf16[96,128,384]{2,1,0:T(8,128)(2,1)}) custom-call(s32[1]{0:T(128)} %constant.17.clone.1._, bf16[96,384,128]{2,1,0:T(8,128)(2,1)} %z_ref.2, f32[128,2]{1,0:T(8,128)} %convert_bitcast_fusion.3.ln_ref.refs_12_), custom_call_target="tpu_custom_call" | custom-call | flops 283115520 | bytes 37748736 | tf_op jit(solution)/shard_map/norm/pallas_call | solution.py:169
  30.8 97.9 %collective-permute-done.7.m_ref.refs_11_ = f32[96,384]{1,0:T(8,128)S(1)} collective-permute-done((f32[96,384]{1,0:T(8,128)S(1)}, f32[96,384]{1,0:T(8,128)S(1)}, u32[]{:S(2)}, u32[]{:S(2)}) %collective-permute-start.7) | collective-permute-done | bytes 147488 | tf_op jit(solution)/shard_map/ppermute | solution.py:446
  137.9 28.4 %collective-permute-done.2.z_ref = bf16[16,384,128]{2,1,0:T(8,128)(2,1)} collective-permute-done((bf16[16,384,128]{2,1,0:T(8,128)(2,1)}, bf16[16,384,128]{2,1,0:T(8,128)(2,1)}, u32[]{:S(2)}, u32[]{:S(2)}) %collective-permute-start.2) | collective-permute-done | bytes 1572896 | tf_op jit(solution)/shard_map/ppermute | solution.py:446
  166.3 33.7 %collective-permute-done.1.z_ref = bf16[16,384,128]{2,1,0:T(8,128)(2,1)} collective-permute-done((bf16[16,384,128]{2,1,0:T(8,128)(2,1)}, bf16[16,384,128]{2,1,0:T(8,128)(2,1)}, u32[]{:S(2)}, u32[]{:S(2)}) %collective-permute-start.1) | collective-permute-done | bytes 1572896 | tf_op jit(solution)/shard_map/ppermute | solution.py:446
  221.8 10.9 collective-permute-done.z_ref
  245.0 14.5 %prep.18 = (bf16[64,384,384]{2,1,0:T(8,128)(2,1)}, bf16[64,384,384]{2,1,0:T(8,128)(2,1)}) custom-call(s32[1]{0:T(128)S(6)} %mul.50.base, bf16[96,128,384]{2,1,0:T(8,128)(2,1)} %get-tuple-element.133.x_ref.refs_5_.refs_4_, f32[96,384]{1,0:T(8,128)} %copy-done, bf16[256,128]{1,0:T(8,128)(2,1)} %bitcast.124), custom_call_target="tpu_custom_call" | custom-call | flops 1887436800 | bytes 18874368 | tf_op jit(solution)/shard_map/prep/pallas_call | solution.py:199
  261.7 14.6 %prep.19 = (bf16[64,384,384]{2,1,0:T(8,128)(2,1)}, bf16[64,384,384]{2,1,0:T(8,128)(2,1)}) custom-call(s32[1]{0:T(128)S(6)} %mul.49.base, bf16[96,128,384]{2,1,0:T(8,128)(2,1)} %collective-permute-done.14.x_ref, f32[96,384]{1,0:T(8,128)} %collective-permute-done.15.m_ref, bf16[256,128]{1,0:T(8,128)(2,1)} %bitcast.125, ...), custom_call_target="tpu_custom_call", output_to_operand_aliasing={{0}: (4, {}), {1}: (5, {})} | custom-call | flops 1887436800 | bytes 18874368 | tf_op jit(solution)/shard_map/prep/pallas_call | solution.py:199
  340.5 14.5 %shard_map.136 = (bf16[2,32,96,384]{3,2,1,0:T(8,128)(2,1)}, bf16[2,32,96,384]{3,2,1,0:T(8,128)(2,1)}) custom-call(s32[5]{0:T(128)} %concatenate.84.idx, bf16[64,384,384]{2,1,0:T(8,128)(2,1)} %get-tuple-element.160.a, bf16[64,384,384]{2,1,0:T(8,128)(2,1)} %get-tuple-element.161.b), custom_call_target="tpu_custom_call" | custom-call | flops 3600000000 | bytes 50000000 | tf_op jit(solution)/shard_map/pallas_call | solution.py:271
  355.6 14.5 %shard_map.135 = (bf16[2,32,96,384]{3,2,1,0:T(8,128)(2,1)}, bf16[2,32,96,384]{3,2,1,0:T(8,128)(2,1)}) custom-call(s32[5]{0:T(128)} %concatenate.82.idx, bf16[64,384,384]{2,1,0:T(8,128)(2,1)} %get-tuple-element.160.a, bf16[64,384,384]{2,1,0:T(8,128)(2,1)} %get-tuple-element.161.b), custom_call_target="tpu_custom_call" | custom-call | flops 3600000000 | bytes 50000000 | tf_op jit(solution)/shard_map/pallas_call | solution.py:271
  378.3 26.5 %finish.3 = (bf16[96,128,384]{2,1,0:T(8,128)(2,1)}, bf16[96,128,384]{2,1,0:T(8,128)(2,1)}) custom-call(s32[1]{0:T(128)} %constant.17.clone.1._, bf16[2,32,96,384]{3,2,1,0:T(8,128)(2,1)} %get-tuple-element.162.refs_0_, bf16[2,32,96,384]{3,2,1,0:T(8,128)(2,1)} %get-tuple-element.163.refs_1_, bf16[2,32,96,384]{3,2,1,0:T(8,128)(2,1)} %collective-permute-done.16.refs_2_, ...), custom_call_target="tpu_custom_call" | custom-call | flops 2831155200 | bytes 47185920 | tf_op jit(solution)/shard_map/finish/pallas_call | solution.py:298
  405.0 26.4 %finish.2 = (bf16[96,128,384]{2,1,0:T(8,128)(2,1)}, bf16[96,128,384]{2,1,0:T(8,128)(2,1)}) custom-call(s32[1]{0:T(128)} %constant.2.clone.1._, bf16[2,32,96,384]{3,2,1,0:T(8,128)(2,1)} %get-tuple-element.162.refs_0_, bf16[2,32,96,384]{3,2,1,0:T(8,128)(2,1)} %get-tuple-element.163.refs_1_, bf16[2,32,96,384]{3,2,1,0:T(8,128)(2,1)} %collective-permute-done.16.refs_2_, ...), custom_call_target="tpu_custom_call" | custom-call | flops 2831155200 | bytes 47185920 | tf_op jit(solution)/shard_map/finish/pallas_call | solution.py:298
  431.8 10.6 turn.1.refs_5_.refs_9_
  444.7 14.6 %prep.32 = (bf16[64,384,384]{2,1,0:T(8,128)(2,1)}, bf16[64,384,384]{2,1,0:T(8,128)(2,1)}) custom-call(s32[1]{0:T(128)S(6)} %mul.50.base, bf16[96,128,384]{2,1,0:T(8,128)(2,1)} %get-tuple-element.170.x_ref.refs_4_, f32[96,384]{1,0:T(8,128)} %copy-done, bf16[256,128]{1,0:T(8,128)(2,1)} %bitcast.138), custom_call_target="tpu_custom_call" | custom-call | flops 1887436800 | bytes 18874368 | tf_op jit(solution)/shard_map/prep/pallas_call | solution.py:199
  459.3 14.6 %prep.33 = (bf16[64,384,384]{2,1,0:T(8,128)(2,1)}, bf16[64,384,384]{2,1,0:T(8,128)(2,1)}) custom-call(s32[1]{0:T(128)S(6)} %mul.49.base, bf16[96,128,384]{2,1,0:T(8,128)(2,1)} %collective-permute-done.19.x_ref, f32[96,384]{1,0:T(8,128)} %collective-permute-done.15.m_ref, bf16[256,128]{1,0:T(8,128)(2,1)} %bitcast.139, ...), custom_call_target="tpu_custom_call", output_to_operand_aliasing={{0}: (4, {}), {1}: (5, {})} | custom-call | flops 1887436800 | bytes 18874368 | tf_op jit(solution)/shard_map/prep/pallas_call | solution.py:199
  473.9 14.6 %prep.34 = (bf16[64,384,384]{2,1,0:T(8,128)(2,1)}, bf16[64,384,384]{2,1,0:T(8,128)(2,1)}) custom-call(s32[1]{0:T(128)S(6)} %mul.48.base, bf16[96,128,384]{2,1,0:T(8,128)(2,1)} %get-tuple-element.168.x_ref.refs_4_, f32[96,384]{1,0:T(8,128)} %copy-done.7, bf16[256,128]{1,0:T(8,128)(2,1)} %bitcast.140, ...), custom_call_target="tpu_custom_call", output_to_operand_aliasing={{0}: (4, {}), {1}: (5, {})} | custom-call | flops 1887436800 | bytes 18874368 | tf_op jit(solution)/shard_map/prep/pallas_call | solution.py:199
  488.5 14.6 %prep.35 = (bf16[64,384,384]{2,1,0:T(8,128)(2,1)}, bf16[64,384,384]{2,1,0:T(8,128)(2,1)}) custom-call(s32[1]{0:T(128)S(6)} %mul.46.base, bf16[96,128,384]{2,1,0:T(8,128)(2,1)} %collective-permute-done.18.x_ref, f32[96,384]{1,0:T(8,128)} %collective-permute-done.8.m_ref, bf16[256,128]{1,0:T(8,128)(2,1)} %bitcast.141, ...), custom_call_target="tpu_custom_call", output_to_operand_aliasing={{0}: (4, {}), {1}: (5, {})} | custom-call | flops 1887436800 | bytes 18874368 | tf_op jit(solution)/shard_map/prep/pallas_call | solution.py:199
  503.1 15.7 %shard_map.138 = (bf16[2,32,96,384]{3,2,1,0:T(8,128)(2,1)}, bf16[2,32,96,384]{3,2,1,0:T(8,128)(2,1)}) custom-call(s32[5]{0:T(128)} %concatenate.84.idx, bf16[64,384,384]{2,1,0:T(8,128)(2,1)} %get-tuple-element.177.a, bf16[64,384,384]{2,1,0:T(8,128)(2,1)} %get-tuple-element.178.b), custom_call_target="tpu_custom_call" | custom-call | flops 3600000000 | bytes 50000000 | tf_op jit(solution)/shard_map/pallas_call | solution.py:271
  518.9 15.7 %shard_map.137 = (bf16[2,32,96,384]{3,2,1,0:T(8,128)(2,1)}, bf16[2,32,96,384]{3,2,1,0:T(8,128)(2,1)}) custom-call(s32[5]{0:T(128)} %concatenate.82.idx, bf16[64,384,384]{2,1,0:T(8,128)(2,1)} %get-tuple-element.177.a, bf16[64,384,384]{2,1,0:T(8,128)(2,1)} %get-tuple-element.178.b), custom_call_target="tpu_custom_call" | custom-call | flops 3600000000 | bytes 50000000 | tf_op jit(solution)/shard_map/pallas_call | solution.py:271
  537.3 110.5 %collective-permute-done.22.refs_5_.refs_9_ = bf16[96,128,384]{2,1,0:T(8,128)(2,1)} collective-permute-done((bf16[96,128,384]{2,1,0:T(8,128)(2,1)}, bf16[96,128,384]{2,1,0:T(8,128)(2,1)}, u32[]{:S(2)}, u32[]{:S(2)}) %collective-permute-start.22) | collective-permute-done | bytes 9437216 | tf_op jit(solution)/shard_map/ppermute | solution.py:446
  647.8 34.8 %head.5 = (bf16[64,96,384]{2,1,0:T(8,128)(2,1)}, bf16[64,96,384]{2,1,0:T(8,128)(2,1)}, bf16[96,128,384]{2,1,0:T(8,128)(2,1)}) custom-call(bf16[2,32,96,384]{3,2,1,0:T(8,128)(2,1)} %get-tuple-element.179.refs_0_, bf16[2,32,96,384]{3,2,1,0:T(8,128)(2,1)} %get-tuple-element.180.refs_1_, bf16[2,32,96,384]{3,2,1,0:T(8,128)(2,1)} %collective-permute-done.20.refs_2_, ...), custom_call_target="tpu_custom_call" | custom-call | flops 3774873600 | bytes 47185920 | tf_op jit(solution)/shard_map/head/pallas_call | solution.py:373
  682.7 38.8 %head.4 = (bf16[64,96,384]{2,1,0:T(8,128)(2,1)}, bf16[64,96,384]{2,1,0:T(8,128)(2,1)}, bf16[96,128,384]{2,1,0:T(8,128)(2,1)}, bf16[96,384,128]{2,1,0:T(8,128)(2,...) custom-call(bf16[2,32,96,384]{3,2,1,0:T(8,128)(2,1)} %get-tuple-element.179.refs_0_, ...), custom_call_target="tpu_custom_call" | custom-call | flops 3774873600 | bytes 47185920 | tf_op jit(solution)/shard_map/head/pallas_call | solution.py:373
  729.9 22.5 %shard_map.140 = (bf16[2,32,96,384]{3,2,1,0:T(8,128)(2,1)}, bf16[2,32,96,384]{3,2,1,0:T(8,128)(2,1)}, bf16[2,32,96,384]{3,2,1,0:T(8,128)(2,1)}, bf16[2,32,96,384]{3,2,1,0:T(8,128)(2,1)}) custom-call(s32[5]{0:T(128)} %concatenate.84.idx, bf16[64,96,384]{2,1,0:T(8,128)(2,1)} %get-tuple-element.185.d0, bf16[64,96,384]{2,1,0:T(8,128)(2,1)} %get-tuple-element.186.d1, ...), custom_call_target="tpu_custom_call" | custom-call | flops 7200000000 | bytes 50000000 | tf_op jit(solution)/shard_map/pallas_call | solution.py:271
  752.9 22.7 %shard_map.139 = (bf16[2,32,96,384]{3,2,1,0:T(8,128)(2,1)}, bf16[2,32,96,384]{3,2,1,0:T(8,128)(2,1)}, bf16[2,32,96,384]{3,2,1,0:T(8,128)(2,1)}, bf16[2,32,96,384]{3,2,1,0:T(8,128)(2,1)}) custom-call(s32[5]{0:T(128)} %concatenate.82.idx, bf16[64,96,384]{2,1,0:T(8,128)(2,1)} %get-tuple-element.185.d0, bf16[64,96,384]{2,1,0:T(8,128)(2,1)} %get-tuple-element.186.d1, ...), custom_call_target="tpu_custom_call" | custom-call | flops 7200000000 | bytes 50000000 | tf_op jit(solution)/shard_map/pallas_call | solution.py:271
  790.5 44.0 %back.4.refs_5_ = bf16[96,128,384]{2,1,0:T(8,128)(2,1)} custom-call(bf16[2,32,96,384]{3,2,1,0:T(8,128)(2,1)} %get-tuple-element.189.refs_0_, bf16[2,32,96,384]{3,2,1,0:T(8,128)(2,1)} %get-tuple-element.190.refs_1_, bf16[2,32,96,384]{3,2,1,0:T(8,128)(2,1)} %collective-permute-done.25.refs_2_, bf16[2,32,96,384]{3,2,1,0:T(8,128)(2,1)} %collective-permute-done.26.refs_3_, ...), custom_call_target="tpu_custom_call" | custom-call | flops 9437184000 | bytes 56623104 | tf_op jit(solution)/shard_map/back/pallas_call | solution.py:431
  834.5 30.6 %head.7 = (bf16[64,96,384]{2,1,0:T(8,128)(2,1)}, bf16[64,96,384]{2,1,0:T(8,128)(2,1)}) custom-call(bf16[2,32,96,384]{3,2,1,0:T(8,128)(2,1)} %get-tuple-element.162.refs_0_, bf16[2,32,96,384]{3,2,1,0:T(8,128)(2,1)} %get-tuple-element.163.refs_1_, bf16[2,32,96,384]{3,2,1,0:T(8,128)(2,1)} %collective-permute-done.16.refs_2_, ...), custom_call_target="tpu_custom_call" | custom-call | flops 3774873600 | bytes 47185920 | tf_op jit(solution)/shard_map/head/pallas_call | solution.py:373
  865.4 52.5 %back.3 = (bf16[96,128,384]{2,1,0:T(8,128)(2,1)}, f32[640,128]{1,0:T(8,128)}, f32[128,128]{1,0:T(8,128)}, f32[128,128]{1,0:T(8,128)}) custom-call(bf16[2,32,96,384]{3,2,1,0:T(8,128)(2,1)} %get-tuple-element.189.refs_0_, bf16[2,32,96,384]{3,2,1,0:T(8,128)(2,1)} %get-tuple-element.190.refs_1_, bf16[2,32,96,384]{3,2,1,0:T(8,128)(2,1)} %collective-permute-done.25.refs_2_, ...), custom_call_target="tpu_custom_call" | custom-call | flops 9437184000 | bytes 56623104 | tf_op jit(solution)/shard_map/back/pallas_call | solution.py:431
  918.0 35.5 %head.6 = (bf16[64,96,384]{2,1,0:T(8,128)(2,1)}, bf16[64,96,384]{2,1,0:T(8,128)(2,1)}, bf16[96,128,384]{2,1,0:T(8,128)(2,1)}, f32[128,128]{1,0:T(8,128)}, f32[128,128]{1,0:T(8,128)}, /*index=5*/f32[128,128]{1,0:T(8,128)}) custom-call(bf16[2,32,96,384]{3,2,1,0:T(8,128)(2,1)} %get-tuple-element.162.refs_0_, ...), custom_call_target="tpu_custom_call" | custom-call | flops 3774873600 | bytes 47185920 | tf_op jit(solution)/shard_map/head/pallas_call | solution.py:373
  961.8 17.6 %shard_map.142 = (bf16[1,32,96,384]{3,2,1,0:T(8,128)(2,1)}, bf16[1,32,96,384]{3,2,1,0:T(8,128)(2,1)}, bf16[1,32,96,384]{3,2,1,0:T(8,128)(2,1)}, bf16[1,32,96,384]{3,2,1,0:T(8,128)(2,1)}) custom-call(s32[5]{0:T(128)} %concatenate.84.idx, bf16[64,96,384]{2,1,0:T(8,128)(2,1)} %get-tuple-element.199.d0, bf16[64,96,384]{2,1,0:T(8,128)(2,1)} %get-tuple-element.202.d1, ...), custom_call_target="tpu_custom_call" | custom-call | flops 3600000000 | bytes 50000000 | tf_op jit(solution)/shard_map/pallas_call | solution.py:271
  979.9 17.6 %shard_map.141 = (bf16[1,32,96,384]{3,2,1,0:T(8,128)(2,1)}, bf16[1,32,96,384]{3,2,1,0:T(8,128)(2,1)}, bf16[1,32,96,384]{3,2,1,0:T(8,128)(2,1)}, bf16[1,32,96,384]{3,2,1,0:T(8,128)(2,1)}) custom-call(s32[5]{0:T(128)} %concatenate.82.idx, bf16[64,96,384]{2,1,0:T(8,128)(2,1)} %get-tuple-element.199.d0, bf16[64,96,384]{2,1,0:T(8,128)(2,1)} %get-tuple-element.202.d1, ...), custom_call_target="tpu_custom_call" | custom-call | flops 3600000000 | bytes 50000000 | tf_op jit(solution)/shard_map/pallas_call | solution.py:271
  1010.0 9.3 collective-permute-done.38
  1021.8 53.3 %back.5 = (bf16[96,384,128]{2,1,0:T(8,128)(2,1)}, f32[640,128]{1,0:T(8,128)}, f32[128,128]{1,0:T(8,128)}, f32[128,128]{1,0:T(8,128)}) custom-call(bf16[1,32,96,384]{3,2,1,0:T(8,128)(2,1)} %get-tuple-element.205.refs_0_, bf16[1,32,96,384]{3,2,1,0:T(8,128)(2,1)} %get-tuple-element.206.refs_1_, bf16[1,32,96,384]{3,2,1,0:T(8,128)(2,1)} %collective-permute-done.31.refs_2_, ...), custom_call_target="tpu_custom_call" | custom-call | flops 9437184000 | bytes 56623104 | tf_op jit(solution)/shard_map/back/pallas_call | solution.py:431
  1083.6 7.9 collective-permute-done.36
  (236 shorter events, 196.8 us)
Async XLA Ops:
  18.2 225.5 %collective-permute-start.14 = (bf16[96,128,384]{2,1,0:T(8,128)(2,1)}, bf16[96,128,384]{2,1,0:T(8,128)(2,1)}, u32[]{:S(2)}, u32[]{:S(2)}) collective-permute-start(bf16[96,128,384]{2,1,0:T(8,128)(2,1)} %get-tuple-element.133.x_ref.refs_5_.refs_4_), channel_id=1, source_target_pairs={{0,1},{1,0},{2,3},{3,2},{4,5},{5,4},{6,7},{7,6}} | collective-permute-start | bytes 28311560 | tf_op jit(solution)/shard_map/ppermute | solution.py:449
  20.6 109.9 %collective-permute-start.5 = (bf16[16,384,128]{2,1,0:T(8,128)(2,1)S(1)}, bf16[16,384,128]{2,1,0:T(8,128)(2,1)}, u32[]{:S(2)}, u32[]{:S(2)}) collective-permute-start(bf16[16,384,128]{2,1,0:T(8,128)(2,1)S(1)} %slice.250), channel_id=1, source_target_pairs={{0,2},{2,0},{1,3},{3,1},{4,6},{6,4},{5,7},{7,5}} | collective-permute-start | bytes 4718600 | tf_op jit(solution)/shard_map/ppermute | solution.py:446
  28.7 107.4 %collective-permute-start.4 = (bf16[16,384,128]{2,1,0:T(8,128)(2,1)}, bf16[16,384,128]{2,1,0:T(8,128)(2,1)S(1)}, u32[]{:S(2)}, u32[]{:S(2)}) collective-permute-start(bf16[16,384,128]{2,1,0:T(8,128)(2,1)} %get-tuple-element.263), channel_id=1, source_target_pairs={{0,2},{2,0},{1,3},{3,1},{4,6},{6,4},{5,7},{7,5}} | collective-permute-start | bytes 4718600 | tf_op jit(solution)/shard_map/ppermute | solution.py:446
  28.8 109.1 %collective-permute-start.3 = (bf16[16,384,128]{2,1,0:T(8,128)(2,1)}, bf16[16,384,128]{2,1,0:T(8,128)(2,1)S(1)}, u32[]{:S(2)}, u32[]{:S(2)}) collective-permute-start(bf16[16,384,128]{2,1,0:T(8,128)(2,1)} %get-tuple-element.264), channel_id=1, source_target_pairs={{0,2},{2,0},{1,3},{3,1},{4,6},{6,4},{5,7},{7,5}} | collective-permute-start | bytes 4718600 | tf_op jit(solution)/shard_map/ppermute | solution.py:446
  30.8 98.0 %collective-permute-start.7 = (f32[96,384]{1,0:T(8,128)S(1)}, f32[96,384]{1,0:T(8,128)S(1)}, u32[]{:S(2)}, u32[]{:S(2)}) collective-permute-start(f32[96,384]{1,0:T(8,128)S(1)} %convert_element_type.43.m_ref.refs_11_), channel_id=1, source_target_pairs={{0,2},{2,0},{1,3},{3,1},{4,6},{6,4},{5,7},{7,5}} | collective-permute-start | bytes 442376 | tf_op jit(solution)/shard_map/ppermute | solution.py:446
  128.8 37.6 %collective-permute-start.2 = (bf16[16,384,128]{2,1,0:T(8,128)(2,1)}, bf16[16,384,128]{2,1,0:T(8,128)(2,1)}, u32[]{:S(2)}, u32[]{:S(2)}) collective-permute-start(bf16[16,384,128]{2,1,0:T(8,128)(2,1)} %get-tuple-element.265), channel_id=1, source_target_pairs={{0,2},{2,0},{1,3},{3,1},{4,6},{6,4},{5,7},{7,5}} | collective-permute-start | bytes 4718600 | tf_op jit(solution)/shard_map/ppermute | solution.py:446
  130.5 69.5 %collective-permute-start.1 = (bf16[16,384,128]{2,1,0:T(8,128)(2,1)}, bf16[16,384,128]{2,1,0:T(8,128)(2,1)}, u32[]{:S(2)}, u32[]{:S(2)}) collective-permute-start(bf16[16,384,128]{2,1,0:T(8,128)(2,1)} %get-tuple-element.266), channel_id=1, source_target_pairs={{0,2},{2,0},{1,3},{3,1},{4,6},{6,4},{5,7},{7,5}} | collective-permute-start | bytes 4718600 | tf_op jit(solution)/shard_map/ppermute | solution.py:446
  136.1 96.6 %collective-permute-start = (bf16[16,384,128]{2,1,0:T(8,128)(2,1)}, bf16[16,384,128]{2,1,0:T(8,128)(2,1)}, u32[]{:S(2)}, u32[]{:S(2)}) collective-permute-start(bf16[16,384,128]{2,1,0:T(8,128)(2,1)} %get-tuple-element.267), channel_id=1, source_target_pairs={{0,2},{2,0},{1,3},{3,1},{4,6},{6,4},{5,7},{7,5}} | collective-permute-start | bytes 4718600 | tf_op jit(solution)/shard_map/ppermute | solution.py:446
  137.9 94.9 %collective-permute-start.13 = (bf16[16,128,384]{2,1,0:T(8,128)(2,1)}, bf16[16,128,384]{2,1,0:T(8,128)(2,1)S(1)}, u32[]{:S(2)}, u32[]{:S(2)}) collective-permute-start(bf16[16,128,384]{2,1,0:T(8,128)(2,1)} %get-tuple-element.132.x_ref), channel_id=1, source_target_pairs={{0,1},{1,0},{2,3},{3,2},{4,5},{5,4},{6,7},{7,6}} | collective-permute-start | bytes 4718600 | tf_op jit(solution)/shard_map/ppermute | solution.py:449
  166.3 54.9 %collective-permute-start.15 = (f32[96,384]{1,0:T(8,128)S(1)}, f32[96,384]{1,0:T(8,128)}, u32[]{:S(2)}, u32[]{:S(2)}) collective-permute-start(f32[96,384]{1,0:T(8,128)S(1)} %convert_element_type.43.m_ref.refs_11_), channel_id=1, source_target_pairs={{0,1},{1,0},{2,3},{3,2},{4,5},{5,4},{6,7},{7,6}} | collective-permute-start | bytes 442376 | tf_op jit(solution)/shard_map/ppermute | solution.py:449
  200.0 21.7 %collective-permute-start.8 = (f32[96,384]{1,0:T(8,128)S(1)}, f32[96,384]{1,0:T(8,128)}, u32[]{:S(2)}, u32[]{:S(2)}) collective-permute-start(f32[96,384]{1,0:T(8,128)S(1)} %collective-permute-done.7.m_ref.refs_11_), channel_id=1, source_target_pairs={{0,1},{1,0},{2,3},{3,2},{4,5},{5,4},{6,7},{7,6}} | collective-permute-start | bytes 442376 | tf_op jit(solution)/shard_map/ppermute | solution.py:449
  221.2 70.8 %collective-permute-start.12 = (bf16[16,128,384]{2,1,0:T(8,128)(2,1)}, bf16[16,128,384]{2,1,0:T(8,128)(2,1)}, u32[]{:S(2)}, u32[]{:S(2)}) collective-permute-start(bf16[16,128,384]{2,1,0:T(8,128)(2,1)} %get-tuple-element.131.x_ref), channel_id=1, source_target_pairs={{0,1},{1,0},{2,3},{3,2},{4,5},{5,4},{6,7},{7,6}} | collective-permute-start | bytes 4718600 | tf_op jit(solution)/shard_map/ppermute | solution.py:449
  221.8 80.9 %collective-permute-start.11 = (bf16[16,128,384]{2,1,0:T(8,128)(2,1)}, bf16[16,128,384]{2,1,0:T(8,128)(2,1)}, u32[]{:S(2)}, u32[]{:S(2)}) collective-permute-start(bf16[16,128,384]{2,1,0:T(8,128)(2,1)} %get-tuple-element.130.x_ref), channel_id=1, source_target_pairs={{0,1},{1,0},{2,3},{3,2},{4,5},{5,4},{6,7},{7,6}} | collective-permute-start | bytes 4718600 | tf_op jit(solution)/shard_map/ppermute | solution.py:449
  232.7 80.4 %collective-permute-start.10 = (bf16[16,128,384]{2,1,0:T(8,128)(2,1)S(1)}, bf16[16,128,384]{2,1,0:T(8,128)(2,1)}, u32[]{:S(2)}, u32[]{:S(2)}) collective-permute-start(bf16[16,128,384]{2,1,0:T(8,128)(2,1)S(1)} %copy-done.2), channel_id=1, source_target_pairs={{0,1},{1,0},{2,3},{3,2},{4,5},{5,4},{6,7},{7,6}} | collective-permute-start | bytes 4718600 | tf_op jit(solution)/shard_map/ppermute | solution.py:449
  233.9 89.7 %collective-permute-start.9 = (bf16[16,128,384]{2,1,0:T(8,128)(2,1)}, bf16[16,128,384]{2,1,0:T(8,128)(2,1)S(1)}, u32[]{:S(2)}, u32[]{:S(2)}) collective-permute-start(bf16[16,128,384]{2,1,0:T(8,128)(2,1)} %get-tuple-element.128.x_ref), channel_id=1, source_target_pairs={{0,1},{1,0},{2,3},{3,2},{4,5},{5,4},{6,7},{7,6}} | collective-permute-start | bytes 4718600 | tf_op jit(solution)/shard_map/ppermute | solution.py:449
  243.7 91.6 %collective-permute-start.6 = (bf16[16,128,384]{2,1,0:T(8,128)(2,1)}, bf16[16,128,384]{2,1,0:T(8,128)(2,1)}, u32[]{:S(2)}, u32[]{:S(2)}) collective-permute-start(bf16[16,128,384]{2,1,0:T(8,128)(2,1)} %get-tuple-element.127.x_ref), channel_id=1, source_target_pairs={{0,1},{1,0},{2,3},{3,2},{4,5},{5,4},{6,7},{7,6}} | collective-permute-start | bytes 4718600 | tf_op jit(solution)/shard_map/ppermute | solution.py:449
  355.0 18.9 %collective-permute-start.17 = (bf16[2,32,96,384]{3,2,1,0:T(8,128)(2,1)}, bf16[2,32,96,384]{3,2,1,0:T(8,128)(2,1)}, u32[]{:S(2)}, u32[]{:S(2)}) collective-permute-start(bf16[2,32,96,384]{3,2,1,0:T(8,128)(2,1)} %get-tuple-element.165), channel_id=1, source_target_pairs={{0,1},{1,0},{2,3},{3,2},{4,5},{5,4},{6,7},{7,6}} | collective-permute-start | bytes 14155784 | tf_op jit(solution)/shard_map/ppermute | solution.py:449
  404.8 54.5 %collective-permute-start.19 = (bf16[96,128,384]{2,1,0:T(8,128)(2,1)}, bf16[96,128,384]{2,1,0:T(8,128)(2,1)}, u32[]{:S(2)}, u32[]{:S(2)}) collective-permute-start(bf16[96,128,384]{2,1,0:T(8,128)(2,1)} %get-tuple-element.170.x_ref.refs_4_), channel_id=1, source_target_pairs={{0,1},{1,0},{2,3},{3,2},{4,5},{5,4},{6,7},{7,6}} | collective-permute-start | bytes 28311560 | tf_op jit(solution)/shard_map/ppermute | solution.py:449
  431.5 57.1 %collective-permute-start.18 = (bf16[96,128,384]{2,1,0:T(8,128)(2,1)}, bf16[96,128,384]{2,1,0:T(8,128)(2,1)}, u32[]{:S(2)}, u32[]{:S(2)}) collective-permute-start(bf16[96,128,384]{2,1,0:T(8,128)(2,1)} %get-tuple-element.168.x_ref.refs_4_), channel_id=1, source_target_pairs={{0,1},{1,0},{2,3},{3,2},{4,5},{5,4},{6,7},{7,6}} | collective-permute-start | bytes 28311560 | tf_op jit(solution)/shard_map/ppermute | solution.py:449
  442.4 205.4 %collective-permute-start.22 = (bf16[96,128,384]{2,1,0:T(8,128)(2,1)}, bf16[96,128,384]{2,1,0:T(8,128)(2,1)}, u32[]{:S(2)}, u32[]{:S(2)}) collective-permute-start(bf16[96,128,384]{2,1,0:T(8,128)(2,1)} %turn.1.refs_5_.refs_9_), channel_id=1, source_target_pairs={{0,2},{2,0},{1,3},{3,1},{4,6},{6,4},{5,7},{7,5}} | collective-permute-start | bytes 28311560 | tf_op jit(solution)/shard_map/ppermute | solution.py:446
  518.9 128.9 %collective-permute-start.21 = (bf16[2,32,96,384]{3,2,1,0:T(8,128)(2,1)}, bf16[2,32,96,384]{3,2,1,0:T(8,128)(2,1)}, u32[]{:S(2)}, u32[]{:S(2)}) collective-permute-start(bf16[2,32,96,384]{3,2,1,0:T(8,128)(2,1)} %get-tuple-element.182), channel_id=1, source_target_pairs={{0,1},{1,0},{2,3},{3,2},{4,5},{5,4},{6,7},{7,6}} | collective-permute-start | bytes 14155784 | tf_op jit(solution)/shard_map/ppermute | solution.py:449
  534.6 113.2 %collective-permute-start.20 = (bf16[2,32,96,384]{3,2,1,0:T(8,128)(2,1)}, bf16[2,32,96,384]{3,2,1,0:T(8,128)(2,1)}, u32[]{:S(2)}, u32[]{:S(2)}) collective-permute-start(bf16[2,32,96,384]{3,2,1,0:T(8,128)(2,1)} %get-tuple-element.181), channel_id=1, source_target_pairs={{0,1},{1,0},{2,3},{3,2},{4,5},{5,4},{6,7},{7,6}} | collective-permute-start | bytes 14155784 | tf_op jit(solution)/shard_map/ppermute | solution.py:449
  682.6 39.3 %collective-permute-start.24 = (bf16[64,96,384]{2,1,0:T(8,128)(2,1)}, bf16[64,96,384]{2,1,0:T(8,128)(2,1)}, u32[]{:S(2)}, u32[]{:S(2)}) collective-permute-start(bf16[64,96,384]{2,1,0:T(8,128)(2,1)} %get-tuple-element.188), channel_id=1, source_target_pairs={{0,1},{1,0},{2,3},{3,2},{4,5},{5,4},{6,7},{7,6}} | collective-permute-start | bytes 14155784 | tf_op jit(solution)/shard_map/ppermute | solution.py:449
  752.4 26.1 %collective-permute-start.26 = (bf16[2,32,96,384]{3,2,1,0:T(8,128)(2,1)}, bf16[2,32,96,384]{3,2,1,0:T(8,128)(2,1)}, u32[]{:S(2)}, u32[]{:S(2)}) collective-permute-start(bf16[2,32,96,384]{3,2,1,0:T(8,128)(2,1)} %get-tuple-element.192), channel_id=1, source_target_pairs={{0,1},{1,0},{2,3},{3,2},{4,5},{5,4},{6,7},{7,6}} | collective-permute-start | bytes 14155784 | tf_op jit(solution)/shard_map/ppermute | solution.py:449
  752.8 25.7 %collective-permute-start.28 = (bf16[2,32,96,384]{3,2,1,0:T(8,128)(2,1)}, bf16[2,32,96,384]{3,2,1,0:T(8,128)(2,1)}, u32[]{:S(2)}, u32[]{:S(2)}) collective-permute-start(bf16[2,32,96,384]{3,2,1,0:T(8,128)(2,1)} %get-tuple-element.196), channel_id=1, source_target_pairs={{0,1},{1,0},{2,3},{3,2},{4,5},{5,4},{6,7},{7,6}} | collective-permute-start | bytes 14155784 | tf_op jit(solution)/shard_map/ppermute | solution.py:449
  775.8 14.7 %collective-permute-start.27 = (bf16[2,32,96,384]{3,2,1,0:T(8,128)(2,1)}, bf16[2,32,96,384]{3,2,1,0:T(8,128)(2,1)}, u32[]{:S(2)}, u32[]{:S(2)}) collective-permute-start(bf16[2,32,96,384]{3,2,1,0:T(8,128)(2,1)} %get-tuple-element.195), channel_id=1, source_target_pairs={{0,1},{1,0},{2,3},{3,2},{4,5},{5,4},{6,7},{7,6}} | collective-permute-start | bytes 14155784 | tf_op jit(solution)/shard_map/ppermute | solution.py:449
  865.1 91.5 %collective-permute-start.30 = (bf16[64,96,384]{2,1,0:T(8,128)(2,1)}, bf16[64,96,384]{2,1,0:T(8,128)(2,1)}, u32[]{:S(2)}, u32[]{:S(2)}) collective-permute-start(bf16[64,96,384]{2,1,0:T(8,128)(2,1)} %get-tuple-element.204), channel_id=1, source_target_pairs={{0,1},{1,0},{2,3},{3,2},{4,5},{5,4},{6,7},{7,6}} | collective-permute-start | bytes 14155784 | tf_op jit(solution)/shard_map/ppermute | solution.py:449
  979.4 41.0 %collective-permute-start.32 = (bf16[1,32,96,384]{3,2,1,0:T(8,128)(2,1)}, bf16[1,32,96,384]{3,2,1,0:T(8,128)(2,1)S(1)}, u32[]{:S(2)}, u32[]{:S(2)}) collective-permute-start(bf16[1,32,96,384]{3,2,1,0:T(8,128)(2,1)} %get-tuple-element.208), channel_id=1, source_target_pairs={{0,1},{1,0},{2,3},{3,2},{4,5},{5,4},{6,7},{7,6}} | collective-permute-start | bytes 7077896 | tf_op jit(solution)/shard_map/ppermute | solution.py:449
  979.7 40.7 %collective-permute-start.34 = (bf16[1,32,96,384]{3,2,1,0:T(8,128)(2,1)}, bf16[1,32,96,384]{3,2,1,0:T(8,128)(2,1)}, u32[]{:S(2)}, u32[]{:S(2)}) collective-permute-start(bf16[1,32,96,384]{3,2,1,0:T(8,128)(2,1)} %get-tuple-element.212), channel_id=1, source_target_pairs={{0,1},{1,0},{2,3},{3,2},{4,5},{5,4},{6,7},{7,6}} | collective-permute-start | bytes 7077896 | tf_op jit(solution)/shard_map/ppermute | solution.py:449
  997.5 22.9 %collective-permute-start.31 = (bf16[1,32,96,384]{3,2,1,0:T(8,128)(2,1)}, bf16[1,32,96,384]{3,2,1,0:T(8,128)(2,1)}, u32[]{:S(2)}, u32[]{:S(2)}) collective-permute-start(bf16[1,32,96,384]{3,2,1,0:T(8,128)(2,1)} %get-tuple-element.207), channel_id=1, source_target_pairs={{0,1},{1,0},{2,3},{3,2},{4,5},{5,4},{6,7},{7,6}} | collective-permute-start | bytes 7077896 | tf_op jit(solution)/shard_map/ppermute | solution.py:449
  997.8 22.6 %collective-permute-start.33 = (bf16[1,32,96,384]{3,2,1,0:T(8,128)(2,1)}, bf16[1,32,96,384]{3,2,1,0:T(8,128)(2,1)}, u32[]{:S(2)}, u32[]{:S(2)}) collective-permute-start(bf16[1,32,96,384]{3,2,1,0:T(8,128)(2,1)} %get-tuple-element.211), channel_id=1, source_target_pairs={{0,1},{1,0},{2,3},{3,2},{4,5},{5,4},{6,7},{7,6}} | collective-permute-start | bytes 7077896 | tf_op jit(solution)/shard_map/ppermute | solution.py:449
  1006.4 12.9 %collective-permute-start.38 = (f32[904,128]{1,0:T(8,128)S(1)}, f32[904,128]{1,0:T(8,128)}, u32[]{:S(2)}, u32[]{:S(2)}) collective-permute-start(f32[904,128]{1,0:T(8,128)S(1)} %add.54), channel_id=1, source_target_pairs={{0,2},{2,0},{1,3},{3,1},{4,6},{6,4},{5,7},{7,5}} | collective-permute-start | bytes 1388552 | tf_op jit(solution)/shard_map/ppermute | solution.py:446
  (34 other events, 835.0 us)

commit v6 on v5

--- a/solution.py
+++ b/solution.py
@@ -136,7 +136,7 @@
 
 
 def turn_body(z_ref, zt_ref):
-    rows_loop(lambda i: put(zt_ref, i, jnp.concatenate([z_ref[G * i + r].T for r in range(G)], axis=1)))
+    rows_loop(lambda i: put(zt_ref, i, jnp.concatenate([z_ref[G * i + r].T for r in range(G)], axis=1)), 1)
 
 
 def turn(z):
@@ -166,7 +166,7 @@
         num_scalar_prefetch=1, grid=(rows // TI,),
         in_specs=[act_spec(), const_spec((C, 2))] + [pl.BlockSpec(memory_space=pl.ANY)] * len(extra),
         out_specs=[spec, spec, actt_spec()])
-    return pl.pallas_call(functools.partial(norm_body, UNROLL if rows == RB else 1), grid_spec=grid_spec, out_shape=[ACTT, ACTT, jax.ShapeDtypeStruct((rows, C, N), BF16)],
+    return pl.pallas_call(functools.partial(norm_body, 1), grid_spec=grid_spec, out_shape=[ACTT, ACTT, jax.ShapeDtypeStruct((rows, C, N), BF16)],
                           input_output_aliases={3: 0, 4: 1} if extra else {},
                           cost_estimate=cost(rows * N * C * 60, rows * N * C * 8), name="norm")(
         jnp.full((1,), part * (ZR // TI), jnp.int32), z, ln, *extra)
@@ -186,7 +186,7 @@
     flush(sb, [b_out])
 
 
-def prep(base, xt, mask, wt, full=None):
+def prep(base, xt, mask, wt, full=None, unroll=UNROLL):
     rows = xt.shape[0]
     npos = rows * N
     out = jax.ShapeDtypeStruct((H, N, N), BF16)
@@ -197,7 +197,7 @@
         in_specs=[actt_spec(), mask_spec_(), const_spec((4 * H, C))] + [pl.BlockSpec(memory_space=pl.ANY)] * len(extra),
         out_specs=[spec, spec], scratch_shapes=[scr(H), scr(H)])
     return pl.pallas_call(
-        functools.partial(prep_body, UNROLL if rows == RB else 1), grid_spec=grid_spec, out_shape=[out, out],
+        functools.partial(prep_body, unroll if rows == RB else 1), grid_spec=grid_spec, out_shape=[out, out],
         input_output_aliases={4: 0, 5: 1} if extra else {},
         cost_estimate=cost(npos * C * 400, npos * C * 4, npos * C), name="prep",
     )(base, xt, mask, wt, *extra)
@@ -219,7 +219,7 @@
         lhs = jnp.concatenate(block_rows(idx, a, c), axis=0)
         emit(dot(lhs, b[c], 1, 1).astype(BF16), keep, send, c)
 
-    rows_loop(chan, 2, CB)
+    rows_loop(chan, 1, CB)
 
 
 def tri_in_body(idx, a, b, keep, send, s):
@@ -228,7 +228,7 @@
         lhs = jnp.concatenate(block_rows(idx, s, c), axis=0)
         emit(dot(lhs, b[c]).astype(BF16), keep, send, c)
 
-    rows_loop(chan, 2, CB)
+    rows_loop(chan, 1, CB)
 
 
 def gather_dt(idx, parts, c, s):
@@ -242,7 +242,7 @@
         emit(dot(jnp.concatenate(block_rows(idx, b, c), axis=0), s[c], 1, 1).astype(BF16), dak, das, c)
         emit(dot(jnp.concatenate(block_rows(idx, a, c), axis=0), s[c]).astype(BF16), dbk, dbs, c)
 
-    rows_loop(chan, 2, CB)
+    rows_loop(chan, 1, CB)
 
 
 def tri_out_bwd_body(idx, d0, d1, d2, d3, a, b, dak, das, dbk, dbs, s, st):
@@ -257,7 +257,7 @@
         dbk[0, c] = db[:RB]
         dbs[0, c] = db[RB:]
 
-    rows_loop(chan, 2, CB)
+    rows_loop(chan, 1, CB)
 
 
 def tri_call(body, idx, part, dts, ab, pieces, n_out, n_scr, flops):
@@ -490,8 +490,8 @@
         xt_part = d2d(xt_own)
         gt_own = turn(d_pair_out)
         gt_cross = ici(gt_own)
-        ab1 = prep(base[0], xt_own, m_own, wt_half[0])
-        ab1 = prep(base[2], xt_part, m_part, wt_half[0], ab1)
+        ab1 = prep(base[0], xt_own, m_own, wt_half[0], None, 1)
+        ab1 = prep(base[2], xt_part, m_part, wt_half[0], ab1, 1)
         full = None
         for j in range(ZC):
             zt_cross, xt_cross, xc = norm(z_parts[j], ln[0], j, full)

time: 1100 us -> 1120 us (1.018)
  Pallas kernels: 692 us -> 720 us
    pallas_call x8, Pallas kernels: 141 us -> 160 us  [tri_call(): pl.pallas_call(body, grid_spec=grid_spec, out_shape=[jax.ShapeDtypeStruct...]
  transfers between devices with their start and end apart: 39 -> 39, of which waited for: 14 -> 14; matrix products, arithmetic and copies ran while one was open for 3% -> 3% of each run, Pallas kernels for 39% -> 40%
where the time goes in v6:
time: 1120 us; the launch traced here: 1110 us
  Pallas kernels  720 us (64%)
  waiting for transfers between devices  326 us (29%)
  local copies, waits for them, and re-layouts  30.3 us (3%)
  starting transfers between devices  19.6 us (2%)
  other arithmetic  17.4 us (2%)
    ppermute x10, waiting for transfers between devices, ici(): return lax.ppermute(v, AX, ICI_SWAP)  291 us
    pallas_call x8, Pallas kernels, tri_call(): pl.pallas_call(body, grid_spec=grid_spec, out_shape=[jax.ShapeDtypeStruct...  160 us
    pallas_call x18, Pallas kernels, prep(): pl.pallas_call(functools.partial(prep_body, unroll if rows == RB else 1),...  159 us
    pallas_call x3, Pallas kernels, back(): pl.pallas_call(functools.partial(back_body, n, emit_w, last), grid=(RB //...  150 us
    pallas_call x4, Pallas kernels, head(): pl.pallas_call(functools.partial(head_body, emit_z, emit_w, emit_dg), gri...  140 us
    pallas_call x2, Pallas kernels, finish(): pl.pallas_call(finish_body, grid_spec=grid_spec, out_shape=[ACTT] * 2, co...  52.9 us
    pallas_call x7, Pallas kernels, norm(): pl.pallas_call(functools.partial(norm_body, 1), grid_spec=grid_spec, out_...  48.1 us
    ppermute x29, waiting for transfers between devices, d2d(): return lax.ppermute(v, AX, D2D_SWAP)  34.9 us
  transfers between devices with their start and end apart: 39, of which 14 were waited for; matrix products, arithmetic and copies ran while one was open for 3% of the time, Pallas kernels for 40%

profile of v6, /device:TPU:0, one launch (start us, length us, event | category | flops | bytes accessed | tf_op | source)
XLA Modules:
  0.0 1114.0 jit_solution(17144830445656562435)
XLA Ops:
  2.6 16.4 %norm.13 = (bf16[96,128,384]{2,1,0:T(8,128)(2,1)}, bf16[96,128,384]{2,1,0:T(8,128)(2,1)}, bf16[96,128,384]{2,1,0:T(8,128)(2,1)}) custom-call(s32[1]{0:T(128)} %constant.17.clone.1._, bf16[96,384,128]{2,1,0:T(8,128)(2,1)} %z_ref.2, f32[128,2]{1,0:T(8,128)} %convert_bitcast_fusion.3.ln_ref.refs_12_), custom_call_target="tpu_custom_call" | custom-call | flops 283115520 | bytes 37748736 | tf_op jit(solution)/shard_map/norm/pallas_call | solution.py:169
  31.6 97.9 %collective-permute-done.7.m_ref.refs_11_ = f32[96,384]{1,0:T(8,128)S(1)} collective-permute-done((f32[96,384]{1,0:T(8,128)S(1)}, f32[96,384]{1,0:T(8,128)S(1)}, u32[]{:S(2)}, u32[]{:S(2)}) %collective-permute-start.7) | collective-permute-done | bytes 147488 | tf_op jit(solution)/shard_map/ppermute | solution.py:446
  138.6 28.4 %collective-permute-done.2.z_ref = bf16[16,384,128]{2,1,0:T(8,128)(2,1)} collective-permute-done((bf16[16,384,128]{2,1,0:T(8,128)(2,1)}, bf16[16,384,128]{2,1,0:T(8,128)(2,1)}, u32[]{:S(2)}, u32[]{:S(2)}) %collective-permute-start.2) | collective-permute-done | bytes 1572896 | tf_op jit(solution)/shard_map/ppermute | solution.py:446
  167.1 33.7 %collective-permute-done.1.z_ref = bf16[16,384,128]{2,1,0:T(8,128)(2,1)} collective-permute-done((bf16[16,384,128]{2,1,0:T(8,128)(2,1)}, bf16[16,384,128]{2,1,0:T(8,128)(2,1)}, u32[]{:S(2)}, u32[]{:S(2)}) %collective-permute-start.1) | collective-permute-done | bytes 1572896 | tf_op jit(solution)/shard_map/ppermute | solution.py:446
  222.5 10.9 collective-permute-done.z_ref
  245.7 18.5 %prep.18 = (bf16[64,384,384]{2,1,0:T(8,128)(2,1)}, bf16[64,384,384]{2,1,0:T(8,128)(2,1)}) custom-call(s32[1]{0:T(128)S(6)} %mul.50.base, bf16[96,128,384]{2,1,0:T(8,128)(2,1)} %get-tuple-element.133.x_ref.refs_5_.refs_4_, f32[96,384]{1,0:T(8,128)} %copy-done, bf16[256,128]{1,0:T(8,128)(2,1)} %bitcast.124), custom_call_target="tpu_custom_call" | custom-call | flops 1887436800 | bytes 18874368 | tf_op jit(solution)/shard_map/prep/pallas_call | solution.py:199
  266.4 18.6 %prep.19 = (bf16[64,384,384]{2,1,0:T(8,128)(2,1)}, bf16[64,384,384]{2,1,0:T(8,128)(2,1)}) custom-call(s32[1]{0:T(128)S(6)} %mul.49.base, bf16[96,128,384]{2,1,0:T(8,128)(2,1)} %collective-permute-done.14.x_ref, f32[96,384]{1,0:T(8,128)} %collective-permute-done.15.m_ref, bf16[256,128]{1,0:T(8,128)(2,1)} %bitcast.125, ...), custom_call_target="tpu_custom_call", output_to_operand_aliasing={{0}: (4, {}), {1}: (5, {})} | custom-call | flops 1887436800 | bytes 18874368 | tf_op jit(solution)/shard_map/prep/pallas_call | solution.py:199
  349.1 16.3 %shard_map.136 = (bf16[2,32,96,384]{3,2,1,0:T(8,128)(2,1)}, bf16[2,32,96,384]{3,2,1,0:T(8,128)(2,1)}) custom-call(s32[5]{0:T(128)} %concatenate.84.idx, bf16[64,384,384]{2,1,0:T(8,128)(2,1)} %get-tuple-element.160.a, bf16[64,384,384]{2,1,0:T(8,128)(2,1)} %get-tuple-element.161.b), custom_call_target="tpu_custom_call" | custom-call | flops 3600000000 | bytes 50000000 | tf_op jit(solution)/shard_map/pallas_call | solution.py:271
  365.9 16.3 %shard_map.135 = (bf16[2,32,96,384]{3,2,1,0:T(8,128)(2,1)}, bf16[2,32,96,384]{3,2,1,0:T(8,128)(2,1)}) custom-call(s32[5]{0:T(128)} %concatenate.82.idx, bf16[64,384,384]{2,1,0:T(8,128)(2,1)} %get-tuple-element.160.a, bf16[64,384,384]{2,1,0:T(8,128)(2,1)} %get-tuple-element.161.b), custom_call_target="tpu_custom_call" | custom-call | flops 3600000000 | bytes 50000000 | tf_op jit(solution)/shard_map/pallas_call | solution.py:271
  390.4 26.5 %finish.3 = (bf16[96,128,384]{2,1,0:T(8,128)(2,1)}, bf16[96,128,384]{2,1,0:T(8,128)(2,1)}) custom-call(s32[1]{0:T(128)} %constant.17.clone.1._, bf16[2,32,96,384]{3,2,1,0:T(8,128)(2,1)} %get-tuple-element.162.refs_0_, bf16[2,32,96,384]{3,2,1,0:T(8,128)(2,1)} %get-tuple-element.163.refs_1_, bf16[2,32,96,384]{3,2,1,0:T(8,128)(2,1)} %collective-permute-done.16.refs_2_, ...), custom_call_target="tpu_custom_call" | custom-call | flops 2831155200 | bytes 47185920 | tf_op jit(solution)/shard_map/finish/pallas_call | solution.py:298
  417.0 26.4 %finish.2 = (bf16[96,128,384]{2,1,0:T(8,128)(2,1)}, bf16[96,128,384]{2,1,0:T(8,128)(2,1)}) custom-call(s32[1]{0:T(128)} %constant.2.clone.1._, bf16[2,32,96,384]{3,2,1,0:T(8,128)(2,1)} %get-tuple-element.162.refs_0_, bf16[2,32,96,384]{3,2,1,0:T(8,128)(2,1)} %get-tuple-element.163.refs_1_, bf16[2,32,96,384]{3,2,1,0:T(8,128)(2,1)} %collective-permute-done.16.refs_2_, ...), custom_call_target="tpu_custom_call" | custom-call | flops 2831155200 | bytes 47185920 | tf_op jit(solution)/shard_map/finish/pallas_call | solution.py:298
  443.9 10.8 turn.1.refs_5_.refs_9_
  457.0 14.6 %prep.32 = (bf16[64,384,384]{2,1,0:T(8,128)(2,1)}, bf16[64,384,384]{2,1,0:T(8,128)(2,1)}) custom-call(s32[1]{0:T(128)S(6)} %mul.50.base, bf16[96,128,384]{2,1,0:T(8,128)(2,1)} %get-tuple-element.170.x_ref.refs_4_, f32[96,384]{1,0:T(8,128)} %copy-done, bf16[256,128]{1,0:T(8,128)(2,1)} %bitcast.138), custom_call_target="tpu_custom_call" | custom-call | flops 1887436800 | bytes 18874368 | tf_op jit(solution)/shard_map/prep/pallas_call | solution.py:199
  471.6 14.7 %prep.33 = (bf16[64,384,384]{2,1,0:T(8,128)(2,1)}, bf16[64,384,384]{2,1,0:T(8,128)(2,1)}) custom-call(s32[1]{0:T(128)S(6)} %mul.49.base, bf16[96,128,384]{2,1,0:T(8,128)(2,1)} %collective-permute-done.19.x_ref, f32[96,384]{1,0:T(8,128)} %collective-permute-done.15.m_ref, bf16[256,128]{1,0:T(8,128)(2,1)} %bitcast.139, ...), custom_call_target="tpu_custom_call", output_to_operand_aliasing={{0}: (4, {}), {1}: (5, {})} | custom-call | flops 1887436800 | bytes 18874368 | tf_op jit(solution)/shard_map/prep/pallas_call | solution.py:199
  486.4 14.6 %prep.34 = (bf16[64,384,384]{2,1,0:T(8,128)(2,1)}, bf16[64,384,384]{2,1,0:T(8,128)(2,1)}) custom-call(s32[1]{0:T(128)S(6)} %mul.48.base, bf16[96,128,384]{2,1,0:T(8,128)(2,1)} %get-tuple-element.168.x_ref.refs_4_, f32[96,384]{1,0:T(8,128)} %copy-done.7, bf16[256,128]{1,0:T(8,128)(2,1)} %bitcast.140, ...), custom_call_target="tpu_custom_call", output_to_operand_aliasing={{0}: (4, {}), {1}: (5, {})} | custom-call | flops 1887436800 | bytes 18874368 | tf_op jit(solution)/shard_map/prep/pallas_call | solution.py:199
  501.0 14.6 %prep.35 = (bf16[64,384,384]{2,1,0:T(8,128)(2,1)}, bf16[64,384,384]{2,1,0:T(8,128)(2,1)}) custom-call(s32[1]{0:T(128)S(6)} %mul.46.base, bf16[96,128,384]{2,1,0:T(8,128)(2,1)} %collective-permute-done.18.x_ref, f32[96,384]{1,0:T(8,128)} %collective-permute-done.8.m_ref, bf16[256,128]{1,0:T(8,128)(2,1)} %bitcast.141, ...), custom_call_target="tpu_custom_call", output_to_operand_aliasing={{0}: (4, {}), {1}: (5, {})} | custom-call | flops 1887436800 | bytes 18874368 | tf_op jit(solution)/shard_map/prep/pallas_call | solution.py:199
  515.6 19.5 %shard_map.138 = (bf16[2,32,96,384]{3,2,1,0:T(8,128)(2,1)}, bf16[2,32,96,384]{3,2,1,0:T(8,128)(2,1)}) custom-call(s32[5]{0:T(128)} %concatenate.84.idx, bf16[64,384,384]{2,1,0:T(8,128)(2,1)} %get-tuple-element.177.a, bf16[64,384,384]{2,1,0:T(8,128)(2,1)} %get-tuple-element.178.b), custom_call_target="tpu_custom_call" | custom-call | flops 3600000000 | bytes 50000000 | tf_op jit(solution)/shard_map/pallas_call | solution.py:271
  535.0 19.4 %shard_map.137 = (bf16[2,32,96,384]{3,2,1,0:T(8,128)(2,1)}, bf16[2,32,96,384]{3,2,1,0:T(8,128)(2,1)}) custom-call(s32[5]{0:T(128)} %concatenate.82.idx, bf16[64,384,384]{2,1,0:T(8,128)(2,1)} %get-tuple-element.177.a, bf16[64,384,384]{2,1,0:T(8,128)(2,1)} %get-tuple-element.178.b), custom_call_target="tpu_custom_call" | custom-call | flops 3600000000 | bytes 50000000 | tf_op jit(solution)/shard_map/pallas_call | solution.py:271
  557.2 102.8 %collective-permute-done.22.refs_5_.refs_9_ = bf16[96,128,384]{2,1,0:T(8,128)(2,1)} collective-permute-done((bf16[96,128,384]{2,1,0:T(8,128)(2,1)}, bf16[96,128,384]{2,1,0:T(8,128)(2,1)}, u32[]{:S(2)}, u32[]{:S(2)}) %collective-permute-start.22) | collective-permute-done | bytes 9437216 | tf_op jit(solution)/shard_map/ppermute | solution.py:446
  659.9 34.8 %head.5 = (bf16[64,96,384]{2,1,0:T(8,128)(2,1)}, bf16[64,96,384]{2,1,0:T(8,128)(2,1)}, bf16[96,128,384]{2,1,0:T(8,128)(2,1)}) custom-call(bf16[2,32,96,384]{3,2,1,0:T(8,128)(2,1)} %get-tuple-element.179.refs_0_, bf16[2,32,96,384]{3,2,1,0:T(8,128)(2,1)} %get-tuple-element.180.refs_1_, bf16[2,32,96,384]{3,2,1,0:T(8,128)(2,1)} %collective-permute-done.20.refs_2_, ...), custom_call_target="tpu_custom_call" | custom-call | flops 3774873600 | bytes 47185920 | tf_op jit(solution)/shard_map/head/pallas_call | solution.py:373
  694.8 38.8 %head.4 = (bf16[64,96,384]{2,1,0:T(8,128)(2,1)}, bf16[64,96,384]{2,1,0:T(8,128)(2,1)}, bf16[96,128,384]{2,1,0:T(8,128)(2,1)}, bf16[96,384,128]{2,1,0:T(8,128)(2,...) custom-call(bf16[2,32,96,384]{3,2,1,0:T(8,128)(2,1)} %get-tuple-element.179.refs_0_, ...), custom_call_target="tpu_custom_call" | custom-call | flops 3774873600 | bytes 47185920 | tf_op jit(solution)/shard_map/head/pallas_call | solution.py:373
  734.1 7.9 collective-permute-done.23.d2
  742.0 24.4 %shard_map.140 = (bf16[2,32,96,384]{3,2,1,0:T(8,128)(2,1)}, bf16[2,32,96,384]{3,2,1,0:T(8,128)(2,1)}, bf16[2,32,96,384]{3,2,1,0:T(8,128)(2,1)}, bf16[2,32,96,384]{3,2,1,0:T(8,128)(2,1)}) custom-call(s32[5]{0:T(128)} %concatenate.84.idx, bf16[64,96,384]{2,1,0:T(8,128)(2,1)} %get-tuple-element.185.d0, bf16[64,96,384]{2,1,0:T(8,128)(2,1)} %get-tuple-element.186.d1, ...), custom_call_target="tpu_custom_call" | custom-call | flops 7200000000 | bytes 50000000 | tf_op jit(solution)/shard_map/pallas_call | solution.py:271
  766.9 24.5 %shard_map.139 = (bf16[2,32,96,384]{3,2,1,0:T(8,128)(2,1)}, bf16[2,32,96,384]{3,2,1,0:T(8,128)(2,1)}, bf16[2,32,96,384]{3,2,1,0:T(8,128)(2,1)}, bf16[2,32,96,384]{3,2,1,0:T(8,128)(2,1)}) custom-call(s32[5]{0:T(128)} %concatenate.82.idx, bf16[64,96,384]{2,1,0:T(8,128)(2,1)} %get-tuple-element.185.d0, bf16[64,96,384]{2,1,0:T(8,128)(2,1)} %get-tuple-element.186.d1, ...), custom_call_target="tpu_custom_call" | custom-call | flops 7200000000 | bytes 50000000 | tf_op jit(solution)/shard_map/pallas_call | solution.py:271
  806.5 44.0 %back.4.refs_5_ = bf16[96,128,384]{2,1,0:T(8,128)(2,1)} custom-call(bf16[2,32,96,384]{3,2,1,0:T(8,128)(2,1)} %get-tuple-element.189.refs_0_, bf16[2,32,96,384]{3,2,1,0:T(8,128)(2,1)} %get-tuple-element.190.refs_1_, bf16[2,32,96,384]{3,2,1,0:T(8,128)(2,1)} %collective-permute-done.25.refs_2_, bf16[2,32,96,384]{3,2,1,0:T(8,128)(2,1)} %collective-permute-done.26.refs_3_, ...), custom_call_target="tpu_custom_call" | custom-call | flops 9437184000 | bytes 56623104 | tf_op jit(solution)/shard_map/back/pallas_call | solution.py:431
  850.5 30.4 %head.7 = (bf16[64,96,384]{2,1,0:T(8,128)(2,1)}, bf16[64,96,384]{2,1,0:T(8,128)(2,1)}) custom-call(bf16[2,32,96,384]{3,2,1,0:T(8,128)(2,1)} %get-tuple-element.162.refs_0_, bf16[2,32,96,384]{3,2,1,0:T(8,128)(2,1)} %get-tuple-element.163.refs_1_, bf16[2,32,96,384]{3,2,1,0:T(8,128)(2,1)} %collective-permute-done.16.refs_2_, ...), custom_call_target="tpu_custom_call" | custom-call | flops 3774873600 | bytes 47185920 | tf_op jit(solution)/shard_map/head/pallas_call | solution.py:373
  881.3 52.7 %back.3 = (bf16[96,128,384]{2,1,0:T(8,128)(2,1)}, f32[640,128]{1,0:T(8,128)}, f32[128,128]{1,0:T(8,128)}, f32[128,128]{1,0:T(8,128)}) custom-call(bf16[2,32,96,384]{3,2,1,0:T(8,128)(2,1)} %get-tuple-element.189.refs_0_, bf16[2,32,96,384]{3,2,1,0:T(8,128)(2,1)} %get-tuple-element.190.refs_1_, bf16[2,32,96,384]{3,2,1,0:T(8,128)(2,1)} %collective-permute-done.25.refs_2_, ...), custom_call_target="tpu_custom_call" | custom-call | flops 9437184000 | bytes 56623104 | tf_op jit(solution)/shard_map/back/pallas_call | solution.py:431
  934.1 35.5 %head.6 = (bf16[64,96,384]{2,1,0:T(8,128)(2,1)}, bf16[64,96,384]{2,1,0:T(8,128)(2,1)}, bf16[96,128,384]{2,1,0:T(8,128)(2,1)}, f32[128,128]{1,0:T(8,128)}, f32[128,128]{1,0:T(8,128)}, /*index=5*/f32[128,128]{1,0:T(8,128)}) custom-call(bf16[2,32,96,384]{3,2,1,0:T(8,128)(2,1)} %get-tuple-element.162.refs_0_, ...), custom_call_target="tpu_custom_call" | custom-call | flops 3774873600 | bytes 47185920 | tf_op jit(solution)/shard_map/head/pallas_call | solution.py:373
  977.9 19.8 %shard_map.142 = (bf16[1,32,96,384]{3,2,1,0:T(8,128)(2,1)}, bf16[1,32,96,384]{3,2,1,0:T(8,128)(2,1)}, bf16[1,32,96,384]{3,2,1,0:T(8,128)(2,1)}, bf16[1,32,96,384]{3,2,1,0:T(8,128)(2,1)}) custom-call(s32[5]{0:T(128)} %concatenate.84.idx, bf16[64,96,384]{2,1,0:T(8,128)(2,1)} %get-tuple-element.199.d0, bf16[64,96,384]{2,1,0:T(8,128)(2,1)} %get-tuple-element.202.d1, ...), custom_call_target="tpu_custom_call" | custom-call | flops 3600000000 | bytes 50000000 | tf_op jit(solution)/shard_map/pallas_call | solution.py:271
  998.3 19.8 %shard_map.141 = (bf16[1,32,96,384]{3,2,1,0:T(8,128)(2,1)}, bf16[1,32,96,384]{3,2,1,0:T(8,128)(2,1)}, bf16[1,32,96,384]{3,2,1,0:T(8,128)(2,1)}, bf16[1,32,96,384]{3,2,1,0:T(8,128)(2,1)}) custom-call(s32[5]{0:T(128)} %concatenate.82.idx, bf16[64,96,384]{2,1,0:T(8,128)(2,1)} %get-tuple-element.199.d0, bf16[64,96,384]{2,1,0:T(8,128)(2,1)} %get-tuple-element.202.d1, ...), custom_call_target="tpu_custom_call" | custom-call | flops 3600000000 | bytes 50000000 | tf_op jit(solution)/shard_map/pallas_call | solution.py:271
  1030.6 9.2 collective-permute-done.38
  1042.3 53.0 %back.5 = (bf16[96,384,128]{2,1,0:T(8,128)(2,1)}, f32[640,128]{1,0:T(8,128)}, f32[128,128]{1,0:T(8,128)}, f32[128,128]{1,0:T(8,128)}) custom-call(bf16[1,32,96,384]{3,2,1,0:T(8,128)(2,1)} %get-tuple-element.205.refs_0_, bf16[1,32,96,384]{3,2,1,0:T(8,128)(2,1)} %get-tuple-element.206.refs_1_, bf16[1,32,96,384]{3,2,1,0:T(8,128)(2,1)} %collective-permute-done.31.refs_2_, ...), custom_call_target="tpu_custom_call" | custom-call | flops 9437184000 | bytes 56623104 | tf_op jit(solution)/shard_map/back/pallas_call | solution.py:431
  (236 shorter events, 196.8 us)
Async XLA Ops:
  19.0 225.5 %collective-permute-start.14 = (bf16[96,128,384]{2,1,0:T(8,128)(2,1)}, bf16[96,128,384]{2,1,0:T(8,128)(2,1)}, u32[]{:S(2)}, u32[]{:S(2)}) collective-permute-start(bf16[96,128,384]{2,1,0:T(8,128)(2,1)} %get-tuple-element.133.x_ref.refs_5_.refs_4_), channel_id=1, source_target_pairs={{0,1},{1,0},{2,3},{3,2},{4,5},{5,4},{6,7},{7,6}} | collective-permute-start | bytes 28311560 | tf_op jit(solution)/shard_map/ppermute | solution.py:449
  21.3 109.9 %collective-permute-start.5 = (bf16[16,384,128]{2,1,0:T(8,128)(2,1)S(1)}, bf16[16,384,128]{2,1,0:T(8,128)(2,1)}, u32[]{:S(2)}, u32[]{:S(2)}) collective-permute-start(bf16[16,384,128]{2,1,0:T(8,128)(2,1)S(1)} %slice.250), channel_id=1, source_target_pairs={{0,2},{2,0},{1,3},{3,1},{4,6},{6,4},{5,7},{7,5}} | collective-permute-start | bytes 4718600 | tf_op jit(solution)/shard_map/ppermute | solution.py:446
  29.4 107.4 %collective-permute-start.4 = (bf16[16,384,128]{2,1,0:T(8,128)(2,1)}, bf16[16,384,128]{2,1,0:T(8,128)(2,1)S(1)}, u32[]{:S(2)}, u32[]{:S(2)}) collective-permute-start(bf16[16,384,128]{2,1,0:T(8,128)(2,1)} %get-tuple-element.263), channel_id=1, source_target_pairs={{0,2},{2,0},{1,3},{3,1},{4,6},{6,4},{5,7},{7,5}} | collective-permute-start | bytes 4718600 | tf_op jit(solution)/shard_map/ppermute | solution.py:446
  29.5 109.1 %collective-permute-start.3 = (bf16[16,384,128]{2,1,0:T(8,128)(2,1)}, bf16[16,384,128]{2,1,0:T(8,128)(2,1)S(1)}, u32[]{:S(2)}, u32[]{:S(2)}) collective-permute-start(bf16[16,384,128]{2,1,0:T(8,128)(2,1)} %get-tuple-element.264), channel_id=1, source_target_pairs={{0,2},{2,0},{1,3},{3,1},{4,6},{6,4},{5,7},{7,5}} | collective-permute-start | bytes 4718600 | tf_op jit(solution)/shard_map/ppermute | solution.py:446
  31.5 98.0 %collective-permute-start.7 = (f32[96,384]{1,0:T(8,128)S(1)}, f32[96,384]{1,0:T(8,128)S(1)}, u32[]{:S(2)}, u32[]{:S(2)}) collective-permute-start(f32[96,384]{1,0:T(8,128)S(1)} %convert_element_type.43.m_ref.refs_11_), channel_id=1, source_target_pairs={{0,2},{2,0},{1,3},{3,1},{4,6},{6,4},{5,7},{7,5}} | collective-permute-start | bytes 442376 | tf_op jit(solution)/shard_map/ppermute | solution.py:446
  129.5 37.6 %collective-permute-start.2 = (bf16[16,384,128]{2,1,0:T(8,128)(2,1)}, bf16[16,384,128]{2,1,0:T(8,128)(2,1)}, u32[]{:S(2)}, u32[]{:S(2)}) collective-permute-start(bf16[16,384,128]{2,1,0:T(8,128)(2,1)} %get-tuple-element.265), channel_id=1, source_target_pairs={{0,2},{2,0},{1,3},{3,1},{4,6},{6,4},{5,7},{7,5}} | collective-permute-start | bytes 4718600 | tf_op jit(solution)/shard_map/ppermute | solution.py:446
  131.2 69.5 %collective-permute-start.1 = (bf16[16,384,128]{2,1,0:T(8,128)(2,1)}, bf16[16,384,128]{2,1,0:T(8,128)(2,1)}, u32[]{:S(2)}, u32[]{:S(2)}) collective-permute-start(bf16[16,384,128]{2,1,0:T(8,128)(2,1)} %get-tuple-element.266), channel_id=1, source_target_pairs={{0,2},{2,0},{1,3},{3,1},{4,6},{6,4},{5,7},{7,5}} | collective-permute-start | bytes 4718600 | tf_op jit(solution)/shard_map/ppermute | solution.py:446
  136.8 96.6 %collective-permute-start = (bf16[16,384,128]{2,1,0:T(8,128)(2,1)}, bf16[16,384,128]{2,1,0:T(8,128)(2,1)}, u32[]{:S(2)}, u32[]{:S(2)}) collective-permute-start(bf16[16,384,128]{2,1,0:T(8,128)(2,1)} %get-tuple-element.267), channel_id=1, source_target_pairs={{0,2},{2,0},{1,3},{3,1},{4,6},{6,4},{5,7},{7,5}} | collective-permute-start | bytes 4718600 | tf_op jit(solution)/shard_map/ppermute | solution.py:446
  138.6 94.9 %collective-permute-start.13 = (bf16[16,128,384]{2,1,0:T(8,128)(2,1)}, bf16[16,128,384]{2,1,0:T(8,128)(2,1)S(1)}, u32[]{:S(2)}, u32[]{:S(2)}) collective-permute-start(bf16[16,128,384]{2,1,0:T(8,128)(2,1)} %get-tuple-element.132.x_ref), channel_id=1, source_target_pairs={{0,1},{1,0},{2,3},{3,2},{4,5},{5,4},{6,7},{7,6}} | collective-permute-start | bytes 4718600 | tf_op jit(solution)/shard_map/ppermute | solution.py:449
  167.1 54.9 %collective-permute-start.15 = (f32[96,384]{1,0:T(8,128)S(1)}, f32[96,384]{1,0:T(8,128)}, u32[]{:S(2)}, u32[]{:S(2)}) collective-permute-start(f32[96,384]{1,0:T(8,128)S(1)} %convert_element_type.43.m_ref.refs_11_), channel_id=1, source_target_pairs={{0,1},{1,0},{2,3},{3,2},{4,5},{5,4},{6,7},{7,6}} | collective-permute-start | bytes 442376 | tf_op jit(solution)/shard_map/ppermute | solution.py:449
  200.8 21.7 %collective-permute-start.8 = (f32[96,384]{1,0:T(8,128)S(1)}, f32[96,384]{1,0:T(8,128)}, u32[]{:S(2)}, u32[]{:S(2)}) collective-permute-start(f32[96,384]{1,0:T(8,128)S(1)} %collective-permute-done.7.m_ref.refs_11_), channel_id=1, source_target_pairs={{0,1},{1,0},{2,3},{3,2},{4,5},{5,4},{6,7},{7,6}} | collective-permute-start | bytes 442376 | tf_op jit(solution)/shard_map/ppermute | solution.py:449
  222.0 78.7 %collective-permute-start.12 = (bf16[16,128,384]{2,1,0:T(8,128)(2,1)}, bf16[16,128,384]{2,1,0:T(8,128)(2,1)}, u32[]{:S(2)}, u32[]{:S(2)}) collective-permute-start(bf16[16,128,384]{2,1,0:T(8,128)(2,1)} %get-tuple-element.131.x_ref), channel_id=1, source_target_pairs={{0,1},{1,0},{2,3},{3,2},{4,5},{5,4},{6,7},{7,6}} | collective-permute-start | bytes 4718600 | tf_op jit(solution)/shard_map/ppermute | solution.py:449
  222.5 88.8 %collective-permute-start.11 = (bf16[16,128,384]{2,1,0:T(8,128)(2,1)}, bf16[16,128,384]{2,1,0:T(8,128)(2,1)}, u32[]{:S(2)}, u32[]{:S(2)}) collective-permute-start(bf16[16,128,384]{2,1,0:T(8,128)(2,1)} %get-tuple-element.130.x_ref), channel_id=1, source_target_pairs={{0,1},{1,0},{2,3},{3,2},{4,5},{5,4},{6,7},{7,6}} | collective-permute-start | bytes 4718600 | tf_op jit(solution)/shard_map/ppermute | solution.py:449
  233.4 88.3 %collective-permute-start.10 = (bf16[16,128,384]{2,1,0:T(8,128)(2,1)S(1)}, bf16[16,128,384]{2,1,0:T(8,128)(2,1)}, u32[]{:S(2)}, u32[]{:S(2)}) collective-permute-start(bf16[16,128,384]{2,1,0:T(8,128)(2,1)S(1)} %copy-done.2), channel_id=1, source_target_pairs={{0,1},{1,0},{2,3},{3,2},{4,5},{5,4},{6,7},{7,6}} | collective-permute-start | bytes 4718600 | tf_op jit(solution)/shard_map/ppermute | solution.py:449
  234.6 97.6 %collective-permute-start.9 = (bf16[16,128,384]{2,1,0:T(8,128)(2,1)}, bf16[16,128,384]{2,1,0:T(8,128)(2,1)S(1)}, u32[]{:S(2)}, u32[]{:S(2)}) collective-permute-start(bf16[16,128,384]{2,1,0:T(8,128)(2,1)} %get-tuple-element.128.x_ref), channel_id=1, source_target_pairs={{0,1},{1,0},{2,3},{3,2},{4,5},{5,4},{6,7},{7,6}} | collective-permute-start | bytes 4718600 | tf_op jit(solution)/shard_map/ppermute | solution.py:449
  244.4 99.5 %collective-permute-start.6 = (bf16[16,128,384]{2,1,0:T(8,128)(2,1)}, bf16[16,128,384]{2,1,0:T(8,128)(2,1)}, u32[]{:S(2)}, u32[]{:S(2)}) collective-permute-start(bf16[16,128,384]{2,1,0:T(8,128)(2,1)} %get-tuple-element.127.x_ref), channel_id=1, source_target_pairs={{0,1},{1,0},{2,3},{3,2},{4,5},{5,4},{6,7},{7,6}} | collective-permute-start | bytes 4718600 | tf_op jit(solution)/shard_map/ppermute | solution.py:449
  365.4 20.4 %collective-permute-start.17 = (bf16[2,32,96,384]{3,2,1,0:T(8,128)(2,1)}, bf16[2,32,96,384]{3,2,1,0:T(8,128)(2,1)}, u32[]{:S(2)}, u32[]{:S(2)}) collective-permute-start(bf16[2,32,96,384]{3,2,1,0:T(8,128)(2,1)} %get-tuple-element.165), channel_id=1, source_target_pairs={{0,1},{1,0},{2,3},{3,2},{4,5},{5,4},{6,7},{7,6}} | collective-permute-start | bytes 14155784 | tf_op jit(solution)/shard_map/ppermute | solution.py:449
  416.9 54.7 %collective-permute-start.19 = (bf16[96,128,384]{2,1,0:T(8,128)(2,1)}, bf16[96,128,384]{2,1,0:T(8,128)(2,1)}, u32[]{:S(2)}, u32[]{:S(2)}) collective-permute-start(bf16[96,128,384]{2,1,0:T(8,128)(2,1)} %get-tuple-element.170.x_ref.refs_4_), channel_id=1, source_target_pairs={{0,1},{1,0},{2,3},{3,2},{4,5},{5,4},{6,7},{7,6}} | collective-permute-start | bytes 28311560 | tf_op jit(solution)/shard_map/ppermute | solution.py:449
  443.5 57.5 %collective-permute-start.18 = (bf16[96,128,384]{2,1,0:T(8,128)(2,1)}, bf16[96,128,384]{2,1,0:T(8,128)(2,1)}, u32[]{:S(2)}, u32[]{:S(2)}) collective-permute-start(bf16[96,128,384]{2,1,0:T(8,128)(2,1)} %get-tuple-element.168.x_ref.refs_4_), channel_id=1, source_target_pairs={{0,1},{1,0},{2,3},{3,2},{4,5},{5,4},{6,7},{7,6}} | collective-permute-start | bytes 28311560 | tf_op jit(solution)/shard_map/ppermute | solution.py:449
  454.7 205.2 %collective-permute-start.22 = (bf16[96,128,384]{2,1,0:T(8,128)(2,1)}, bf16[96,128,384]{2,1,0:T(8,128)(2,1)}, u32[]{:S(2)}, u32[]{:S(2)}) collective-permute-start(bf16[96,128,384]{2,1,0:T(8,128)(2,1)} %turn.1.refs_5_.refs_9_), channel_id=1, source_target_pairs={{0,2},{2,0},{1,3},{3,1},{4,6},{6,4},{5,7},{7,5}} | collective-permute-start | bytes 28311560 | tf_op jit(solution)/shard_map/ppermute | solution.py:446
  535.0 124.9 %collective-permute-start.21 = (bf16[2,32,96,384]{3,2,1,0:T(8,128)(2,1)}, bf16[2,32,96,384]{3,2,1,0:T(8,128)(2,1)}, u32[]{:S(2)}, u32[]{:S(2)}) collective-permute-start(bf16[2,32,96,384]{3,2,1,0:T(8,128)(2,1)} %get-tuple-element.182), channel_id=1, source_target_pairs={{0,1},{1,0},{2,3},{3,2},{4,5},{5,4},{6,7},{7,6}} | collective-permute-start | bytes 14155784 | tf_op jit(solution)/shard_map/ppermute | solution.py:449
  554.5 105.5 %collective-permute-start.20 = (bf16[2,32,96,384]{3,2,1,0:T(8,128)(2,1)}, bf16[2,32,96,384]{3,2,1,0:T(8,128)(2,1)}, u32[]{:S(2)}, u32[]{:S(2)}) collective-permute-start(bf16[2,32,96,384]{3,2,1,0:T(8,128)(2,1)} %get-tuple-element.181), channel_id=1, source_target_pairs={{0,1},{1,0},{2,3},{3,2},{4,5},{5,4},{6,7},{7,6}} | collective-permute-start | bytes 14155784 | tf_op jit(solution)/shard_map/ppermute | solution.py:449
  694.8 39.3 %collective-permute-start.24 = (bf16[64,96,384]{2,1,0:T(8,128)(2,1)}, bf16[64,96,384]{2,1,0:T(8,128)(2,1)}, u32[]{:S(2)}, u32[]{:S(2)}) collective-permute-start(bf16[64,96,384]{2,1,0:T(8,128)(2,1)} %get-tuple-element.188), channel_id=1, source_target_pairs={{0,1},{1,0},{2,3},{3,2},{4,5},{5,4},{6,7},{7,6}} | collective-permute-start | bytes 14155784 | tf_op jit(solution)/shard_map/ppermute | solution.py:449
  766.4 28.0 %collective-permute-start.26 = (bf16[2,32,96,384]{3,2,1,0:T(8,128)(2,1)}, bf16[2,32,96,384]{3,2,1,0:T(8,128)(2,1)}, u32[]{:S(2)}, u32[]{:S(2)}) collective-permute-start(bf16[2,32,96,384]{3,2,1,0:T(8,128)(2,1)} %get-tuple-element.192), channel_id=1, source_target_pairs={{0,1},{1,0},{2,3},{3,2},{4,5},{5,4},{6,7},{7,6}} | collective-permute-start | bytes 14155784 | tf_op jit(solution)/shard_map/ppermute | solution.py:449
  766.9 27.5 %collective-permute-start.28 = (bf16[2,32,96,384]{3,2,1,0:T(8,128)(2,1)}, bf16[2,32,96,384]{3,2,1,0:T(8,128)(2,1)}, u32[]{:S(2)}, u32[]{:S(2)}) collective-permute-start(bf16[2,32,96,384]{3,2,1,0:T(8,128)(2,1)} %get-tuple-element.196), channel_id=1, source_target_pairs={{0,1},{1,0},{2,3},{3,2},{4,5},{5,4},{6,7},{7,6}} | collective-permute-start | bytes 14155784 | tf_op jit(solution)/shard_map/ppermute | solution.py:449
  791.9 14.6 %collective-permute-start.27 = (bf16[2,32,96,384]{3,2,1,0:T(8,128)(2,1)}, bf16[2,32,96,384]{3,2,1,0:T(8,128)(2,1)}, u32[]{:S(2)}, u32[]{:S(2)}) collective-permute-start(bf16[2,32,96,384]{3,2,1,0:T(8,128)(2,1)} %get-tuple-element.195), channel_id=1, source_target_pairs={{0,1},{1,0},{2,3},{3,2},{4,5},{5,4},{6,7},{7,6}} | collective-permute-start | bytes 14155784 | tf_op jit(solution)/shard_map/ppermute | solution.py:449
  881.0 91.8 %collective-permute-start.30 = (bf16[64,96,384]{2,1,0:T(8,128)(2,1)}, bf16[64,96,384]{2,1,0:T(8,128)(2,1)}, u32[]{:S(2)}, u32[]{:S(2)}) collective-permute-start(bf16[64,96,384]{2,1,0:T(8,128)(2,1)} %get-tuple-element.204), channel_id=1, source_target_pairs={{0,1},{1,0},{2,3},{3,2},{4,5},{5,4},{6,7},{7,6}} | collective-permute-start | bytes 14155784 | tf_op jit(solution)/shard_map/ppermute | solution.py:449
  997.7 43.1 %collective-permute-start.32 = (bf16[1,32,96,384]{3,2,1,0:T(8,128)(2,1)}, bf16[1,32,96,384]{3,2,1,0:T(8,128)(2,1)S(1)}, u32[]{:S(2)}, u32[]{:S(2)}) collective-permute-start(bf16[1,32,96,384]{3,2,1,0:T(8,128)(2,1)} %get-tuple-element.208), channel_id=1, source_target_pairs={{0,1},{1,0},{2,3},{3,2},{4,5},{5,4},{6,7},{7,6}} | collective-permute-start | bytes 7077896 | tf_op jit(solution)/shard_map/ppermute | solution.py:449
  997.9 42.9 %collective-permute-start.34 = (bf16[1,32,96,384]{3,2,1,0:T(8,128)(2,1)}, bf16[1,32,96,384]{3,2,1,0:T(8,128)(2,1)}, u32[]{:S(2)}, u32[]{:S(2)}) collective-permute-start(bf16[1,32,96,384]{3,2,1,0:T(8,128)(2,1)} %get-tuple-element.212), channel_id=1, source_target_pairs={{0,1},{1,0},{2,3},{3,2},{4,5},{5,4},{6,7},{7,6}} | collective-permute-start | bytes 7077896 | tf_op jit(solution)/shard_map/ppermute | solution.py:449
  1018.0 22.8 %collective-permute-start.31 = (bf16[1,32,96,384]{3,2,1,0:T(8,128)(2,1)}, bf16[1,32,96,384]{3,2,1,0:T(8,128)(2,1)}, u32[]{:S(2)}, u32[]{:S(2)}) collective-permute-start(bf16[1,32,96,384]{3,2,1,0:T(8,128)(2,1)} %get-tuple-element.207), channel_id=1, source_target_pairs={{0,1},{1,0},{2,3},{3,2},{4,5},{5,4},{6,7},{7,6}} | collective-permute-start | bytes 7077896 | tf_op jit(solution)/shard_map/ppermute | solution.py:449
  1018.3 22.6 %collective-permute-start.33 = (bf16[1,32,96,384]{3,2,1,0:T(8,128)(2,1)}, bf16[1,32,96,384]{3,2,1,0:T(8,128)(2,1)}, u32[]{:S(2)}, u32[]{:S(2)}) collective-permute-start(bf16[1,32,96,384]{3,2,1,0:T(8,128)(2,1)} %get-tuple-element.211), channel_id=1, source_target_pairs={{0,1},{1,0},{2,3},{3,2},{4,5},{5,4},{6,7},{7,6}} | collective-permute-start | bytes 7077896 | tf_op jit(solution)/shard_map/ppermute | solution.py:449
  1026.9 12.8 %collective-permute-start.38 = (f32[904,128]{1,0:T(8,128)S(1)}, f32[904,128]{1,0:T(8,128)}, u32[]{:S(2)}, u32[]{:S(2)}) collective-permute-start(f32[904,128]{1,0:T(8,128)S(1)} %add.54), channel_id=1, source_target_pairs={{0,2},{2,0},{1,3},{3,1},{4,6},{6,4},{5,7},{7,5}} | collective-permute-start | bytes 1388552 | tf_op jit(solution)/shard_map/ppermute | solution.py:446
  (34 other events, 859.4 us)

commit v7 on v6

--- a/solution.py
+++ b/solution.py
@@ -219,7 +219,7 @@
         lhs = jnp.concatenate(block_rows(idx, a, c), axis=0)
         emit(dot(lhs, b[c], 1, 1).astype(BF16), keep, send, c)
 
-    rows_loop(chan, 1, CB)
+    rows_loop(chan, 2, CB)
 
 
 def tri_in_body(idx, a, b, keep, send, s):
@@ -228,7 +228,7 @@
         lhs = jnp.concatenate(block_rows(idx, s, c), axis=0)
         emit(dot(lhs, b[c]).astype(BF16), keep, send, c)
 
-    rows_loop(chan, 1, CB)
+    rows_loop(chan, 2, CB)
 
 
 def gather_dt(idx, parts, c, s):
@@ -257,7 +257,7 @@
         dbk[0, c] = db[:RB]
         dbs[0, c] = db[RB:]
 
-    rows_loop(chan, 1, CB)
+    rows_loop(chan, 2, CB)
 
 
 def tri_call(body, idx, part, dts, ab, pieces, n_out, n_scr, flops):
@@ -351,7 +351,7 @@
             ggain[...] += fold(dy * th)
             gshift[...] += fold(dy)
 
-    rows_loop(row)
+    rows_loop(row, UNROLL if emit_dg else 1)
     flush(sd, [dt_keep, dt_send])
 
 

time: 1120 us -> 1110 us (level)
    pallas_call x8, Pallas kernels: 160 us -> 145 us  [tri_call(): pl.pallas_call(body, grid_spec=grid_spec, out_shape=[jax.ShapeDtypeStruct...]
  transfers between devices with their start and end apart: 39 -> 39, of which waited for: 14 -> 14; matrix products, arithmetic and copies ran while one was open for 3% -> 3% of each run, Pallas kernels for 40% -> 39%
where the time goes in v7:
time: 1110 us
  Pallas kernels  709 us (64%)
  waiting for transfers between devices  333 us (30%)
  local copies, waits for them, and re-layouts  30.3 us (3%)
  starting transfers between devices  19.9 us (2%)
  other arithmetic  17.4 us (2%)
    ppermute x10, waiting for transfers between devices, ici(): return lax.ppermute(v, AX, ICI_SWAP)  298 us
    pallas_call x18, Pallas kernels, prep(): pl.pallas_call(functools.partial(prep_body, unroll if rows == RB else 1),...  158 us
    pallas_call x3, Pallas kernels, back(): pl.pallas_call(functools.partial(back_body, n, emit_w, last), grid=(RB //...  150 us
    pallas_call x8, Pallas kernels, tri_call(): pl.pallas_call(body, grid_spec=grid_spec, out_shape=[jax.ShapeDtypeStruct...  145 us
    pallas_call x4, Pallas kernels, head(): pl.pallas_call(functools.partial(head_body, emit_z, emit_w, emit_dg), gri...  144 us
    pallas_call x2, Pallas kernels, finish(): pl.pallas_call(finish_body, grid_spec=grid_spec, out_shape=[ACTT] * 2, co...  52.9 us
    pallas_call x7, Pallas kernels, norm(): pl.pallas_call(functools.partial(norm_body, 1), grid_spec=grid_spec, out_...  48.1 us
    ppermute x29, waiting for transfers between devices, d2d(): return lax.ppermute(v, AX, D2D_SWAP)  34.7 us
  transfers between devices with their start and end apart: 39, of which 14 were waited for; matrix products, arithmetic and copies ran while one was open for 3% of the time, Pallas kernels for 39%

profile of v7, /device:TPU:0, one launch (start us, length us, event | category | flops | bytes accessed | tf_op | source)
XLA Modules:
  0.0 1111.1 jit_solution(8154037246767637397)
XLA Ops:
  2.6 16.4 %norm.13 = (bf16[96,128,384]{2,1,0:T(8,128)(2,1)}, bf16[96,128,384]{2,1,0:T(8,128)(2,1)}, bf16[96,128,384]{2,1,0:T(8,128)(2,1)}) custom-call(s32[1]{0:T(128)} %constant.17.clone.1._, bf16[96,384,128]{2,1,0:T(8,128)(2,1)} %z_ref.2, f32[128,2]{1,0:T(8,128)} %convert_bitcast_fusion.3.ln_ref.refs_12_), custom_call_target="tpu_custom_call" | custom-call | flops 283115520 | bytes 37748736 | tf_op jit(solution)/shard_map/norm/pallas_call | solution.py:169
  31.6 97.9 %collective-permute-done.7.m_ref.refs_11_ = f32[96,384]{1,0:T(8,128)S(1)} collective-permute-done((f32[96,384]{1,0:T(8,128)S(1)}, f32[96,384]{1,0:T(8,128)S(1)}, u32[]{:S(2)}, u32[]{:S(2)}) %collective-permute-start.7) | collective-permute-done | bytes 147488 | tf_op jit(solution)/shard_map/ppermute | solution.py:446
  138.6 28.4 %collective-permute-done.2.z_ref = bf16[16,384,128]{2,1,0:T(8,128)(2,1)} collective-permute-done((bf16[16,384,128]{2,1,0:T(8,128)(2,1)}, bf16[16,384,128]{2,1,0:T(8,128)(2,1)}, u32[]{:S(2)}, u32[]{:S(2)}) %collective-permute-start.2) | collective-permute-done | bytes 1572896 | tf_op jit(solution)/shard_map/ppermute | solution.py:446
  167.1 33.7 %collective-permute-done.1.z_ref = bf16[16,384,128]{2,1,0:T(8,128)(2,1)} collective-permute-done((bf16[16,384,128]{2,1,0:T(8,128)(2,1)}, bf16[16,384,128]{2,1,0:T(8,128)(2,1)}, u32[]{:S(2)}, u32[]{:S(2)}) %collective-permute-start.1) | collective-permute-done | bytes 1572896 | tf_op jit(solution)/shard_map/ppermute | solution.py:446
  222.5 10.9 collective-permute-done.z_ref
  245.7 18.5 %prep.18 = (bf16[64,384,384]{2,1,0:T(8,128)(2,1)}, bf16[64,384,384]{2,1,0:T(8,128)(2,1)}) custom-call(s32[1]{0:T(128)S(6)} %mul.50.base, bf16[96,128,384]{2,1,0:T(8,128)(2,1)} %get-tuple-element.133.x_ref.refs_5_.refs_4_, f32[96,384]{1,0:T(8,128)} %copy-done, bf16[256,128]{1,0:T(8,128)(2,1)} %bitcast.124), custom_call_target="tpu_custom_call" | custom-call | flops 1887436800 | bytes 18874368 | tf_op jit(solution)/shard_map/prep/pallas_call | solution.py:199
  266.4 18.6 %prep.19 = (bf16[64,384,384]{2,1,0:T(8,128)(2,1)}, bf16[64,384,384]{2,1,0:T(8,128)(2,1)}) custom-call(s32[1]{0:T(128)S(6)} %mul.49.base, bf16[96,128,384]{2,1,0:T(8,128)(2,1)} %collective-permute-done.14.x_ref, f32[96,384]{1,0:T(8,128)} %collective-permute-done.15.m_ref, bf16[256,128]{1,0:T(8,128)(2,1)} %bitcast.125, ...), custom_call_target="tpu_custom_call", output_to_operand_aliasing={{0}: (4, {}), {1}: (5, {})} | custom-call | flops 1887436800 | bytes 18874368 | tf_op jit(solution)/shard_map/prep/pallas_call | solution.py:199
  349.1 14.5 %shard_map.136 = (bf16[2,32,96,384]{3,2,1,0:T(8,128)(2,1)}, bf16[2,32,96,384]{3,2,1,0:T(8,128)(2,1)}) custom-call(s32[5]{0:T(128)} %concatenate.84.idx, bf16[64,384,384]{2,1,0:T(8,128)(2,1)} %get-tuple-element.160.a, bf16[64,384,384]{2,1,0:T(8,128)(2,1)} %get-tuple-element.161.b), custom_call_target="tpu_custom_call" | custom-call | flops 3600000000 | bytes 50000000 | tf_op jit(solution)/shard_map/pallas_call | solution.py:271
  364.2 14.5 %shard_map.135 = (bf16[2,32,96,384]{3,2,1,0:T(8,128)(2,1)}, bf16[2,32,96,384]{3,2,1,0:T(8,128)(2,1)}) custom-call(s32[5]{0:T(128)} %concatenate.82.idx, bf16[64,384,384]{2,1,0:T(8,128)(2,1)} %get-tuple-element.160.a, bf16[64,384,384]{2,1,0:T(8,128)(2,1)} %get-tuple-element.161.b), custom_call_target="tpu_custom_call" | custom-call | flops 3600000000 | bytes 50000000 | tf_op jit(solution)/shard_map/pallas_call | solution.py:271
  386.9 26.5 %finish.3 = (bf16[96,128,384]{2,1,0:T(8,128)(2,1)}, bf16[96,128,384]{2,1,0:T(8,128)(2,1)}) custom-call(s32[1]{0:T(128)} %constant.17.clone.1._, bf16[2,32,96,384]{3,2,1,0:T(8,128)(2,1)} %get-tuple-element.162.refs_0_, bf16[2,32,96,384]{3,2,1,0:T(8,128)(2,1)} %get-tuple-element.163.refs_1_, bf16[2,32,96,384]{3,2,1,0:T(8,128)(2,1)} %collective-permute-done.16.refs_2_, ...), custom_call_target="tpu_custom_call" | custom-call | flops 2831155200 | bytes 47185920 | tf_op jit(solution)/shard_map/finish/pallas_call | solution.py:298
  413.7 26.4 %finish.2 = (bf16[96,128,384]{2,1,0:T(8,128)(2,1)}, bf16[96,128,384]{2,1,0:T(8,128)(2,1)}) custom-call(s32[1]{0:T(128)} %constant.2.clone.1._, bf16[2,32,96,384]{3,2,1,0:T(8,128)(2,1)} %get-tuple-element.162.refs_0_, bf16[2,32,96,384]{3,2,1,0:T(8,128)(2,1)} %get-tuple-element.163.refs_1_, bf16[2,32,96,384]{3,2,1,0:T(8,128)(2,1)} %collective-permute-done.16.refs_2_, ...), custom_call_target="tpu_custom_call" | custom-call | flops 2831155200 | bytes 47185920 | tf_op jit(solution)/shard_map/finish/pallas_call | solution.py:298
  440.4 10.8 turn.1.refs_5_.refs_9_
  453.5 14.6 %prep.32 = (bf16[64,384,384]{2,1,0:T(8,128)(2,1)}, bf16[64,384,384]{2,1,0:T(8,128)(2,1)}) custom-call(s32[1]{0:T(128)S(6)} %mul.50.base, bf16[96,128,384]{2,1,0:T(8,128)(2,1)} %get-tuple-element.170.x_ref.refs_4_, f32[96,384]{1,0:T(8,128)} %copy-done, bf16[256,128]{1,0:T(8,128)(2,1)} %bitcast.138), custom_call_target="tpu_custom_call" | custom-call | flops 1887436800 | bytes 18874368 | tf_op jit(solution)/shard_map/prep/pallas_call | solution.py:199
  468.1 14.6 %prep.33 = (bf16[64,384,384]{2,1,0:T(8,128)(2,1)}, bf16[64,384,384]{2,1,0:T(8,128)(2,1)}) custom-call(s32[1]{0:T(128)S(6)} %mul.49.base, bf16[96,128,384]{2,1,0:T(8,128)(2,1)} %collective-permute-done.19.x_ref, f32[96,384]{1,0:T(8,128)} %collective-permute-done.15.m_ref, bf16[256,128]{1,0:T(8,128)(2,1)} %bitcast.139, ...), custom_call_target="tpu_custom_call", output_to_operand_aliasing={{0}: (4, {}), {1}: (5, {})} | custom-call | flops 1887436800 | bytes 18874368 | tf_op jit(solution)/shard_map/prep/pallas_call | solution.py:199
  482.7 14.6 %prep.34 = (bf16[64,384,384]{2,1,0:T(8,128)(2,1)}, bf16[64,384,384]{2,1,0:T(8,128)(2,1)}) custom-call(s32[1]{0:T(128)S(6)} %mul.48.base, bf16[96,128,384]{2,1,0:T(8,128)(2,1)} %get-tuple-element.168.x_ref.refs_4_, f32[96,384]{1,0:T(8,128)} %copy-done.7, bf16[256,128]{1,0:T(8,128)(2,1)} %bitcast.140, ...), custom_call_target="tpu_custom_call", output_to_operand_aliasing={{0}: (4, {}), {1}: (5, {})} | custom-call | flops 1887436800 | bytes 18874368 | tf_op jit(solution)/shard_map/prep/pallas_call | solution.py:199
  497.3 14.6 %prep.35 = (bf16[64,384,384]{2,1,0:T(8,128)(2,1)}, bf16[64,384,384]{2,1,0:T(8,128)(2,1)}) custom-call(s32[1]{0:T(128)S(6)} %mul.46.base, bf16[96,128,384]{2,1,0:T(8,128)(2,1)} %collective-permute-done.18.x_ref, f32[96,384]{1,0:T(8,128)} %collective-permute-done.8.m_ref, bf16[256,128]{1,0:T(8,128)(2,1)} %bitcast.141, ...), custom_call_target="tpu_custom_call", output_to_operand_aliasing={{0}: (4, {}), {1}: (5, {})} | custom-call | flops 1887436800 | bytes 18874368 | tf_op jit(solution)/shard_map/prep/pallas_call | solution.py:199
  511.9 15.7 %shard_map.138 = (bf16[2,32,96,384]{3,2,1,0:T(8,128)(2,1)}, bf16[2,32,96,384]{3,2,1,0:T(8,128)(2,1)}) custom-call(s32[5]{0:T(128)} %concatenate.84.idx, bf16[64,384,384]{2,1,0:T(8,128)(2,1)} %get-tuple-element.177.a, bf16[64,384,384]{2,1,0:T(8,128)(2,1)} %get-tuple-element.178.b), custom_call_target="tpu_custom_call" | custom-call | flops 3600000000 | bytes 50000000 | tf_op jit(solution)/shard_map/pallas_call | solution.py:271
  527.6 15.7 %shard_map.137 = (bf16[2,32,96,384]{3,2,1,0:T(8,128)(2,1)}, bf16[2,32,96,384]{3,2,1,0:T(8,128)(2,1)}) custom-call(s32[5]{0:T(128)} %concatenate.82.idx, bf16[64,384,384]{2,1,0:T(8,128)(2,1)} %get-tuple-element.177.a, bf16[64,384,384]{2,1,0:T(8,128)(2,1)} %get-tuple-element.178.b), custom_call_target="tpu_custom_call" | custom-call | flops 3600000000 | bytes 50000000 | tf_op jit(solution)/shard_map/pallas_call | solution.py:271
  546.1 110.5 %collective-permute-done.22.refs_5_.refs_9_ = bf16[96,128,384]{2,1,0:T(8,128)(2,1)} collective-permute-done((bf16[96,128,384]{2,1,0:T(8,128)(2,1)}, bf16[96,128,384]{2,1,0:T(8,128)(2,1)}, u32[]{:S(2)}, u32[]{:S(2)}) %collective-permute-start.22) | collective-permute-done | bytes 9437216 | tf_op jit(solution)/shard_map/ppermute | solution.py:446
  656.6 34.8 %head.5 = (bf16[64,96,384]{2,1,0:T(8,128)(2,1)}, bf16[64,96,384]{2,1,0:T(8,128)(2,1)}, bf16[96,128,384]{2,1,0:T(8,128)(2,1)}) custom-call(bf16[2,32,96,384]{3,2,1,0:T(8,128)(2,1)} %get-tuple-element.179.refs_0_, bf16[2,32,96,384]{3,2,1,0:T(8,128)(2,1)} %get-tuple-element.180.refs_1_, bf16[2,32,96,384]{3,2,1,0:T(8,128)(2,1)} %collective-permute-done.20.refs_2_, ...), custom_call_target="tpu_custom_call" | custom-call | flops 3774873600 | bytes 47185920 | tf_op jit(solution)/shard_map/head/pallas_call | solution.py:373
  691.4 38.8 %head.4 = (bf16[64,96,384]{2,1,0:T(8,128)(2,1)}, bf16[64,96,384]{2,1,0:T(8,128)(2,1)}, bf16[96,128,384]{2,1,0:T(8,128)(2,1)}, bf16[96,384,128]{2,1,0:T(8,128)(2,...) custom-call(bf16[2,32,96,384]{3,2,1,0:T(8,128)(2,1)} %get-tuple-element.179.refs_0_, ...), custom_call_target="tpu_custom_call" | custom-call | flops 3774873600 | bytes 47185920 | tf_op jit(solution)/shard_map/head/pallas_call | solution.py:373
  730.8 7.9 collective-permute-done.23.d2
  738.6 24.4 %shard_map.140 = (bf16[2,32,96,384]{3,2,1,0:T(8,128)(2,1)}, bf16[2,32,96,384]{3,2,1,0:T(8,128)(2,1)}, bf16[2,32,96,384]{3,2,1,0:T(8,128)(2,1)}, bf16[2,32,96,384]{3,2,1,0:T(8,128)(2,1)}) custom-call(s32[5]{0:T(128)} %concatenate.84.idx, bf16[64,96,384]{2,1,0:T(8,128)(2,1)} %get-tuple-element.185.d0, bf16[64,96,384]{2,1,0:T(8,128)(2,1)} %get-tuple-element.186.d1, ...), custom_call_target="tpu_custom_call" | custom-call | flops 7200000000 | bytes 50000000 | tf_op jit(solution)/shard_map/pallas_call | solution.py:271
  763.6 24.5 %shard_map.139 = (bf16[2,32,96,384]{3,2,1,0:T(8,128)(2,1)}, bf16[2,32,96,384]{3,2,1,0:T(8,128)(2,1)}, bf16[2,32,96,384]{3,2,1,0:T(8,128)(2,1)}, bf16[2,32,96,384]{3,2,1,0:T(8,128)(2,1)}) custom-call(s32[5]{0:T(128)} %concatenate.82.idx, bf16[64,96,384]{2,1,0:T(8,128)(2,1)} %get-tuple-element.185.d0, bf16[64,96,384]{2,1,0:T(8,128)(2,1)} %get-tuple-element.186.d1, ...), custom_call_target="tpu_custom_call" | custom-call | flops 7200000000 | bytes 50000000 | tf_op jit(solution)/shard_map/pallas_call | solution.py:271
  803.2 44.0 %back.4.refs_5_ = bf16[96,128,384]{2,1,0:T(8,128)(2,1)} custom-call(bf16[2,32,96,384]{3,2,1,0:T(8,128)(2,1)} %get-tuple-element.189.refs_0_, bf16[2,32,96,384]{3,2,1,0:T(8,128)(2,1)} %get-tuple-element.190.refs_1_, bf16[2,32,96,384]{3,2,1,0:T(8,128)(2,1)} %collective-permute-done.25.refs_2_, bf16[2,32,96,384]{3,2,1,0:T(8,128)(2,1)} %collective-permute-done.26.refs_3_, ...), custom_call_target="tpu_custom_call" | custom-call | flops 9437184000 | bytes 56623104 | tf_op jit(solution)/shard_map/back/pallas_call | solution.py:431
  847.2 35.3 %head.7 = (bf16[64,96,384]{2,1,0:T(8,128)(2,1)}, bf16[64,96,384]{2,1,0:T(8,128)(2,1)}) custom-call(bf16[2,32,96,384]{3,2,1,0:T(8,128)(2,1)} %get-tuple-element.162.refs_0_, bf16[2,32,96,384]{3,2,1,0:T(8,128)(2,1)} %get-tuple-element.163.refs_1_, bf16[2,32,96,384]{3,2,1,0:T(8,128)(2,1)} %collective-permute-done.16.refs_2_, ...), custom_call_target="tpu_custom_call" | custom-call | flops 3774873600 | bytes 47185920 | tf_op jit(solution)/shard_map/head/pallas_call | solution.py:373
  882.8 52.7 %back.3 = (bf16[96,128,384]{2,1,0:T(8,128)(2,1)}, f32[640,128]{1,0:T(8,128)}, f32[128,128]{1,0:T(8,128)}, f32[128,128]{1,0:T(8,128)}) custom-call(bf16[2,32,96,384]{3,2,1,0:T(8,128)(2,1)} %get-tuple-element.189.refs_0_, bf16[2,32,96,384]{3,2,1,0:T(8,128)(2,1)} %get-tuple-element.190.refs_1_, bf16[2,32,96,384]{3,2,1,0:T(8,128)(2,1)} %collective-permute-done.25.refs_2_, ...), custom_call_target="tpu_custom_call" | custom-call | flops 9437184000 | bytes 56623104 | tf_op jit(solution)/shard_map/back/pallas_call | solution.py:431
  935.6 35.5 %head.6 = (bf16[64,96,384]{2,1,0:T(8,128)(2,1)}, bf16[64,96,384]{2,1,0:T(8,128)(2,1)}, bf16[96,128,384]{2,1,0:T(8,128)(2,1)}, f32[128,128]{1,0:T(8,128)}, f32[128,128]{1,0:T(8,128)}, /*index=5*/f32[128,128]{1,0:T(8,128)}) custom-call(bf16[2,32,96,384]{3,2,1,0:T(8,128)(2,1)} %get-tuple-element.162.refs_0_, ...), custom_call_target="tpu_custom_call" | custom-call | flops 3774873600 | bytes 47185920 | tf_op jit(solution)/shard_map/head/pallas_call | solution.py:373
  979.4 17.6 %shard_map.142 = (bf16[1,32,96,384]{3,2,1,0:T(8,128)(2,1)}, bf16[1,32,96,384]{3,2,1,0:T(8,128)(2,1)}, bf16[1,32,96,384]{3,2,1,0:T(8,128)(2,1)}, bf16[1,32,96,384]{3,2,1,0:T(8,128)(2,1)}) custom-call(s32[5]{0:T(128)} %concatenate.84.idx, bf16[64,96,384]{2,1,0:T(8,128)(2,1)} %get-tuple-element.199.d0, bf16[64,96,384]{2,1,0:T(8,128)(2,1)} %get-tuple-element.202.d1, ...), custom_call_target="tpu_custom_call" | custom-call | flops 3600000000 | bytes 50000000 | tf_op jit(solution)/shard_map/pallas_call | solution.py:271
  997.6 17.6 %shard_map.141 = (bf16[1,32,96,384]{3,2,1,0:T(8,128)(2,1)}, bf16[1,32,96,384]{3,2,1,0:T(8,128)(2,1)}, bf16[1,32,96,384]{3,2,1,0:T(8,128)(2,1)}, bf16[1,32,96,384]{3,2,1,0:T(8,128)(2,1)}) custom-call(s32[5]{0:T(128)} %concatenate.82.idx, bf16[64,96,384]{2,1,0:T(8,128)(2,1)} %get-tuple-element.199.d0, bf16[64,96,384]{2,1,0:T(8,128)(2,1)} %get-tuple-element.202.d1, ...), custom_call_target="tpu_custom_call" | custom-call | flops 3600000000 | bytes 50000000 | tf_op jit(solution)/shard_map/pallas_call | solution.py:271
  1027.7 9.1 collective-permute-done.38
  1039.4 53.0 %back.5 = (bf16[96,384,128]{2,1,0:T(8,128)(2,1)}, f32[640,128]{1,0:T(8,128)}, f32[128,128]{1,0:T(8,128)}, f32[128,128]{1,0:T(8,128)}) custom-call(bf16[1,32,96,384]{3,2,1,0:T(8,128)(2,1)} %get-tuple-element.205.refs_0_, bf16[1,32,96,384]{3,2,1,0:T(8,128)(2,1)} %get-tuple-element.206.refs_1_, bf16[1,32,96,384]{3,2,1,0:T(8,128)(2,1)} %collective-permute-done.31.refs_2_, ...), custom_call_target="tpu_custom_call" | custom-call | flops 9437184000 | bytes 56623104 | tf_op jit(solution)/shard_map/back/pallas_call | solution.py:431
  (236 shorter events, 197.0 us)
Async XLA Ops:
  19.0 225.5 %collective-permute-start.14 = (bf16[96,128,384]{2,1,0:T(8,128)(2,1)}, bf16[96,128,384]{2,1,0:T(8,128)(2,1)}, u32[]{:S(2)}, u32[]{:S(2)}) collective-permute-start(bf16[96,128,384]{2,1,0:T(8,128)(2,1)} %get-tuple-element.133.x_ref.refs_5_.refs_4_), channel_id=1, source_target_pairs={{0,1},{1,0},{2,3},{3,2},{4,5},{5,4},{6,7},{7,6}} | collective-permute-start | bytes 28311560 | tf_op jit(solution)/shard_map/ppermute | solution.py:449
  21.3 109.9 %collective-permute-start.5 = (bf16[16,384,128]{2,1,0:T(8,128)(2,1)S(1)}, bf16[16,384,128]{2,1,0:T(8,128)(2,1)}, u32[]{:S(2)}, u32[]{:S(2)}) collective-permute-start(bf16[16,384,128]{2,1,0:T(8,128)(2,1)S(1)} %slice.250), channel_id=1, source_target_pairs={{0,2},{2,0},{1,3},{3,1},{4,6},{6,4},{5,7},{7,5}} | collective-permute-start | bytes 4718600 | tf_op jit(solution)/shard_map/ppermute | solution.py:446
  29.4 107.4 %collective-permute-start.4 = (bf16[16,384,128]{2,1,0:T(8,128)(2,1)}, bf16[16,384,128]{2,1,0:T(8,128)(2,1)S(1)}, u32[]{:S(2)}, u32[]{:S(2)}) collective-permute-start(bf16[16,384,128]{2,1,0:T(8,128)(2,1)} %get-tuple-element.263), channel_id=1, source_target_pairs={{0,2},{2,0},{1,3},{3,1},{4,6},{6,4},{5,7},{7,5}} | collective-permute-start | bytes 4718600 | tf_op jit(solution)/shard_map/ppermute | solution.py:446
  29.5 109.1 %collective-permute-start.3 = (bf16[16,384,128]{2,1,0:T(8,128)(2,1)}, bf16[16,384,128]{2,1,0:T(8,128)(2,1)S(1)}, u32[]{:S(2)}, u32[]{:S(2)}) collective-permute-start(bf16[16,384,128]{2,1,0:T(8,128)(2,1)} %get-tuple-element.264), channel_id=1, source_target_pairs={{0,2},{2,0},{1,3},{3,1},{4,6},{6,4},{5,7},{7,5}} | collective-permute-start | bytes 4718600 | tf_op jit(solution)/shard_map/ppermute | solution.py:446
  31.5 98.0 %collective-permute-start.7 = (f32[96,384]{1,0:T(8,128)S(1)}, f32[96,384]{1,0:T(8,128)S(1)}, u32[]{:S(2)}, u32[]{:S(2)}) collective-permute-start(f32[96,384]{1,0:T(8,128)S(1)} %convert_element_type.43.m_ref.refs_11_), channel_id=1, source_target_pairs={{0,2},{2,0},{1,3},{3,1},{4,6},{6,4},{5,7},{7,5}} | collective-permute-start | bytes 442376 | tf_op jit(solution)/shard_map/ppermute | solution.py:446
  129.5 37.6 %collective-permute-start.2 = (bf16[16,384,128]{2,1,0:T(8,128)(2,1)}, bf16[16,384,128]{2,1,0:T(8,128)(2,1)}, u32[]{:S(2)}, u32[]{:S(2)}) collective-permute-start(bf16[16,384,128]{2,1,0:T(8,128)(2,1)} %get-tuple-element.265), channel_id=1, source_target_pairs={{0,2},{2,0},{1,3},{3,1},{4,6},{6,4},{5,7},{7,5}} | collective-permute-start | bytes 4718600 | tf_op jit(solution)/shard_map/ppermute | solution.py:446
  131.2 69.5 %collective-permute-start.1 = (bf16[16,384,128]{2,1,0:T(8,128)(2,1)}, bf16[16,384,128]{2,1,0:T(8,128)(2,1)}, u32[]{:S(2)}, u32[]{:S(2)}) collective-permute-start(bf16[16,384,128]{2,1,0:T(8,128)(2,1)} %get-tuple-element.266), channel_id=1, source_target_pairs={{0,2},{2,0},{1,3},{3,1},{4,6},{6,4},{5,7},{7,5}} | collective-permute-start | bytes 4718600 | tf_op jit(solution)/shard_map/ppermute | solution.py:446
  136.8 96.6 %collective-permute-start = (bf16[16,384,128]{2,1,0:T(8,128)(2,1)}, bf16[16,384,128]{2,1,0:T(8,128)(2,1)}, u32[]{:S(2)}, u32[]{:S(2)}) collective-permute-start(bf16[16,384,128]{2,1,0:T(8,128)(2,1)} %get-tuple-element.267), channel_id=1, source_target_pairs={{0,2},{2,0},{1,3},{3,1},{4,6},{6,4},{5,7},{7,5}} | collective-permute-start | bytes 4718600 | tf_op jit(solution)/shard_map/ppermute | solution.py:446
  138.6 94.9 %collective-permute-start.13 = (bf16[16,128,384]{2,1,0:T(8,128)(2,1)}, bf16[16,128,384]{2,1,0:T(8,128)(2,1)S(1)}, u32[]{:S(2)}, u32[]{:S(2)}) collective-permute-start(bf16[16,128,384]{2,1,0:T(8,128)(2,1)} %get-tuple-element.132.x_ref), channel_id=1, source_target_pairs={{0,1},{1,0},{2,3},{3,2},{4,5},{5,4},{6,7},{7,6}} | collective-permute-start | bytes 4718600 | tf_op jit(solution)/shard_map/ppermute | solution.py:449
  167.1 54.9 %collective-permute-start.15 = (f32[96,384]{1,0:T(8,128)S(1)}, f32[96,384]{1,0:T(8,128)}, u32[]{:S(2)}, u32[]{:S(2)}) collective-permute-start(f32[96,384]{1,0:T(8,128)S(1)} %convert_element_type.43.m_ref.refs_11_), channel_id=1, source_target_pairs={{0,1},{1,0},{2,3},{3,2},{4,5},{5,4},{6,7},{7,6}} | collective-permute-start | bytes 442376 | tf_op jit(solution)/shard_map/ppermute | solution.py:449
  200.8 21.7 %collective-permute-start.8 = (f32[96,384]{1,0:T(8,128)S(1)}, f32[96,384]{1,0:T(8,128)}, u32[]{:S(2)}, u32[]{:S(2)}) collective-permute-start(f32[96,384]{1,0:T(8,128)S(1)} %collective-permute-done.7.m_ref.refs_11_), channel_id=1, source_target_pairs={{0,1},{1,0},{2,3},{3,2},{4,5},{5,4},{6,7},{7,6}} | collective-permute-start | bytes 442376 | tf_op jit(solution)/shard_map/ppermute | solution.py:449
  222.0 78.7 %collective-permute-start.12 = (bf16[16,128,384]{2,1,0:T(8,128)(2,1)}, bf16[16,128,384]{2,1,0:T(8,128)(2,1)}, u32[]{:S(2)}, u32[]{:S(2)}) collective-permute-start(bf16[16,128,384]{2,1,0:T(8,128)(2,1)} %get-tuple-element.131.x_ref), channel_id=1, source_target_pairs={{0,1},{1,0},{2,3},{3,2},{4,5},{5,4},{6,7},{7,6}} | collective-permute-start | bytes 4718600 | tf_op jit(solution)/shard_map/ppermute | solution.py:449
  222.5 88.8 %collective-permute-start.11 = (bf16[16,128,384]{2,1,0:T(8,128)(2,1)}, bf16[16,128,384]{2,1,0:T(8,128)(2,1)}, u32[]{:S(2)}, u32[]{:S(2)}) collective-permute-start(bf16[16,128,384]{2,1,0:T(8,128)(2,1)} %get-tuple-element.130.x_ref), channel_id=1, source_target_pairs={{0,1},{1,0},{2,3},{3,2},{4,5},{5,4},{6,7},{7,6}} | collective-permute-start | bytes 4718600 | tf_op jit(solution)/shard_map/ppermute | solution.py:449
  233.4 88.3 %collective-permute-start.10 = (bf16[16,128,384]{2,1,0:T(8,128)(2,1)S(1)}, bf16[16,128,384]{2,1,0:T(8,128)(2,1)}, u32[]{:S(2)}, u32[]{:S(2)}) collective-permute-start(bf16[16,128,384]{2,1,0:T(8,128)(2,1)S(1)} %copy-done.2), channel_id=1, source_target_pairs={{0,1},{1,0},{2,3},{3,2},{4,5},{5,4},{6,7},{7,6}} | collective-permute-start | bytes 4718600 | tf_op jit(solution)/shard_map/ppermute | solution.py:449
  234.6 97.6 %collective-permute-start.9 = (bf16[16,128,384]{2,1,0:T(8,128)(2,1)}, bf16[16,128,384]{2,1,0:T(8,128)(2,1)S(1)}, u32[]{:S(2)}, u32[]{:S(2)}) collective-permute-start(bf16[16,128,384]{2,1,0:T(8,128)(2,1)} %get-tuple-element.128.x_ref), channel_id=1, source_target_pairs={{0,1},{1,0},{2,3},{3,2},{4,5},{5,4},{6,7},{7,6}} | collective-permute-start | bytes 4718600 | tf_op jit(solution)/shard_map/ppermute | solution.py:449
  244.4 99.5 %collective-permute-start.6 = (bf16[16,128,384]{2,1,0:T(8,128)(2,1)}, bf16[16,128,384]{2,1,0:T(8,128)(2,1)}, u32[]{:S(2)}, u32[]{:S(2)}) collective-permute-start(bf16[16,128,384]{2,1,0:T(8,128)(2,1)} %get-tuple-element.127.x_ref), channel_id=1, source_target_pairs={{0,1},{1,0},{2,3},{3,2},{4,5},{5,4},{6,7},{7,6}} | collective-permute-start | bytes 4718600 | tf_op jit(solution)/shard_map/ppermute | solution.py:449
  363.6 18.9 %collective-permute-start.17 = (bf16[2,32,96,384]{3,2,1,0:T(8,128)(2,1)}, bf16[2,32,96,384]{3,2,1,0:T(8,128)(2,1)}, u32[]{:S(2)}, u32[]{:S(2)}) collective-permute-start(bf16[2,32,96,384]{3,2,1,0:T(8,128)(2,1)} %get-tuple-element.165), channel_id=1, source_target_pairs={{0,1},{1,0},{2,3},{3,2},{4,5},{5,4},{6,7},{7,6}} | collective-permute-start | bytes 14155784 | tf_op jit(solution)/shard_map/ppermute | solution.py:449
  413.4 54.7 %collective-permute-start.19 = (bf16[96,128,384]{2,1,0:T(8,128)(2,1)}, bf16[96,128,384]{2,1,0:T(8,128)(2,1)}, u32[]{:S(2)}, u32[]{:S(2)}) collective-permute-start(bf16[96,128,384]{2,1,0:T(8,128)(2,1)} %get-tuple-element.170.x_ref.refs_4_), channel_id=1, source_target_pairs={{0,1},{1,0},{2,3},{3,2},{4,5},{5,4},{6,7},{7,6}} | collective-permute-start | bytes 28311560 | tf_op jit(solution)/shard_map/ppermute | solution.py:449
  440.1 57.2 %collective-permute-start.18 = (bf16[96,128,384]{2,1,0:T(8,128)(2,1)}, bf16[96,128,384]{2,1,0:T(8,128)(2,1)}, u32[]{:S(2)}, u32[]{:S(2)}) collective-permute-start(bf16[96,128,384]{2,1,0:T(8,128)(2,1)} %get-tuple-element.168.x_ref.refs_4_), channel_id=1, source_target_pairs={{0,1},{1,0},{2,3},{3,2},{4,5},{5,4},{6,7},{7,6}} | collective-permute-start | bytes 28311560 | tf_op jit(solution)/shard_map/ppermute | solution.py:449
  451.2 205.3 %collective-permute-start.22 = (bf16[96,128,384]{2,1,0:T(8,128)(2,1)}, bf16[96,128,384]{2,1,0:T(8,128)(2,1)}, u32[]{:S(2)}, u32[]{:S(2)}) collective-permute-start(bf16[96,128,384]{2,1,0:T(8,128)(2,1)} %turn.1.refs_5_.refs_9_), channel_id=1, source_target_pairs={{0,2},{2,0},{1,3},{3,1},{4,6},{6,4},{5,7},{7,5}} | collective-permute-start | bytes 28311560 | tf_op jit(solution)/shard_map/ppermute | solution.py:446
  527.6 128.9 %collective-permute-start.21 = (bf16[2,32,96,384]{3,2,1,0:T(8,128)(2,1)}, bf16[2,32,96,384]{3,2,1,0:T(8,128)(2,1)}, u32[]{:S(2)}, u32[]{:S(2)}) collective-permute-start(bf16[2,32,96,384]{3,2,1,0:T(8,128)(2,1)} %get-tuple-element.182), channel_id=1, source_target_pairs={{0,1},{1,0},{2,3},{3,2},{4,5},{5,4},{6,7},{7,6}} | collective-permute-start | bytes 14155784 | tf_op jit(solution)/shard_map/ppermute | solution.py:449
  543.3 113.2 %collective-permute-start.20 = (bf16[2,32,96,384]{3,2,1,0:T(8,128)(2,1)}, bf16[2,32,96,384]{3,2,1,0:T(8,128)(2,1)}, u32[]{:S(2)}, u32[]{:S(2)}) collective-permute-start(bf16[2,32,96,384]{3,2,1,0:T(8,128)(2,1)} %get-tuple-element.181), channel_id=1, source_target_pairs={{0,1},{1,0},{2,3},{3,2},{4,5},{5,4},{6,7},{7,6}} | collective-permute-start | bytes 14155784 | tf_op jit(solution)/shard_map/ppermute | solution.py:449
  691.4 39.3 %collective-permute-start.24 = (bf16[64,96,384]{2,1,0:T(8,128)(2,1)}, bf16[64,96,384]{2,1,0:T(8,128)(2,1)}, u32[]{:S(2)}, u32[]{:S(2)}) collective-permute-start(bf16[64,96,384]{2,1,0:T(8,128)(2,1)} %get-tuple-element.188), channel_id=1, source_target_pairs={{0,1},{1,0},{2,3},{3,2},{4,5},{5,4},{6,7},{7,6}} | collective-permute-start | bytes 14155784 | tf_op jit(solution)/shard_map/ppermute | solution.py:449
  763.0 28.0 %collective-permute-start.26 = (bf16[2,32,96,384]{3,2,1,0:T(8,128)(2,1)}, bf16[2,32,96,384]{3,2,1,0:T(8,128)(2,1)}, u32[]{:S(2)}, u32[]{:S(2)}) collective-permute-start(bf16[2,32,96,384]{3,2,1,0:T(8,128)(2,1)} %get-tuple-element.192), channel_id=1, source_target_pairs={{0,1},{1,0},{2,3},{3,2},{4,5},{5,4},{6,7},{7,6}} | collective-permute-start | bytes 14155784 | tf_op jit(solution)/shard_map/ppermute | solution.py:449
  763.5 27.5 %collective-permute-start.28 = (bf16[2,32,96,384]{3,2,1,0:T(8,128)(2,1)}, bf16[2,32,96,384]{3,2,1,0:T(8,128)(2,1)}, u32[]{:S(2)}, u32[]{:S(2)}) collective-permute-start(bf16[2,32,96,384]{3,2,1,0:T(8,128)(2,1)} %get-tuple-element.196), channel_id=1, source_target_pairs={{0,1},{1,0},{2,3},{3,2},{4,5},{5,4},{6,7},{7,6}} | collective-permute-start | bytes 14155784 | tf_op jit(solution)/shard_map/ppermute | solution.py:449
  788.6 14.6 %collective-permute-start.27 = (bf16[2,32,96,384]{3,2,1,0:T(8,128)(2,1)}, bf16[2,32,96,384]{3,2,1,0:T(8,128)(2,1)}, u32[]{:S(2)}, u32[]{:S(2)}) collective-permute-start(bf16[2,32,96,384]{3,2,1,0:T(8,128)(2,1)} %get-tuple-element.195), channel_id=1, source_target_pairs={{0,1},{1,0},{2,3},{3,2},{4,5},{5,4},{6,7},{7,6}} | collective-permute-start | bytes 14155784 | tf_op jit(solution)/shard_map/ppermute | solution.py:449
  882.5 91.8 %collective-permute-start.30 = (bf16[64,96,384]{2,1,0:T(8,128)(2,1)}, bf16[64,96,384]{2,1,0:T(8,128)(2,1)}, u32[]{:S(2)}, u32[]{:S(2)}) collective-permute-start(bf16[64,96,384]{2,1,0:T(8,128)(2,1)} %get-tuple-element.204), channel_id=1, source_target_pairs={{0,1},{1,0},{2,3},{3,2},{4,5},{5,4},{6,7},{7,6}} | collective-permute-start | bytes 14155784 | tf_op jit(solution)/shard_map/ppermute | solution.py:449
  997.0 40.9 %collective-permute-start.32 = (bf16[1,32,96,384]{3,2,1,0:T(8,128)(2,1)}, bf16[1,32,96,384]{3,2,1,0:T(8,128)(2,1)S(1)}, u32[]{:S(2)}, u32[]{:S(2)}) collective-permute-start(bf16[1,32,96,384]{3,2,1,0:T(8,128)(2,1)} %get-tuple-element.208), channel_id=1, source_target_pairs={{0,1},{1,0},{2,3},{3,2},{4,5},{5,4},{6,7},{7,6}} | collective-permute-start | bytes 7077896 | tf_op jit(solution)/shard_map/ppermute | solution.py:449
  997.2 40.7 %collective-permute-start.34 = (bf16[1,32,96,384]{3,2,1,0:T(8,128)(2,1)}, bf16[1,32,96,384]{3,2,1,0:T(8,128)(2,1)}, u32[]{:S(2)}, u32[]{:S(2)}) collective-permute-start(bf16[1,32,96,384]{3,2,1,0:T(8,128)(2,1)} %get-tuple-element.212), channel_id=1, source_target_pairs={{0,1},{1,0},{2,3},{3,2},{4,5},{5,4},{6,7},{7,6}} | collective-permute-start | bytes 7077896 | tf_op jit(solution)/shard_map/ppermute | solution.py:449
  1015.2 22.8 %collective-permute-start.31 = (bf16[1,32,96,384]{3,2,1,0:T(8,128)(2,1)}, bf16[1,32,96,384]{3,2,1,0:T(8,128)(2,1)}, u32[]{:S(2)}, u32[]{:S(2)}) collective-permute-start(bf16[1,32,96,384]{3,2,1,0:T(8,128)(2,1)} %get-tuple-element.207), channel_id=1, source_target_pairs={{0,1},{1,0},{2,3},{3,2},{4,5},{5,4},{6,7},{7,6}} | collective-permute-start | bytes 7077896 | tf_op jit(solution)/shard_map/ppermute | solution.py:449
  1015.3 22.6 %collective-permute-start.33 = (bf16[1,32,96,384]{3,2,1,0:T(8,128)(2,1)}, bf16[1,32,96,384]{3,2,1,0:T(8,128)(2,1)}, u32[]{:S(2)}, u32[]{:S(2)}) collective-permute-start(bf16[1,32,96,384]{3,2,1,0:T(8,128)(2,1)} %get-tuple-element.211), channel_id=1, source_target_pairs={{0,1},{1,0},{2,3},{3,2},{4,5},{5,4},{6,7},{7,6}} | collective-permute-start | bytes 7077896 | tf_op jit(solution)/shard_map/ppermute | solution.py:449
  1024.0 12.8 %collective-permute-start.38 = (f32[904,128]{1,0:T(8,128)S(1)}, f32[904,128]{1,0:T(8,128)}, u32[]{:S(2)}, u32[]{:S(2)}) collective-permute-start(f32[904,128]{1,0:T(8,128)S(1)} %add.54), channel_id=1, source_target_pairs={{0,2},{2,0},{1,3},{3,1},{4,6},{6,4},{5,7},{7,5}} | collective-permute-start | bytes 1388552 | tf_op jit(solution)/shard_map/ppermute | solution.py:446
  (34 other events, 844.6 us)
